TPU v7x, 32 devices: a whole 2x2x4 slice. The times are simulated.
32 devices in a mesh: src: 4 (over y, core), tgt: 8 (over z, x).
Axes of the slice: x: 2, y: 2, z: 4, core: 2. Of those that a mesh axis runs over, the one named last changes fastest.
Arguments:
- sources: float32 [256, 8192], P('tgt', 'src'), may hold values from -24 to 24, as said below
- targets: float32 [256, 8192], P('src', 'tgt'), may hold values from -24 to 24, as said below
- source_logw: float32 [8192], P('src'), may hold values from -1 to 1
- target_logw: float32 [8192], P('tgt'), may hold values from -1 to 1
- times: float32 [8192], P('src'), may hold values from 0 to 1
Outputs:
- row_potential: float32 [8192], P('src')
- moved: float32 [256, 8192], P('tgt', 'src')
- col_potential: float32 [8192], P('tgt')
Inputs may be any that keep to these rules, and one draw needn't show every extreme that they name: `sources`: point coordinates. `targets`: point coordinates.
All inputs are finite; a program needn't handle non-finite values.
Results may differ from a plain program's by a relative error of at most 0.00025.
Values sent between devices are 32-bit elements; how exact they have to be, the bound alone decides.
No kernel may reach another device: no remote copies, remote signals or barrier semaphores. Data moves between devices by JAX's collectives and lax.ppermute only.
A program may use at most 64 MiB of HBM per device.

v0:
```python
import jax
import jax.numpy as jnp
from jax import lax
from jax.sharding import PartitionSpec as P

ITERS = 2


EPSILON = 16.0


def cost_block(rows, cols):
    cross = jnp.dot(
        rows, cols.T, precision=lax.Precision.HIGHEST, preferred_element_type=jnp.float32
    )
    return 0.5 * jnp.sum(rows * rows, 1)[:, None] + 0.5 * jnp.sum(cols * cols, 1)[None, :] - cross


def merge_rows(top, total):
    largest = lax.pmax(top, "tgt")
    total = lax.psum(total * jnp.exp(top - largest), "tgt")
    top = largest
    return top + jnp.log(total)


def merge_cols(top, total):
    largest = lax.pmax(top, "src")
    total = lax.psum(total * jnp.exp(top - largest), "src")
    top = largest
    return top + jnp.log(total)


def row_partials(blocks, cols_full, col_pot):

    def one(blk):
        scores = (col_pot[None, :] - cost_block(blk, cols_full)) / EPSILON
        top = jnp.max(scores, 1)
        return (top, jnp.sum(jnp.exp(scores - top[:, None]), 1))

    top, total = lax.map(one, blocks)
    return (top.reshape(-1), total.reshape(-1))


def col_partials(blocks, cols_full, row_pot):
    count, block = (blocks.shape[0], blocks.shape[1])
    cols = cols_full.shape[0]

    def step(carry, item):
        top, total = carry
        blk, pot = item
        scores = (pot[:, None] - cost_block(blk, cols_full)) / EPSILON
        fresh = jnp.maximum(top, jnp.max(scores, 0))
        total = total * jnp.exp(top - fresh) + jnp.sum(jnp.exp(scores - fresh[None, :]), 0)
        return ((fresh, total), None)

    init = (jnp.full((cols,), -1e30, jnp.float32), jnp.zeros((cols,), jnp.float32))
    (top, total), _ = lax.scan(step, init, (blocks, row_pot.reshape(count, block)))
    return (top, total)


def per_device(sources, targets, source_logw, target_logw, times):
    rows_full = lax.all_gather(sources, "tgt", axis=0, tiled=True).T
    cols_full = lax.all_gather(targets, "src", axis=0, tiled=True).T
    rows = rows_full.shape[0]
    width = rows_full.shape[1]
    block = min(512, rows)
    count = rows // block
    blocks = rows_full.reshape(count, block, width)
    col_pot = jnp.zeros((cols_full.shape[0],), jnp.float32)
    row_pot = jnp.zeros((rows,), jnp.float32)
    for sweep in range(ITERS):
        top, total = row_partials(blocks, cols_full, col_pot)
        row_pot = EPSILON * (source_logw - merge_rows(top, total))
        top, total = col_partials(blocks, cols_full, row_pot)
        col_pot = EPSILON * (target_logw - merge_cols(top, total))

    def transport(item):
        blk, pot = item
        plan = jnp.exp((pot[:, None] + col_pot[None, :] - cost_block(blk, cols_full)) / EPSILON)
        weighted = jnp.dot(
            plan, cols_full, precision=lax.Precision.HIGHEST, preferred_element_type=jnp.float32
        )
        return (weighted, jnp.sum(plan, 1))

    weighted, mass = lax.map(transport, (blocks, row_pot.reshape(count, block)))
    weighted = weighted.reshape(rows, width)
    mass = mass.reshape(rows)
    weighted, mass = lax.psum((weighted, mass), "tgt")
    moved_full = (1.0 - times)[:, None] * rows_full + times[:, None] * (weighted / mass[:, None])
    narrow = sources.shape[0]
    moved = lax.dynamic_slice_in_dim(moved_full.T, lax.axis_index("tgt") * narrow, narrow, 0)
    top, total = col_partials(moved_full.reshape(count, block, width), cols_full, row_pot)
    final_pot = EPSILON * (target_logw - merge_cols(top, total))
    return (row_pot, moved, final_pot)


def solution(mesh):
    placed = (P("tgt", "src"), P("src", "tgt"), P("src"), P("tgt"), P("src"))
    return jax.shard_map(
        per_device,
        mesh=mesh,
        in_specs=placed,
        out_specs=(P("src"), P("tgt", "src"), P("tgt")),
        check_vma=False,
    )
```

profile of v0, /device:TPU:0, one launch (start us, length us, event | category | flops | bytes accessed | tf_op | source)
XLA Modules:
  0.0 444.5 jit_solution(551319761794600499)
XLA Ops:
  8.7 20.2 %all-gather.5.cloned.1.call-done = f32[256,1024]{1,0:T(8,128)} async-done(((f32[64,1024]{1,0:T(8,128)}), f32[256,1024]{1,0:T(8,128)}) %all-gather.5.cloned.1.call-update) | async-done | bytes 1048592 | tf_op jit(solution)/shard_map/all_gather | solution.py:63
  30.8 49.5 %all-gather.3.cloned.1.call-done = f32[256,2048]{1,0:T(8,128)} async-done(((f32[32,2048]{1,0:T(8,128)}), f32[256,2048]{1,0:T(8,128)}) %all-gather.3.cloned.1.call-update) | async-done | bytes 2097168 | tf_op jit(solution)/shard_map/all_gather | solution.py:62
  82.2 16.9 %while.87 = (s32[]{:T(128)}, f32[4,512]{1,0:T(4,128)S(1)}, f32[4,512]{1,0:T(4,128)S(1)}, f32[4,512,256]{2,1,0:T(8,128)S(1)}, f32[1024]{0:T(1024)S(1)}, /*index=5*/f32[256,1024]{1,0:T(8,128)}, s32[]{:T(128)}, s32[]{:T(128)}) while((s32[]{:T(128)}, f32[4,512]{1,0:T(4,128)S(1)}, f32[4,512]{1,0:T(4,128)S(1)}, f32[4,512,256]{2,1,0:T(8,128)S(1)}, ...), condition=%wide.region_5.6_spmd, body=%wide.region_1.5_spmd.sunk | while | flops 1614544896 | bytes 6326373 | solution.py:40
  82.4 3.4 fusion.68
  86.6 3.4 fusion.68
  90.9 3.4 fusion.68
  95.1 3.4 fusion.68
  99.2 19.2 %pmax.35 = f32[2048]{0:T(1024)S(1)} all-reduce(f32[2048]{0:T(1024)S(1)} %bitcast.156), channel_id=1, replica_groups=mesh['src'=4,'tgt'=8] {'tgt'}, use_global_device_ids=true, to_apply=%region_6.7 | all-reduce | flops 2048 | bytes 16384 | tf_op jit(solution)/shard_map/pmax | solution.py:20
  118.4 17.7 %psum.49 = f32[2048]{0:T(1024)S(1)} all-reduce(f32[2048]{0:T(1024)S(1)} %exponential_multiply_fusion.1), channel_id=1, replica_groups=mesh['src'=4,'tgt'=8] {'tgt'}, use_global_device_ids=true, to_apply=%region_7.8 | all-reduce | flops 2048 | bytes 16384 | tf_op jit(solution)/shard_map/psum | solution.py:21
  136.2 27.2 %while.90 = (s32[]{:T(128)}, f32[1024]{0:T(1024)S(1)}, f32[1024]{0:T(1024)S(1)}, f32[4,512]{1,0:T(4,128)S(1)}, f32[4,512,256]{2,1,0:T(8,128)S(1)}, /*index=5*/f3...) while((s32[]{:T(128)}, f32[1024]{0:T(1024)S(1)}, f32[1024]{0:T(1024)S(1)}, ...), condition=%wide.region_12.13_spmd.clone, body=%wide.region_8.12_spmd.clone.sunk | while | flops 1614551040 | bytes 6371444 | solution.py:57
  136.4 4.7 %fusion.80 = (f32[1024]{0:T(1024)S(1)}, f32[512,1024]{1,0:T(8,128)}) fusion(f32[256,1024]{1,0:T(8,128)} %get-tuple-element.1078, f32[4,512,256]{2,1,0:T(8,128)S(1)} %get-tuple-element.1076, s32[]{:T(128)} %get-tuple-element.1063, f32[1024]{0:T(1024)S(1)} %broadcast_multiply_fusion.30, f32[512]{0:T(512)S(1)} %broadcast_multiply_fusion.31, ...), kind=kOutput, calls=%fused_computation.85.clone.1 | convolution fusion | flops 1613233152 | bytes 3682308 | tf_op jit(solution)/shard_map/while/body/eval_jaxpr/dot_general | solution.py:13
  143.2 4.7 %fusion.80 = (f32[1024]{0:T(1024)S(1)}, f32[512,1024]{1,0:T(8,128)}) fusion(f32[256,1024]{1,0:T(8,128)} %get-tuple-element.1078, f32[4,512,256]{2,1,0:T(8,128)S(1)} %get-tuple-element.1076, s32[]{:T(128)} %get-tuple-element.1063, f32[1024]{0:T(1024)S(1)} %broadcast_multiply_fusion.30, f32[512]{0:T(512)S(1)} %broadcast_multiply_fusion.31, ...), kind=kOutput, calls=%fused_computation.85.clone.1 | convolution fusion | flops 1613233152 | bytes 3682308 | tf_op jit(solution)/shard_map/while/body/eval_jaxpr/dot_general | solution.py:13
  150.0 4.7 %fusion.80 = (f32[1024]{0:T(1024)S(1)}, f32[512,1024]{1,0:T(8,128)}) fusion(f32[256,1024]{1,0:T(8,128)} %get-tuple-element.1078, f32[4,512,256]{2,1,0:T(8,128)S(1)} %get-tuple-element.1076, s32[]{:T(128)} %get-tuple-element.1063, f32[1024]{0:T(1024)S(1)} %broadcast_multiply_fusion.30, f32[512]{0:T(512)S(1)} %broadcast_multiply_fusion.31, ...), kind=kOutput, calls=%fused_computation.85.clone.1 | convolution fusion | flops 1613233152 | bytes 3682308 | tf_op jit(solution)/shard_map/while/body/eval_jaxpr/dot_general | solution.py:13
  156.8 4.7 %fusion.80 = (f32[1024]{0:T(1024)S(1)}, f32[512,1024]{1,0:T(8,128)}) fusion(f32[256,1024]{1,0:T(8,128)} %get-tuple-element.1078, f32[4,512,256]{2,1,0:T(8,128)S(1)} %get-tuple-element.1076, s32[]{:T(128)} %get-tuple-element.1063, f32[1024]{0:T(1024)S(1)} %broadcast_multiply_fusion.30, f32[512]{0:T(512)S(1)} %broadcast_multiply_fusion.31, ...), kind=kOutput, calls=%fused_computation.85.clone.1 | convolution fusion | flops 1613233152 | bytes 3682308 | tf_op jit(solution)/shard_map/while/body/eval_jaxpr/dot_general | solution.py:13
  163.4 5.7 %pmax.36 = f32[1024]{0:T(1024)S(1)} all-reduce(f32[1024]{0:T(1024)S(1)} %get-tuple-element.519), channel_id=1, replica_groups=mesh['src'=4,'tgt'=8] {'src'}, use_global_device_ids=true, to_apply=%region_13.14 | all-reduce | flops 1024 | bytes 8192 | tf_op jit(solution)/shard_map/pmax | solution.py:27
  169.1 6.6 %psum.50 = f32[1024]{0:T(1024)S(1)} all-reduce(f32[1024]{0:T(1024)S(1)} %exponential_multiply_fusion.4), channel_id=1, replica_groups=mesh['src'=4,'tgt'=8] {'src'}, use_global_device_ids=true, to_apply=%region_14.15 | all-reduce | flops 1024 | bytes 8192 | tf_op jit(solution)/shard_map/psum | solution.py:28
  175.8 17.0 %while.88 = (s32[]{:T(128)}, f32[4,512]{1,0:T(4,128)S(1)}, f32[4,512]{1,0:T(4,128)S(1)}, f32[1024]{0:T(1024)S(1)}, f32[4,512,256]{2,1,0:T(8,128)S(1)}, /*index=5...) while((s32[]{:T(128)}, f32[4,512]{1,0:T(4,128)S(1)}, f32[4,512]{1,0:T(4,128)S(1)}, ...), condition=%wide.region_19.20_spmd, body=%wide.region_15.0_spmd.sunk | while | flops 1614544896 | bytes 6330477 | solution.py:40
  175.9 3.4 fusion.71
  180.2 3.4 fusion.71
  184.4 3.4 fusion.71
  188.7 3.4 fusion.71
  192.7 19.1 %pmax.37 = f32[2048]{0:T(1024)S(1)} all-reduce(f32[2048]{0:T(1024)S(1)} %bitcast.158), channel_id=1, replica_groups=mesh['src'=4,'tgt'=8] {'tgt'}, use_global_device_ids=true, to_apply=%region_20.21 | all-reduce | flops 2048 | bytes 16384 | tf_op jit(solution)/shard_map/pmax | solution.py:20
  211.9 17.9 %psum.51 = f32[2048]{0:T(1024)S(1)} all-reduce(f32[2048]{0:T(1024)S(1)} %exponential_multiply_fusion), channel_id=1, replica_groups=mesh['src'=4,'tgt'=8] {'tgt'}, use_global_device_ids=true, to_apply=%region_21.22 | all-reduce | flops 2048 | bytes 16384 | tf_op jit(solution)/shard_map/psum | solution.py:21
  230.4 27.2 %while.91 = (s32[]{:T(128)}, f32[1024]{0:T(1024)S(1)}, f32[1024]{0:T(1024)S(1)}, f32[4,512]{1,0:T(4,128)S(1)}, f32[4,512,256]{2,1,0:T(8,128)S(1)}, /*index=5*/f3...) while((s32[]{:T(128)}, f32[1024]{0:T(1024)S(1)}, f32[1024]{0:T(1024)S(1)}, ...), condition=%wide.region_26.27_spmd.clone, body=%wide.region_22.0_spmd.clone.sunk | while | flops 1614551040 | bytes 6371444 | solution.py:57
  230.5 4.7 %fusion.84 = (f32[1024]{0:T(1024)S(1)}, f32[512,1024]{1,0:T(8,128)}) fusion(f32[256,1024]{1,0:T(8,128)} %get-tuple-element.1132, f32[4,512,256]{2,1,0:T(8,128)S(1)} %get-tuple-element.1130, s32[]{:T(128)} %get-tuple-element.1117, f32[1024]{0:T(1024)S(1)} %broadcast_multiply_fusion.32, f32[512]{0:T(512)S(1)} %broadcast_multiply_fusion.33, ...), kind=kOutput, calls=%fused_computation.86.clone.1 | convolution fusion | flops 1613233152 | bytes 3682308 | tf_op jit(solution)/shard_map/while/body/eval_jaxpr/dot_general | solution.py:13
  237.4 4.7 %fusion.84 = (f32[1024]{0:T(1024)S(1)}, f32[512,1024]{1,0:T(8,128)}) fusion(f32[256,1024]{1,0:T(8,128)} %get-tuple-element.1132, f32[4,512,256]{2,1,0:T(8,128)S(1)} %get-tuple-element.1130, s32[]{:T(128)} %get-tuple-element.1117, f32[1024]{0:T(1024)S(1)} %broadcast_multiply_fusion.32, f32[512]{0:T(512)S(1)} %broadcast_multiply_fusion.33, ...), kind=kOutput, calls=%fused_computation.86.clone.1 | convolution fusion | flops 1613233152 | bytes 3682308 | tf_op jit(solution)/shard_map/while/body/eval_jaxpr/dot_general | solution.py:13
  244.2 4.7 %fusion.84 = (f32[1024]{0:T(1024)S(1)}, f32[512,1024]{1,0:T(8,128)}) fusion(f32[256,1024]{1,0:T(8,128)} %get-tuple-element.1132, f32[4,512,256]{2,1,0:T(8,128)S(1)} %get-tuple-element.1130, s32[]{:T(128)} %get-tuple-element.1117, f32[1024]{0:T(1024)S(1)} %broadcast_multiply_fusion.32, f32[512]{0:T(512)S(1)} %broadcast_multiply_fusion.33, ...), kind=kOutput, calls=%fused_computation.86.clone.1 | convolution fusion | flops 1613233152 | bytes 3682308 | tf_op jit(solution)/shard_map/while/body/eval_jaxpr/dot_general | solution.py:13
  251.0 4.7 %fusion.84 = (f32[1024]{0:T(1024)S(1)}, f32[512,1024]{1,0:T(8,128)}) fusion(f32[256,1024]{1,0:T(8,128)} %get-tuple-element.1132, f32[4,512,256]{2,1,0:T(8,128)S(1)} %get-tuple-element.1130, s32[]{:T(128)} %get-tuple-element.1117, f32[1024]{0:T(1024)S(1)} %broadcast_multiply_fusion.32, f32[512]{0:T(512)S(1)} %broadcast_multiply_fusion.33, ...), kind=kOutput, calls=%fused_computation.86.clone.1 | convolution fusion | flops 1613233152 | bytes 3682308 | tf_op jit(solution)/shard_map/while/body/eval_jaxpr/dot_general | solution.py:13
  257.6 5.7 %pmax.38 = f32[1024]{0:T(1024)S(1)} all-reduce(f32[1024]{0:T(1024)S(1)} %get-tuple-element.523), channel_id=1, replica_groups=mesh['src'=4,'tgt'=8] {'src'}, use_global_device_ids=true, to_apply=%region_27.28 | all-reduce | flops 1024 | bytes 8192 | tf_op jit(solution)/shard_map/pmax | solution.py:27
  263.3 6.3 %psum.52 = f32[1024]{0:T(1024)S(1)} all-reduce(f32[1024]{0:T(1024)S(1)} %exponential_multiply_fusion.3), channel_id=1, replica_groups=mesh['src'=4,'tgt'=8] {'src'}, use_global_device_ids=true, to_apply=%region_28.29 | all-reduce | flops 1024 | bytes 8192 | tf_op jit(solution)/shard_map/psum | solution.py:28
  269.5 26.2 %while.89 = (s32[]{:T(128)}, f32[4,512,256]{2,1,0:T(8,128)}, f32[4,512]{1,0:T(4,128)S(1)}, f32[4,512]{1,0:T(4,128)S(1)}, f32[1024]{0:T(1024)S(1)}, /*index=5*/f3...) while((s32[]{:T(128)}, f32[4,512,256]{2,1,0:T(8,128)}, ...), condition=%wide.region_32.33_spmd, body=%wide.region_29.32_spmd.sunk | while | flops 3224633856 | bytes 7901821 | solution.py:85
  269.8 3.7 fusion.76
  276.3 3.7 fusion.76
  280.0 2.6 fusion.77
  282.8 3.7 fusion.76
  289.4 3.7 fusion.76
  293.1 2.6 fusion.77
  295.7 2.9 copy.16
  299.4 20.4 %psum.54 = f32[2048]{0:T(1024)S(1)} all-reduce(f32[2048]{0:T(1024)S(1)} %bitcast.170), channel_id=1, replica_groups=mesh['src'=4,'tgt'=8] {'tgt'}, use_global_device_ids=true, to_apply=%region_34.35 | all-reduce | flops 2048 | bytes 16384 | tf_op jit(solution)/shard_map/psum | solution.py:88
  319.7 79.9 %all-reduce.2.cloned.1.call-done = f32[2048,256]{0,1:T(8,128)} async-done(((f32[2048,256]{0,1:T(8,128)}), f32[2048,256]{0,1:T(8,128)}) %all-reduce.2.cloned.1.call-update) | async-done | bytes 2097168 | tf_op jit(solution)/shard_map/psum | solution.py:88
  399.6 2.6 multiply_add_fusion
  404.3 19.1 %while.92 = (s32[]{:T(128)}, f32[1024]{0:T(1024)S(1)}, f32[1024]{0:T(1024)S(1)}, f32[4,512]{1,0:T(4,128)S(1)}, f32[4,512,256]{2,1,0:T(8,128)}, /*index=5*/f32[10...) while((s32[]{:T(128)}, f32[1024]{0:T(1024)S(1)}, f32[1024]{0:T(1024)S(1)}, ...), condition=%wide.region_39.40_spmd.clone, body=%wide.region_35.39_spmd.clone.sunk | while | flops 1614551040 | bytes 6371952 | solution.py:57
  405.5 3.2 fusion.88
  410.3 3.2 fusion.88
  415.1 3.2 fusion.88
  419.9 3.2 fusion.88
  423.4 6.2 %pmax.39 = f32[1024]{0:T(1024)S(1)} all-reduce(f32[1024]{0:T(1024)S(1)} %get-tuple-element.527), channel_id=1, replica_groups=mesh['src'=4,'tgt'=8] {'src'}, use_global_device_ids=true, to_apply=%region_40.41 | all-reduce | flops 1024 | bytes 8192 | tf_op jit(solution)/shard_map/pmax | solution.py:27
  429.6 6.1 %psum.55 = f32[1024]{0:T(1024)S(1)} all-reduce(f32[1024]{0:T(1024)S(1)} %exponential_multiply_fusion.2), channel_id=1, replica_groups=mesh['src'=4,'tgt'=8] {'src'}, use_global_device_ids=true, to_apply=%region_41.42 | all-reduce | flops 1024 | bytes 8192 | tf_op jit(solution)/shard_map/psum | solution.py:28
  (221 shorter events, 46.0 us)
Async XLA Ops:
  7.2 21.8 %all-gather.5.cloned.1.call-start = ((), (), s32[]{:S(2)}) async-start(), calls=%async_computation.1 | async-start | bytes 1310720 | tf_op jit(solution)/shard_map/all_gather | solution.py:63
  7.9 72.3 %all-gather.3.cloned.1.call-start = ((), (), s32[]{:S(2)}) async-start(), calls=%async_computation | async-start | bytes 2359296 | tf_op jit(solution)/shard_map/all_gather | solution.py:62
  8.6 391.0 %all-reduce.2.cloned.1.call-start = ((), (), s32[]{:S(2)}) async-start(), calls=%async_computation.2 | async-start | bytes 4194304 | tf_op jit(solution)/shard_map/psum | solution.py:88
  29.0 1.7 copy-start.1
  82.2 53.9 %copy-start.6 = (f32[2048]{0:T(1024)S(1)}, f32[2048]{0:T(1024)}, u32[]{:S(2)}) copy-start(f32[2048]{0:T(1024)} %param.19) | copy-start | bytes 24580
  136.2 39.5 %copy-start.3 = (f32[1024]{0:T(1024)S(1)}, f32[1024]{0:T(1024)}, u32[]{:S(2)}) copy-start(f32[1024]{0:T(1024)} %param.20) | copy-start | bytes 12292
  229.8 0.6 copy-start.5
  298.7 0.7 copy-start.4
  402.3 2.0 copy-start
  402.3 2.0 copy-start.2
Sparse Core Ops, SparseCore 0:
  9.5 19.4 all-gather.4
  31.1 49.0 all-gather.2
  298.8 100.7 all-reduce.1
where the time goes:
time: 446 us; the launch traced here: 445 us
  waiting for transfers between devices  151 us (34%)
  blocking collectives  131 us (29%)
  matrix products  103 us (23%)
  other arithmetic  32.3 us (7%)
  between operations  14.1 us (3%)
  local copies, waits for them, and re-layouts  12.6 us (3%)
    dot_general x24, matrix products, cost_block(): jnp.dot(rows, cols.T, precision=lax.Precision.HIGHEST, preferred_element_...  92.1 us
    psum x1, waiting for transfers between devices, per_device(): weighted, mass = lax.psum((weighted, mass), 'tgt')  79.9 us
    all_gather x1, waiting for transfers between devices, per_device(): rows_full = lax.all_gather(sources, 'tgt', axis=0, tiled=True).T  49.5 us
    pmax x2, blocking collectives, merge_rows(): largest = lax.pmax(top, 'tgt')  38.3 us
    psum x2, blocking collectives, merge_rows(): total = lax.psum(total * jnp.exp(top - largest), 'tgt')  35.6 us
    psum x1, blocking collectives, per_device(): weighted, mass = lax.psum((weighted, mass), 'tgt')  20.4 us
    all_gather x1, waiting for transfers between devices, per_device(): cols_full = lax.all_gather(targets, 'src', axis=0, tiled=True).T  20.2 us
    psum x3, blocking collectives, merge_cols(): total = lax.psum(total * jnp.exp(top - largest), 'src')  19 us
  transfers between devices with their start and end apart: 3, of which 3 were waited for; matrix products, arithmetic and copies ran while one was open for 0% of the time, Pallas kernels for 0%

commit v1 on v0

v1 whole, which is shorter than its diff:
```python
import jax
import jax.numpy as jnp
from jax import lax
from jax.experimental import pallas as pl
from jax.experimental.pallas import tpu as pltpu
from jax.sharding import PartitionSpec as P


EPS = 16.0
LOG2E = 1.4426950408889634
LN2 = 0.6931471805599453
L = LOG2E / EPS
LANES = 128
F32 = jnp.float32
BF16 = jnp.bfloat16
MB = 1024 * 1024


def split(v):
    hi = v.astype(BF16)
    return hi, (v - hi.astype(F32)).astype(BF16)


def dot3(ah, al, bh, bl, dims):
    d = lambda p, q: lax.dot_general(p, q, (dims, ((), ())), preferred_element_type=F32)
    return d(ah, bh) + d(ah, bl) + d(al, bh)


def to_col(row):
    return jnp.broadcast_to(row, (LANES, LANES)).T


def log2(v):
    return jnp.log(v) * LOG2E


def groups(v):
    return v.reshape(v.shape[0] // 8, 8, v.shape[1])


def call(body, outs, scratch, limit):
    return pl.pallas_call(
        body,
        out_shape=outs,
        scratch_shapes=scratch,
        compiler_params=pltpu.CompilerParams(vmem_limit_bytes=limit * MB),
    )


def sds(*shape, dtype=F32):
    return jax.ShapeDtypeStruct(shape, dtype)


def position():
    s, t = lax.axis_index("src"), lax.axis_index("tgt")
    return s >> 1, s & 1, t >> 1, t & 1


def lanes_at(index, size):
    return pl.ds(pl.multiple_of(index * size, LANES), size)


def rows_at(index, size):
    return pl.ds(pl.multiple_of(index * size, 8), size)


def joined(p, q):
    top = jnp.maximum(p[0:1, :], q[0:1, :])
    return top, p[1:2, :] * jnp.exp2(p[0:1, :] - top) + q[1:2, :] * jnp.exp2(q[0:1, :] - top)


def lse2(p, q):
    top, total = joined(p, q)
    return top + log2(total)


class Kernels:
    def __init__(self, F, fs, ft, A, Y, half, pb, Q):
        self.F, self.fs, self.ft, self.A, self.Y, self.half, self.pb, self.Q = F, fs, ft, A, Y, half, pb, Q
        self.M, self.N = 2 * pb, A * half
        self.nl, self.nr = self.N // LANES, self.M // LANES
        self.qr = pb // Q
        self.mw = min(self.qr, F)
        self.hw = min(half, pb)

    def prep(self, sources, targets, source_logw, target_logw, times):
        fs, ft, A, half, pb = self.fs, self.ft, self.A, self.half, self.pb

        def body(x, v, la, lb, tm, sent, kept, *rest):
            blocks, side = rest[:A], rest[A]
            _, c, a, _ = position()
            sent[...] = v[:, lanes_at(1 - c, half)]
            kept[0:fs, :] = v[:, lanes_at(c, half)]
            kept[fs : fs + 8, :] = jnp.broadcast_to(lb[0:1, lanes_at(c, half)], (8, half))
            for k in range(A):
                blocks[k][...] = x[:, lanes_at(a ^ k, pb)]
            side[0:4, :] = jnp.broadcast_to(la[0:1, lanes_at(a, pb)], (4, pb))
            side[4:8, :] = jnp.broadcast_to(tm[0:1, lanes_at(a, pb)], (4, pb))

        outs = (sds(fs, half), sds(fs + 8, half), *(sds(ft, pb) for _ in range(A)), sds(8, pb))
        out = call(body, outs, (), 8)(sources, targets, source_logw[None], target_logw[None], times[None])
        return out[0], out[1], out[2 : 2 + A], out[2 + A]

    def cross(self, own, other, pieces):
        F, M, N, A, Y, fs, ft, half, pb, nl = (
            self.F, self.M, self.N, self.A, self.Y, self.fs, self.ft, self.half, self.pb, self.nl,
        )

        def body(own, other, *refs):
            pieces = refs[: A * Y]
            s_ref, xt_ref, yh_ref, yl_ref, hy_ref, rowc_ref, logb_ref, stat_ref = refs[A * Y : A * Y + 8]
            x_ref, y_ref, xh_ref, xl_ref = refs[A * Y + 8 :]
            y, c, a, b = position()
            for k in range(A):
                for q in range(2):
                    at = rows_at((a ^ k) * 2 + (b ^ q), ft)
                    src = slice((q * A + k) * ft, (q * A + k + 1) * ft)
                    x_ref[at, lanes_at(c, pb)] = own[src, :]
                    x_ref[at, lanes_at(1 - c, pb)] = other[src, :]
            for row in range(2):
                rowc_ref[row : row + 1, lanes_at(c, pb)] = own[F + 4 * row : F + 4 * row + 1, :]
                rowc_ref[row : row + 1, lanes_at(1 - c, pb)] = other[F + 4 * row : F + 4 * row + 1, :]
            for k in range(A):
                cols = lanes_at(a ^ k, half)
                for m in range(Y):
                    p = pieces[k * Y + m]
                    y_ref[rows_at((y ^ m) * 2 + c, fs), cols] = p[0:fs, :]
                    y_ref[rows_at((y ^ m) * 2 + (1 - c), fs), cols] = p[fs + 8 : 2 * fs + 8, :]
                logb_ref[0:1, cols] = pieces[k * Y][fs : fs + 1, :]
            for j in range(N // 256):
                cols = slice(j * 256, (j + 1) * 256)
                v = y_ref[:, cols]
                hy_ref[0:1, cols] = (0.5 * L) * jnp.sum(v * v, 0, keepdims=True)
                yh_ref[:, cols], yl_ref[:, cols] = split(v)
            for r in range(self.nr):
                rows = slice(r * LANES, (r + 1) * LANES)
                v = x_ref[:, rows]
                rowc_ref[2:3, rows] = (0.5 * L) * jnp.sum(v * v, 0, keepdims=True)
                vt = v.T
                xt_ref[rows, :] = vt
                xh_ref[rows, :], xl_ref[rows, :] = split(vt * L)
            wide = 512
            deep = min(256, M)
            for r in range(M // deep):
                rows = slice(r * deep, (r + 1) * deep)
                for j in range(N // wide):
                    cols = slice(j * wide, (j + 1) * wide)
                    s = dot3(xh_ref[rows, :], xl_ref[rows, :], yh_ref[:, cols], yl_ref[:, cols], ((1,), (0,)))
                    s_ref[rows, cols] = s - hy_ref[0:1, cols]
                for h in range(deep // LANES):
                    at = r * deep + h * LANES
                    sub = slice(at, at + LANES)
                    top = s_ref[sub, 0:LANES]
                    for l in range(1, nl):
                        top = jnp.maximum(top, s_ref[sub, l * LANES : (l + 1) * LANES])
                    peak = jnp.broadcast_to(jnp.max(top, 1, keepdims=True), (LANES, LANES))
                    acc = jnp.zeros((LANES, LANES), F32)
                    for l in range(nl):
                        acc = acc + jnp.exp2(s_ref[sub, l * LANES : (l + 1) * LANES] - peak)
                    stat_ref[0:1, sub] = jnp.max(top.T, 0, keepdims=True)
                    stat_ref[1:2, sub] = jnp.sum(acc.T, 0, keepdims=True)

        outs = (
            sds(M, N), sds(M, F), sds(F, N, dtype=BF16), sds(F, N, dtype=BF16), sds(1, N), sds(3, M), sds(1, N), sds(2, M),
        )
        scratch = (pltpu.VMEM((F, M), F32), pltpu.VMEM((F, N), F32), pltpu.VMEM((M, F), BF16), pltpu.VMEM((M, F), BF16))
        return call(body, outs, scratch, 20)(own, other, *pieces)

    def fill_cols(self, col_ref, row):
        for r in range(self.nr):
            sub = slice(r * LANES, (r + 1) * LANES)
            col_ref[sub, :] = to_col(row[:, sub])

    def online(self, v, l, m_ref, e_ref):
        lane = slice(l * LANES, (l + 1) * LANES)
        g = groups(v)
        old = m_ref[:, lane]
        new = jnp.maximum(old, jnp.max(g, 0))
        e_ref[:, lane] = e_ref[:, lane] * jnp.exp2(old - new) + jnp.sum(jnp.exp2(g - new[None]), 0)
        m_ref[:, lane] = new

    def finish(self, m_ref, e_ref, out_ref):
        m = m_ref[...]
        top = jnp.max(m, 0, keepdims=True)
        out_ref[0:1, :] = top
        out_ref[1:2, :] = jnp.sum(e_ref[...] * jnp.exp2(m - top), 0, keepdims=True)

    def start(self, m_ref, e_ref):
        m_ref[...] = jnp.full((8, self.N), -1e30, F32)
        e_ref[...] = jnp.zeros((8, self.N), F32)

    def stats(self):
        return pltpu.VMEM((8, self.N), F32), pltpu.VMEM((8, self.N), F32)

    def cols(self):
        return pltpu.VMEM((self.M, LANES), F32)

    def col1(self, s, stat, far, rowc):
        def body(s_ref, stat, far, rowc, f_ref, out_ref, col_ref, m_ref, e_ref):
            f = rowc[0:1, :] * LOG2E - lse2(stat, far)
            f_ref[...] = f
            self.fill_cols(col_ref, f)
            self.start(m_ref, e_ref)

            @pl.loop(0, self.nr)
            def _(r):
                rows = pl.ds(pl.multiple_of(r * LANES, LANES), LANES)
                fc = col_ref[rows, :]
                for l in range(self.nl):
                    self.online(s_ref[rows, l * LANES : (l + 1) * LANES] + fc, l, m_ref, e_ref)

            self.finish(m_ref, e_ref, out_ref)

        return call(body, (sds(1, self.M), sds(2, self.N)), (self.cols(), *self.stats()), 10)(s, stat, far, rowc)

    def row2(self, s, f, stat, far, logb):
        def body(s_ref, f, stat, far, logb, g_ref, out_ref, col_ref):
            g_ref[...] = logb[...] * LOG2E - lse2(stat, far)
            self.fill_cols(col_ref, f)
            for r in range(self.nr):
                rows = slice(r * LANES, (r + 1) * LANES)
                fc = col_ref[rows, :]
                acc = jnp.zeros((LANES, LANES), F32)
                for l in range(self.nl):
                    lane = slice(l * LANES, (l + 1) * LANES)
                    acc = acc + jnp.exp2(s_ref[rows, lane] + fc + g_ref[:, lane])
                out_ref[0:1, rows] = jnp.sum(acc.T, 0, keepdims=True)

        return call(body, (sds(1, self.N), sds(1, self.M)), (self.cols(),), 10)(s, f, stat, far, logb)

    def col2(self, s, f, g, total, far, rowc):
        def body(s_ref, f, g, total, far, rowc, f_ref, out_ref, col_ref, acc_ref):
            f2 = f[...] + rowc[0:1, :] * LOG2E - log2(total[...] + far[...])
            f_ref[...] = f2
            self.fill_cols(col_ref, f2)
            acc_ref[...] = jnp.zeros((8, self.N), F32)

            @pl.loop(0, self.nr)
            def _(r):
                rows = pl.ds(pl.multiple_of(r * LANES, LANES), LANES)
                fc = col_ref[rows, :]
                for l in range(self.nl):
                    lane = slice(l * LANES, (l + 1) * LANES)
                    p = jnp.exp2(s_ref[rows, lane] + fc + g[:, lane])
                    acc_ref[:, lane] = acc_ref[:, lane] + jnp.sum(groups(p), 0)

            out_ref[...] = jnp.sum(acc_ref[...], 0, keepdims=True)

        scratch = (self.cols(), self.stats()[0])
        return call(body, (sds(1, self.M), sds(1, self.N)), scratch, 10)(s, f, g, total, far, rowc)

    def plan(self, s, f, g, total, far, logb, yh, yl, mine, q, base):
        N, F, qr, mw = self.N, self.F, self.qr, self.mw

        def body(s_ref, f, g, total, far, logb, yh, yl, *rest):
            extra, (w_ref, g_ref, ph_ref, pl_ref) = rest[:-4], rest[-4:]
            _, c, _, _ = position()
            at = (c if mine else 1 - c) * self.pb + q * qr
            g_ref[...] = g[...] + logb[...] * LOG2E - log2(total[...] + far[...])
            for r in range(qr // LANES):
                fc = to_col(f[0:1, pl.ds(pl.multiple_of(at + r * LANES, LANES), LANES)])
                rows = pl.ds(pl.multiple_of(at + r * LANES, LANES), LANES)
                local = slice(r * LANES, (r + 1) * LANES)
                acc = jnp.zeros((LANES, LANES), F32)
                for l in range(self.nl):
                    lane = slice(l * LANES, (l + 1) * LANES)
                    p = jnp.exp2(s_ref[rows, lane] + fc + g_ref[:, lane])
                    acc = acc + p
                    ph_ref[local, lane], pl_ref[local, lane] = split(p)
                i, j = divmod(r * LANES, mw)
                mass = jnp.sum(acc.T, 0, keepdims=True)
                if extra:
                    mass = mass + extra[0][qr + i : qr + i + 1, j : j + LANES]
                w_ref[qr + i : qr + i + 1, j : j + LANES] = mass
            w = dot3(ph_ref[...], pl_ref[...], yh[...], yl[...], ((1,), (1,)))
            w_ref[0:qr, :] = w + extra[0][0:qr, :] if extra else w

        scratch = (pltpu.VMEM((1, N), F32), pltpu.VMEM((qr, N), BF16), pltpu.VMEM((qr, N), BF16))
        args = (s, f, g, total, far, logb, yh, yl) + (() if base is None else (base,))
        return call(body, sds(qr + 8, F), scratch, 14)(*args)

    def last(self, own, other, xt, f, rowc, yh, yl, hy, q):
        F, M, N, A, ft, pb, qr, mw = self.F, self.M, self.N, self.A, self.ft, self.pb, self.qr, self.mw

        def entry(*refs):
            ins, outs, (m_ref, e_ref, mt_ref) = refs[:8], refs[8:-3], refs[-3:]
            parcels, out_ref = outs[:A], outs[A]
            body(*ins, parcels, out_ref, m_ref, e_ref, mt_ref)

        def body(own, other, xt, f, rowc, yh, yl, hy, parcels, out_ref, m_ref, e_ref, mt_ref):
            _, c, a, b = position()
            self.start(m_ref, e_ref)
            wide = min(512, N)
            for src, core in ((own, c), (other, 1 - c)):
                for r in range(qr // LANES):
                    at = pl.ds(pl.multiple_of(core * pb + (q * qr + r * LANES), LANES), LANES)
                    i, j = divmod(r * LANES, mw)
                    t = rowc[1:2, at]
                    nx = rowc[2:3, at]
                    keep = jnp.tile(to_col(1.0 - t), (1, F // LANES))
                    take = jnp.tile(to_col(t / src[qr + i : qr + i + 1, j : j + LANES]), (1, F // LANES))
                    mv = keep * xt[at, :] + take * src[r * LANES : (r + 1) * LANES, :]
                    mt = mv.T
                    if src is own:
                        lane = slice(r * LANES, (r + 1) * LANES)
                        mt_ref[:, lane] = mt
                        for k in range(A):
                            parcels[k][ft : ft + 8, lane] = jnp.broadcast_to((EPS * LN2) * (f[0:1, at] + nx), (8, LANES))
                    fc = to_col(f[0:1, at] + nx - (0.5 * L) * jnp.sum(mt * mt, 0, keepdims=True))
                    mh, ml = split(mv * L)
                    for n in range(N // wide):
                        cols = slice(n * wide, (n + 1) * wide)
                        v = dot3(mh, ml, yh[:, cols], yl[:, cols], ((1,), (0,))) - hy[0:1, cols]
                        for l in range(wide // LANES):
                            lane = slice(l * LANES, (l + 1) * LANES)
                            self.online(v[:, lane] + fc, n * (wide // LANES) + l, m_ref, e_ref)
            for k in range(A):
                parcels[k][0:ft, :] = mt_ref[rows_at((a ^ k) * 2 + b, ft), :]
            self.finish(m_ref, e_ref, out_ref)

        outs = (*(sds(ft + 8, qr) for _ in range(A)), sds(2, N))
        out = call(entry, outs, (*self.stats(), pltpu.VMEM((F, qr), F32)), 14)(own, other, xt, f, rowc, yh, yl, hy)
        return out[:A], out[A]

    def pack(self, parcels, stat, far):
        A, Q, ft, qr, pb, half, hw = self.A, self.Q, self.ft, self.qr, self.pb, self.half, self.hw

        def body(*refs):
            parts, (p, q), outs, st = refs[: A * Q], refs[A * Q : A * Q + 2], refs[A * Q + 2 : -1], refs[-1]
            _, _, a, _ = position()
            st[0:1, :], st[1:2, :] = joined(p, q)
            for k in range(A):
                for i in range(Q):
                    outs[k][:, i * qr : (i + 1) * qr] = parts[i * A + k][...]
                for i in range(half // hw):
                    at = pl.ds(pl.multiple_of((a ^ k) * half + i * hw, LANES), hw)
                    outs[k][ft + 1 + 2 * i : ft + 3 + 2 * i, 0:hw] = st[0:2, at]

        outs = tuple(sds(ft + 8, pb) for _ in range(A))
        flat = [p for part in parcels for p in part]
        return call(body, outs, (pltpu.VMEM((2, self.N), F32),), 8)(*flat, stat, far)

    def unpack(self, got, kept):
        A, fs, ft, pb, half, hw = self.A, self.fs, self.ft, self.pb, self.half, self.hw

        def body(*refs):
            got, kept, moved, row_pot, pot = refs[:A], refs[A], refs[A + 1], refs[A + 2], refs[A + 3]
            _, _, a, _ = position()
            for k in range(A):
                cols = lanes_at(a ^ k, pb)
                moved[:, cols] = got[k][0:ft, :]
                row_pot[0:1, cols] = got[k][ft : ft + 1, :]
            for i in range(half // hw):
                tops = [got[k][ft + 1 + 2 * i : ft + 2 + 2 * i, 0:hw] for k in range(A)]
                top = tops[0]
                for v in tops[1:]:
                    top = jnp.maximum(top, v)
                total = jnp.zeros_like(top)
                for k in range(A):
                    total = total + got[k][ft + 2 + 2 * i : ft + 3 + 2 * i, 0:hw] * jnp.exp2(tops[k] - top)
                lanes = slice(i * hw, (i + 1) * hw)
                pot[0:1, lanes] = EPS * (kept[fs : fs + 1, lanes] - LN2 * (top + log2(total)))

        return call(body, (sds(ft, A * pb), sds(1, A * pb), sds(1, half)), (), 8)(*got, kept)

    def pair(self, pot, far):
        def body(p, q, out):
            _, c, _, _ = position()
            out[0:1, lanes_at(c, self.half)] = p[...]
            out[0:1, lanes_at(1 - c, self.half)] = q[...]

        return call(body, sds(1, 2 * self.half), (), 8)(pot, far)


def solution(mesh):
    S, T = mesh.shape["src"], mesh.shape["tgt"]
    Y, A = S // 2, T // 2

    def swap(v, axis, size, k):
        return lax.ppermute(v, axis, [(i, i ^ k) for i in range(size)])

    def over_c(v):
        return swap(v, "src", S, 1)

    def over_y(v, k):
        return swap(v, "src", S, 2 * k)

    def over_b(v):
        return swap(v, "tgt", T, 1)

    def over_a(v, k):
        return swap(v, "tgt", T, 2 * k)

    def join(p, q):
        return jnp.concatenate(joined(p, q))

    def add(p, q):
        return p + q

    def last_two(v, op, sends):
        for send in sends[:-1]:
            v = op(v, send(v))
        return v, sends[-1](v)

    def bits(size):
        return [1 << i for i in range(size.bit_length() - 1)]

    over_rows = [over_c, over_b]
    along_y = [lambda v, k=k: over_y(v, k) for k in bits(Y)]
    over_cols = along_y + [lambda v, k=k: over_a(v, k) for k in bits(A)]

    def per_device(sources, targets, source_logw, target_logw, times):
        ft, ns = sources.shape
        fs, nt = targets.shape
        half, pb = nt // 2, ns // A
        Q = 2 if pb % 256 == 0 else 1
        kern = Kernels(ft * T, fs, ft, A, Y, half, pb, Q)

        sent, kept, blocks, side = kern.prep(sources, targets, source_logw, target_logw, times)
        own = jnp.concatenate([kept, over_c(sent)])
        chunks = {0: own}
        for bit in reversed(bits(A)):
            for k in list(chunks):
                chunks[k ^ bit] = over_a(chunks[k], bit)
        pieces = []
        for k in range(A):
            pieces.append(chunks[k])
            for m in range(1, Y):
                pieces.append(over_y(chunks[k], m))
        parts = [blocks[0]]
        for k in range(1, A):
            parts.append(over_a(blocks[k], k))
        xs = jnp.concatenate(parts)
        xb = over_b(xs)
        x_own = jnp.concatenate([xs, xb, side])
        x_other = over_c(x_own)

        sc, xt, yh, yl, hy, rowc, logb, stat = kern.cross(x_own, x_other, pieces)
        f1, stat = kern.col1(sc, *last_two(stat, join, over_rows), rowc)
        g1, total = kern.row2(sc, f1, *last_two(stat, join, over_cols), logb)
        f2, total = kern.col2(sc, f1, g1, *last_two(total, add, over_rows), rowc)
        total = last_two(total, add, over_cols)

        def plan(mine, q, base):
            return kern.plan(sc, f2, g1, *total, logb, yh, yl, mine, q, base)

        theirs = [over_c(plan(False, q, None)) for q in range(Q)]
        parcels, stat = [], None
        for q in range(Q):
            w = plan(True, q, theirs[q])
            w = w + over_b(w)
            part, fresh = kern.last(w, over_c(w), xt, f2, rowc, yh, yl, hy, q)
            parcels.append(part)
            stat = fresh if stat is None else join(stat, fresh)

        packed = kern.pack(parcels, *last_two(stat, join, along_y))
        got = [packed[0]] + [over_a(packed[k], k) for k in range(1, A)]
        moved, row_pot, pot = kern.unpack(got, kept)
        col_pot = kern.pair(pot, over_c(pot))
        return row_pot[0], moved, col_pot[0]

    placed = (P("tgt", "src"), P("src", "tgt"), P("src"), P("tgt"), P("src"))
    return jax.shard_map(
        per_device,
        mesh=mesh,
        in_specs=placed,
        out_specs=(P("src"), P("tgt", "src"), P("tgt")),
        check_vma=False,
    )
```

time: 446 us -> 144 us (0.32)
  blocking collectives: 131 us -> 0 us
  matrix products: 103 us -> 0 us
  waiting for transfers between devices: 151 us -> 81.4 us
  starting transfers between devices: 0.11 us -> 35.6 us
  other arithmetic: 32.3 us -> 0.34 us
  Pallas kernels: 0 us -> 21.2 us
  between operations: 14.1 us -> 0.89 us
  local copies, waits for them, and re-layouts: 12.6 us -> 4.04 us
    dot_general x28 -> x0, matrix products: 103 us -> none  [the longest x24 92.1 us: cost_block(): jnp.dot(rows, cols.T, precision=lax.Precision.HIGHEST, preferred_element_...]
    ppermute x0 -> x34, waiting for transfers between devices: none -> 81.4 us  [swap(): return lax.ppermute(v, axis, [(i, i ^ k) for i in range(size)])]
    psum x1 -> x0, waiting for transfers between devices: 79.9 us -> none  [per_device(): weighted, mass = lax.psum((weighted, mass), 'tgt')]
    psum x6 -> x0, blocking collectives: 74.9 us -> none  [the longest x2 35.6 us: merge_rows(): total = lax.psum(total * jnp.exp(top - largest), 'tgt')]
    all_gather x2 -> x0, waiting for transfers between devices: 69.7 us -> none  [the longest x1 49.5 us: per_device(): rows_full = lax.all_gather(sources, 'tgt', axis=0, tiled=True).T]
    pmax x5 -> x0, blocking collectives: 55.8 us -> none  [the longest x2 38.3 us: merge_rows(): largest = lax.pmax(top, 'tgt')]
    ppermute x0 -> x34, starting transfers between devices: none -> 35.6 us  [swap(): return lax.ppermute(v, axis, [(i, i ^ k) for i in range(size)])]
    reduce_sum x45 -> x0, other arithmetic: 28.6 us -> none  [the longest x12 16.6 us: step(): jnp.sum(jnp.exp(scores - fresh[None, :]), 0)]
  transfers between devices with their start and end apart: 3 -> 34, of which waited for: 3 -> 24; matrix products, arithmetic and copies ran while one was open for 0% -> 0% of each run, Pallas kernels for 0% -> 5%
where the time goes in v1:
time: 144 us; the launch traced here: 143 us
  waiting for transfers between devices  81.4 us (57%)
  starting transfers between devices  35.6 us (25%)
  Pallas kernels  21.2 us (15%)
  local copies, waits for them, and re-layouts  4.04 us (3%)
    ppermute x34, waiting for transfers between devices, swap(): return lax.ppermute(v, axis, [(i, i ^ k) for i in range(size)])  81.4 us
    ppermute x34, starting transfers between devices, swap(): return lax.ppermute(v, axis, [(i, i ^ k) for i in range(size)])  35.6 us
    pallas_call x4, Pallas kernels, plan(): return call(body, sds(qr + 8, F), scratch, 14)(*args)  5.75 us
    pallas_call x1, Pallas kernels, cross(): return call(body, outs, scratch, 20)(own, other, *pieces)  4.55 us
    pallas_call x2, Pallas kernels, last(): call(entry, outs, (*self.stats(), pltpu.VMEM((F, qr), F32)), 14)  4.47 us
    unnamed x16, local copies, waits for them, and re-layouts  4.02 us
  transfers between devices with their start and end apart: 34, of which 24 were waited for; matrix products, arithmetic and copies ran while one was open for 0% of the time, Pallas kernels for 5%

profile of v1, /device:TPU:0, one launch (start us, length us, event | category | flops | bytes accessed | tf_op | source)
XLA Modules:
  0.0 143.4 jit_solution(16996255447393925116)
XLA Ops:
  4.7 3.1 %collective-permute-start = (f32[32,512]{1,0:T(8,128)S(1)}, f32[32,512]{1,0:T(8,128)S(1)}, u32[]{:S(2)}, u32[]{:S(2)}) collective-permute-start(f32[32,512]{1,0:T(8,128)S(1)} %get-tuple-element.42), channel_id=1, source_target_pairs={{0,2},{1,3},{2,0},{3,1},{4,6},{5,7},{6,4},{7,5},{8,10},{9,11},{10,... | collective-permute-start | bytes 196616 | tf_op jit(solution)/shard_map/ppermute | solution.py:380
  7.8 2.6 %collective-permute-start.1 = (f32[32,512]{1,0:T(8,128)S(1)}, f32[32,512]{1,0:T(8,128)S(1)}, u32[]{:S(2)}, u32[]{:S(2)}) collective-permute-start(f32[32,512]{1,0:T(8,128)S(1)} %get-tuple-element.43), channel_id=1, source_target_pairs={{0,4},{1,5},{2,6},{3,7},{4,0},{5,1},{6,2},{7,3},{8,12},{9,13},{10,... | collective-permute-start | bytes 196616 | tf_op jit(solution)/shard_map/ppermute | solution.py:380
  10.4 4.6 %collective-permute-done.1 = f32[32,512]{1,0:T(8,128)S(1)} collective-permute-done((f32[32,512]{1,0:T(8,128)S(1)}, f32[32,512]{1,0:T(8,128)S(1)}, u32[]{:S(2)}, u32[]{:S(2)}) %collective-permute-start.1) | collective-permute-done | bytes 65568 | tf_op jit(solution)/shard_map/ppermute | solution.py:380
  15.0 1.4 collective-permute-done.2
  16.5 1.6 %collective-permute-start.3 = (f32[128,512]{1,0:T(8,128)S(1)}, f32[128,512]{1,0:T(8,128)S(1)}, u32[]{:S(2)}, u32[]{:S(2)}) collective-permute-start(f32[128,512]{1,0:T(8,128)S(1)} %pad_maximum_fusion), channel_id=1, source_target_pairs={{0,1},{1,0},{2,3},{3,2},{4,5},{5,4},{6,7},{7,6},{8,9},{9,8},{10,11... | collective-permute-start | bytes 786440 | tf_op jit(solution)/shard_map/ppermute | solution.py:380
  18.1 1.6 %collective-permute-start.9 = (f32[136,512]{1,0:T(8,128)S(1)}, f32[136,512]{1,0:T(8,128)S(1)}, u32[]{:S(2)}, u32[]{:S(2)}) collective-permute-start(f32[136,512]{1,0:T(8,128)S(1)} %constant_dynamic-update-slice_fusion.6.refs_0_), channel_id=1, source_target_pairs={{0,4},{1,5},{2,6},{3,7},{4,0},{5,1},{6,2},{7,3},{8,12},{9,13},{10,... | collective-permute-start | bytes 835592 | tf_op jit(solution)/shard_map/ppermute | solution.py:380
  20.5 2.4 %collective-permute-done.3 = f32[128,512]{1,0:T(8,128)S(1)} collective-permute-done((f32[128,512]{1,0:T(8,128)S(1)}, f32[128,512]{1,0:T(8,128)S(1)}, u32[]{:S(2)}, u32[]{:S(2)}) %collective-permute-start.3) | collective-permute-done | bytes 262176 | tf_op jit(solution)/shard_map/ppermute | solution.py:380
  23.0 8.6 %collective-permute-done.9.refs_4_ = f32[136,512]{1,0:T(8,128)S(1)} collective-permute-done((f32[136,512]{1,0:T(8,128)S(1)}, f32[136,512]{1,0:T(8,128)S(1)}, u32[]{:S(2)}, u32[]{:S(2)}) %collective-permute-start.9) | collective-permute-done | bytes 278560 | tf_op jit(solution)/shard_map/ppermute | solution.py:380
  31.6 1.6 %collective-permute-start.6 = (f32[136,512]{1,0:T(8,128)S(1)}, f32[136,512]{1,0:T(8,128)S(1)}, u32[]{:S(2)}, u32[]{:S(2)}) collective-permute-start(f32[136,512]{1,0:T(8,128)S(1)} %constant_dynamic-update-slice_fusion.6.refs_0_), channel_id=1, source_target_pairs={{0,16},{8,24},{16,0},{24,8},{1,17},{9,25},{17,1},{25,9},{2,18},{10... | collective-permute-start | bytes 835592 | tf_op jit(solution)/shard_map/ppermute | solution.py:380
  33.7 1.5 %collective-permute-start.8 = (f32[136,512]{1,0:T(8,128)S(1)}, f32[136,512]{1,0:T(8,128)S(1)}, u32[]{:S(2)}, u32[]{:S(2)}) collective-permute-start(f32[136,512]{1,0:T(8,128)S(1)} %collective-permute-done.7.refs_2_), channel_id=1, source_target_pairs={{0,16},{8,24},{16,0},{24,8},{1,17},{9,25},{17,1},{25,9},{2,18},{10... | collective-permute-start | bytes 835592 | tf_op jit(solution)/shard_map/ppermute | solution.py:380
  35.2 4.7 %collective-permute-done.11.refs_6_ = f32[136,512]{1,0:T(8,128)S(1)} collective-permute-done((f32[136,512]{1,0:T(8,128)S(1)}, f32[136,512]{1,0:T(8,128)S(1)}, u32[]{:S(2)}, u32[]{:S(2)}) %collective-permute-start.11) | collective-permute-done | bytes 278560 | tf_op jit(solution)/shard_map/ppermute | solution.py:380
  40.0 1.5 %collective-permute-start.12 = (f32[136,512]{1,0:T(8,128)S(1)}, f32[136,512]{1,0:T(8,128)S(1)}, u32[]{:S(2)}, u32[]{:S(2)}) collective-permute-start(f32[136,512]{1,0:T(8,128)S(1)} %collective-permute-done.11.refs_6_), channel_id=1, source_target_pairs={{0,16},{8,24},{16,0},{24,8},{1,17},{9,25},{17,1},{25,9},{2,18},{10... | collective-permute-start | bytes 835592 | tf_op jit(solution)/shard_map/ppermute | solution.py:380
  41.5 5.7 %collective-permute-done.10.refs_5_ = f32[136,512]{1,0:T(8,128)S(1)} collective-permute-done((f32[136,512]{1,0:T(8,128)S(1)}, f32[136,512]{1,0:T(8,128)S(1)}, u32[]{:S(2)}, u32[]{:S(2)}) %collective-permute-start.10) | collective-permute-done | bytes 278560 | tf_op jit(solution)/shard_map/ppermute | solution.py:380
  47.2 6.0 %collective-permute-done.8.refs_3_ = f32[136,512]{1,0:T(8,128)S(1)} collective-permute-done((f32[136,512]{1,0:T(8,128)S(1)}, f32[136,512]{1,0:T(8,128)S(1)}, u32[]{:S(2)}, u32[]{:S(2)}) %collective-permute-start.8) | collective-permute-done | bytes 278560 | tf_op jit(solution)/shard_map/ppermute | solution.py:380
  53.1 5.4 %collective-permute-done.12.refs_7_ = f32[136,512]{1,0:T(8,128)S(1)} collective-permute-done((f32[136,512]{1,0:T(8,128)S(1)}, f32[136,512]{1,0:T(8,128)S(1)}, u32[]{:S(2)}, u32[]{:S(2)}) %collective-permute-start.12) | collective-permute-done | bytes 278560 | tf_op jit(solution)/shard_map/ppermute | solution.py:380
  58.6 4.5 %shard_map.77 = (f32[1024,2048]{1,0:T(8,128)S(1)}, f32[1024,256]{1,0:T(8,128)S(1)}, bf16[256,2048]{1,0:T(8,128)(2,1)S(1)}, bf16[256,2048]{1,0:T(8,128)(2,1)S(1)}...) custom-call(f32[264,512]{1,0:T(8,128)S(1)} %constant_dynamic-update-slice_fusion, ...), custom_call_target="tpu_custom_call" | custom-call | tf_op jit(solution)/shard_map/pallas_call | solution.py:167
  65.0 3.1 %collective-permute-done.14.far = f32[2,1024]{1,0:T(2,128)S(1)} collective-permute-done((f32[2,1024]{1,0:T(2,128)S(1)}, f32[2,1024]{1,0:T(2,128)S(1)}, u32[]{:S(2)}, u32[]{:S(2)}) %collective-permute-start.14) | collective-permute-done | bytes 8224 | tf_op jit(solution)/shard_map/ppermute | solution.py:380
  68.1 2.0 %shard_map.78 = (f32[1,1024]{1,0:T(1,128)S(1)}, f32[2,2048]{1,0:T(2,128)S(1)}) custom-call(f32[1024,2048]{1,0:T(8,128)S(1)} %get-tuple-element.48.s_ref, f32[2,1024]{1,0:T(2,128)S(1)} %pad_maximum_fusion.4.stat, f32[2,1024]{1,0:T(2,128)S(1)} %collective-permute-done.14.far, f32[3,1024]{1,0:T(4,128)S(1)} %get-tuple-element.50.rowc.refs_4_), custom_call_target="tpu_custom_call" | custom-call | tf_op jit(solution)/shard_map/pallas_call | solution.py:214
  70.1 1.6 %collective-permute-start.15 = (f32[2,2048]{1,0:T(2,128)S(1)}, f32[2,2048]{1,0:T(2,128)S(1)}, u32[]{:S(2)}, u32[]{:S(2)}) collective-permute-start(f32[2,2048]{1,0:T(2,128)S(1)} %get-tuple-element.52), channel_id=1, source_target_pairs={{0,16},{8,24},{16,0},{24,8},{1,17},{9,25},{17,1},{25,9},{2,18},{10... | collective-permute-start | bytes 49160 | tf_op jit(solution)/shard_map/ppermute | solution.py:380
  71.7 2.2 %collective-permute-done.15 = f32[2,2048]{1,0:T(2,128)S(1)} collective-permute-done((f32[2,2048]{1,0:T(2,128)S(1)}, f32[2,2048]{1,0:T(2,128)S(1)}, u32[]{:S(2)}, u32[]{:S(2)}) %collective-permute-start.15) | collective-permute-done | bytes 16416 | tf_op jit(solution)/shard_map/ppermute | solution.py:380
  74.0 2.1 %collective-permute-start.16 = (f32[2,2048]{1,0:T(2,128)S(1)}, f32[2,2048]{1,0:T(2,128)S(1)}, u32[]{:S(2)}, u32[]{:S(2)}) collective-permute-start(f32[2,2048]{1,0:T(2,128)S(1)} %pad_maximum_fusion.1), channel_id=1, source_target_pairs={{0,2},{1,3},{2,0},{3,1},{4,6},{5,7},{6,4},{7,5},{8,10},{9,11},{10,... | collective-permute-start | bytes 49160 | tf_op jit(solution)/shard_map/ppermute | solution.py:380
  76.1 1.7 %collective-permute-done.16 = f32[2,2048]{1,0:T(2,128)S(1)} collective-permute-done((f32[2,2048]{1,0:T(2,128)S(1)}, f32[2,2048]{1,0:T(2,128)S(1)}, u32[]{:S(2)}, u32[]{:S(2)}) %collective-permute-start.16) | collective-permute-done | bytes 16416 | tf_op jit(solution)/shard_map/ppermute | solution.py:380
  77.9 1.5 %collective-permute-start.17 = (f32[2,2048]{1,0:T(2,128)S(1)}, f32[2,2048]{1,0:T(2,128)S(1)}, u32[]{:S(2)}, u32[]{:S(2)}) collective-permute-start(f32[2,2048]{1,0:T(2,128)S(1)} %pad_maximum_fusion.2.stat), channel_id=1, source_target_pairs={{0,4},{1,5},{2,6},{3,7},{4,0},{5,1},{6,2},{7,3},{8,12},{9,13},{10,... | collective-permute-start | bytes 49160 | tf_op jit(solution)/shard_map/ppermute | solution.py:380
  79.4 3.2 %collective-permute-done.17.far = f32[2,2048]{1,0:T(2,128)S(1)} collective-permute-done((f32[2,2048]{1,0:T(2,128)S(1)}, f32[2,2048]{1,0:T(2,128)S(1)}, u32[]{:S(2)}, u32[]{:S(2)}) %collective-permute-start.17) | collective-permute-done | bytes 16416 | tf_op jit(solution)/shard_map/ppermute | solution.py:380
  82.6 1.3 shard_map.79
  85.6 3.1 %collective-permute-done.19.far = f32[1,1024]{1,0:T(1,128)S(1)} collective-permute-done((f32[1,1024]{1,0:T(1,128)S(1)}, f32[1,1024]{1,0:T(1,128)S(1)}, u32[]{:S(2)}, u32[]{:S(2)}) %collective-permute-start.19) | collective-permute-done | bytes 4128 | tf_op jit(solution)/shard_map/ppermute | solution.py:380
  88.7 1.7 %shard_map.80 = (f32[1,1024]{1,0:T(1,128)S(1)}, f32[1,2048]{1,0:T(1,128)S(1)}) custom-call(f32[1024,2048]{1,0:T(8,128)S(1)} %get-tuple-element.48.s_ref, f32[1,1024]{1,0:T(1,128)S(1)} %get-tuple-element.51.f, f32[1,2048]{1,0:T(1,128)S(1)} %get-tuple-element.54.g, f32[1,1024]{1,0:T(1,128)S(1)} %add.30.total, f32[1,1024]{1,0:T(1,128)S(1)} %collective-permute-done.19.far, ...), custom_call_target="tpu_custom_call" | custom-call | tf_op jit(solution)/shard_map/pallas_call | solution.py:250
  90.5 1.6 %collective-permute-start.20 = (f32[1,2048]{1,0:T(1,128)S(1)}, f32[1,2048]{1,0:T(1,128)S(1)}, u32[]{:S(2)}, u32[]{:S(2)}) collective-permute-start(f32[1,2048]{1,0:T(1,128)S(1)} %get-tuple-element.57), channel_id=1, source_target_pairs={{0,16},{8,24},{16,0},{24,8},{1,17},{9,25},{17,1},{25,9},{2,18},{10... | collective-permute-start | bytes 24584 | tf_op jit(solution)/shard_map/ppermute | solution.py:380
  92.0 2.1 %collective-permute-done.20 = f32[1,2048]{1,0:T(1,128)S(1)} collective-permute-done((f32[1,2048]{1,0:T(1,128)S(1)}, f32[1,2048]{1,0:T(1,128)S(1)}, u32[]{:S(2)}, u32[]{:S(2)}) %collective-permute-start.20) | collective-permute-done | bytes 8224 | tf_op jit(solution)/shard_map/ppermute | solution.py:380
  94.2 2.1 %collective-permute-start.21 = (f32[1,2048]{1,0:T(1,128)S(1)}, f32[1,2048]{1,0:T(1,128)S(1)}, u32[]{:S(2)}, u32[]{:S(2)}) collective-permute-start(f32[1,2048]{1,0:T(1,128)S(1)} %add.31), channel_id=1, source_target_pairs={{0,2},{1,3},{2,0},{3,1},{4,6},{5,7},{6,4},{7,5},{8,10},{9,11},{10,... | collective-permute-start | bytes 24584 | tf_op jit(solution)/shard_map/ppermute | solution.py:380
  96.3 1.6 %collective-permute-done.21 = f32[1,2048]{1,0:T(1,128)S(1)} collective-permute-done((f32[1,2048]{1,0:T(1,128)S(1)}, f32[1,2048]{1,0:T(1,128)S(1)}, u32[]{:S(2)}, u32[]{:S(2)}) %collective-permute-start.21) | collective-permute-done | bytes 8224 | tf_op jit(solution)/shard_map/ppermute | solution.py:380
  97.9 1.5 %collective-permute-start.22 = (f32[1,2048]{1,0:T(1,128)S(1)}, f32[1,2048]{1,0:T(1,128)S(1)}, u32[]{:S(2)}, u32[]{:S(2)}) collective-permute-start(f32[1,2048]{1,0:T(1,128)S(1)} %add.32.total), channel_id=1, source_target_pairs={{0,4},{1,5},{2,6},{3,7},{4,0},{5,1},{6,2},{7,3},{8,12},{9,13},{10,... | collective-permute-start | bytes 24584 | tf_op jit(solution)/shard_map/ppermute | solution.py:380
  99.5 3.1 %collective-permute-done.22.far = f32[1,2048]{1,0:T(1,128)S(1)} collective-permute-done((f32[1,2048]{1,0:T(1,128)S(1)}, f32[1,2048]{1,0:T(1,128)S(1)}, u32[]{:S(2)}, u32[]{:S(2)}) %collective-permute-start.22) | collective-permute-done | bytes 8224 | tf_op jit(solution)/shard_map/ppermute | solution.py:380
  102.5 1.4 %shard_map.81 = f32[264,256]{1,0:T(8,128)S(1)} custom-call(f32[1024,2048]{1,0:T(8,128)S(1)} %get-tuple-element.48.s_ref, f32[1,1024]{1,0:T(1,128)S(1)} %get-tuple-element.56.f.refs_3_, f32[1,2048]{1,0:T(1,128)S(1)} %get-tuple-element.54.g, f32[1,2048]{1,0:T(1,128)S(1)} %add.32.total, f32[1,2048]{1,0:T(1,128)S(1)} %collective-permute-done.22.far, ...), custom_call_target="tpu_custom_call" | custom-call | tf_op jit(solution)/shard_map/pallas_call | solution.py:280
  104.1 1.4 %shard_map.84 = f32[264,256]{1,0:T(8,128)S(1)} custom-call(f32[1024,2048]{1,0:T(8,128)S(1)} %get-tuple-element.48.s_ref, f32[1,1024]{1,0:T(1,128)S(1)} %get-tuple-element.56.f.refs_3_, f32[1,2048]{1,0:T(1,128)S(1)} %get-tuple-element.54.g, f32[1,2048]{1,0:T(1,128)S(1)} %add.32.total, f32[1,2048]{1,0:T(1,128)S(1)} %collective-permute-done.22.far, ...), custom_call_target="tpu_custom_call" | custom-call | tf_op jit(solution)/shard_map/pallas_call | solution.py:280
  106.1 1.4 %shard_map.82 = f32[264,256]{1,0:T(8,128)S(1)} custom-call(f32[1024,2048]{1,0:T(8,128)S(1)} %get-tuple-element.48.s_ref, f32[1,1024]{1,0:T(1,128)S(1)} %get-tuple-element.56.f.refs_3_, f32[1,2048]{1,0:T(1,128)S(1)} %get-tuple-element.54.g, f32[1,2048]{1,0:T(1,128)S(1)} %add.32.total, f32[1,2048]{1,0:T(1,128)S(1)} %collective-permute-done.22.far, ...), custom_call_target="tpu_custom_call" | custom-call | tf_op jit(solution)/shard_map/pallas_call | solution.py:280
  108.1 1.4 %shard_map.85 = f32[264,256]{1,0:T(8,128)S(1)} custom-call(f32[1024,2048]{1,0:T(8,128)S(1)} %get-tuple-element.48.s_ref, f32[1,1024]{1,0:T(1,128)S(1)} %get-tuple-element.56.f.refs_3_, f32[1,2048]{1,0:T(1,128)S(1)} %get-tuple-element.54.g, f32[1,2048]{1,0:T(1,128)S(1)} %add.32.total, f32[1,2048]{1,0:T(1,128)S(1)} %collective-permute-done.22.far, ...), custom_call_target="tpu_custom_call" | custom-call | tf_op jit(solution)/shard_map/pallas_call | solution.py:280
  109.6 1.6 %collective-permute-start.27 = (f32[264,256]{1,0:T(8,128)S(1)}, f32[264,256]{1,0:T(8,128)S(1)}, u32[]{:S(2)}, u32[]{:S(2)}) collective-permute-start(f32[264,256]{1,0:T(8,128)S(1)} %shard_map.85), channel_id=1, source_target_pairs={{0,1},{1,0},{2,3},{3,2},{4,5},{5,4},{6,7},{7,6},{8,9},{9,8},{10,11... | collective-permute-start | bytes 811016 | tf_op jit(solution)/shard_map/ppermute | solution.py:380
  111.1 5.8 %collective-permute-done.24 = f32[264,256]{1,0:T(8,128)S(1)} collective-permute-done((f32[264,256]{1,0:T(8,128)S(1)}, f32[264,256]{1,0:T(8,128)S(1)}, u32[]{:S(2)}, u32[]{:S(2)}) %collective-permute-start.24) | collective-permute-done | bytes 270368 | tf_op jit(solution)/shard_map/ppermute | solution.py:380
  117.1 4.7 %collective-permute-done.27 = f32[264,256]{1,0:T(8,128)S(1)} collective-permute-done((f32[264,256]{1,0:T(8,128)S(1)}, f32[264,256]{1,0:T(8,128)S(1)}, u32[]{:S(2)}, u32[]{:S(2)}) %collective-permute-start.27) | collective-permute-done | bytes 270368 | tf_op jit(solution)/shard_map/ppermute | solution.py:380
  121.9 2.2 %shard_map.83 = (f32[40,256]{1,0:T(8,128)S(1)}, f32[40,256]{1,0:T(8,128)S(1)}, f32[40,256]{1,0:T(8,128)S(1)}, f32[40,256]{1,0:T(8,128)S(1)}, f32[2,2048]{1,0:T(2,128)S(1)}) custom-call(f32[264,256]{1,0:T(8,128)S(1)} %add.33.refs_0_, f32[264,256]{1,0:T(8,128)S(1)} %collective-permute-done.25.refs_1_, f32[1024,256]{1,0:T(8,128)S(1)} %get-tuple-element.60.refs_2_, ...), custom_call_target="tpu_custom_call" | custom-call | tf_op jit(solution)/shard_map/pallas_call | solution.py:322
  124.2 2.2 %shard_map.86 = (f32[40,256]{1,0:T(8,128)S(1)}, f32[40,256]{1,0:T(8,128)S(1)}, f32[40,256]{1,0:T(8,128)S(1)}, f32[40,256]{1,0:T(8,128)S(1)}, f32[2,2048]{1,0:T(2,128)S(1)}) custom-call(f32[264,256]{1,0:T(8,128)S(1)} %add.34.refs_0_, f32[264,256]{1,0:T(8,128)S(1)} %collective-permute-done.28.refs_1_, f32[1024,256]{1,0:T(8,128)S(1)} %get-tuple-element.60.refs_2_, ...), custom_call_target="tpu_custom_call" | custom-call | tf_op jit(solution)/shard_map/pallas_call | solution.py:322
  126.5 1.6 %collective-permute-start.29 = (f32[2,2048]{1,0:T(2,128)S(1)}, f32[2,2048]{1,0:T(2,128)S(1)}, u32[]{:S(2)}, u32[]{:S(2)}) collective-permute-start(f32[2,2048]{1,0:T(2,128)S(1)} %pad_maximum_fusion.3.refs_8_), channel_id=1, source_target_pairs={{0,16},{8,24},{16,0},{24,8},{1,17},{9,25},{17,1},{25,9},{2,18},{10... | collective-permute-start | bytes 49160 | tf_op jit(solution)/shard_map/ppermute | solution.py:380
  128.1 2.2 %collective-permute-done.29.refs_9_ = f32[2,2048]{1,0:T(2,128)S(1)} collective-permute-done((f32[2,2048]{1,0:T(2,128)S(1)}, f32[2,2048]{1,0:T(2,128)S(1)}, u32[]{:S(2)}, u32[]{:S(2)}) %collective-permute-start.29) | collective-permute-done | bytes 16416 | tf_op jit(solution)/shard_map/ppermute | solution.py:380
  130.3 2.1 %collective-permute-start.30 = (f32[40,512]{1,0:T(8,128)S(1)}, f32[40,512]{1,0:T(8,128)S(1)}, u32[]{:S(2)}, u32[]{:S(2)}) collective-permute-start(f32[40,512]{1,0:T(8,128)S(1)} %get-tuple-element.73), channel_id=1, source_target_pairs={{0,2},{1,3},{2,0},{3,1},{4,6},{5,7},{6,4},{7,5},{8,10},{9,11},{10,... | collective-permute-start | bytes 245768 | tf_op jit(solution)/shard_map/ppermute | solution.py:380
  132.4 2.4 %collective-permute-start.32 = (f32[40,512]{1,0:T(8,128)S(1)}, f32[40,512]{1,0:T(8,128)S(1)}, u32[]{:S(2)}, u32[]{:S(2)}) collective-permute-start(f32[40,512]{1,0:T(8,128)S(1)} %get-tuple-element.75), channel_id=1, source_target_pairs={{0,6},{1,7},{2,4},{3,5},{4,2},{5,3},{6,0},{7,1},{8,14},{9,15},{10,... | collective-permute-start | bytes 245768 | tf_op jit(solution)/shard_map/ppermute | solution.py:380
  135.0 6.0 %collective-permute-done.31.refs_2_ = f32[40,512]{1,0:T(8,128)S(1)} collective-permute-done((f32[40,512]{1,0:T(8,128)S(1)}, f32[40,512]{1,0:T(8,128)S(1)}, u32[]{:S(2)}, u32[]{:S(2)}) %collective-permute-start.31) | collective-permute-done | bytes 81952 | tf_op jit(solution)/shard_map/ppermute | solution.py:380
  141.7 1.2 collective-permute-done.33.q
  (66 shorter events, 12.2 us)
Async XLA Ops:
  0.6 1.0 copy-start
  1.6 0.9 copy-start.1
  2.5 0.7 copy-start.2
  3.2 0.7 copy-start.3
  3.9 0.7 copy-start.4
  4.7 5.7 %collective-permute-start = (f32[32,512]{1,0:T(8,128)S(1)}, f32[32,512]{1,0:T(8,128)S(1)}, u32[]{:S(2)}, u32[]{:S(2)}) collective-permute-start(f32[32,512]{1,0:T(8,128)S(1)} %get-tuple-element.42), channel_id=1, source_target_pairs={{0,2},{1,3},{2,0},{3,1},{4,6},{5,7},{6,4},{7,5},{8,10},{9,11},{10,... | collective-permute-start | bytes 196616 | tf_op jit(solution)/shard_map/ppermute | solution.py:380
  7.8 7.3 %collective-permute-start.1 = (f32[32,512]{1,0:T(8,128)S(1)}, f32[32,512]{1,0:T(8,128)S(1)}, u32[]{:S(2)}, u32[]{:S(2)}) collective-permute-start(f32[32,512]{1,0:T(8,128)S(1)} %get-tuple-element.43), channel_id=1, source_target_pairs={{0,4},{1,5},{2,6},{3,7},{4,0},{5,1},{6,2},{7,3},{8,12},{9,13},{10,... | collective-permute-start | bytes 196616 | tf_op jit(solution)/shard_map/ppermute | solution.py:380
  10.4 6.1 %collective-permute-start.2 = (f32[32,512]{1,0:T(8,128)S(1)}, f32[32,512]{1,0:T(8,128)S(1)}, u32[]{:S(2)}, u32[]{:S(2)}) collective-permute-start(f32[32,512]{1,0:T(8,128)S(1)} %get-tuple-element.44), channel_id=1, source_target_pairs={{0,6},{1,7},{2,4},{3,5},{4,2},{5,3},{6,0},{7,1},{8,14},{9,15},{10,... | collective-permute-start | bytes 196616 | tf_op jit(solution)/shard_map/ppermute | solution.py:380
  10.4 7.7 %collective-permute-start.5 = (f32[64,512]{1,0:T(8,128)S(1)}, f32[64,512]{1,0:T(8,128)S(1)}, u32[]{:S(2)}, u32[]{:S(2)}) collective-permute-start(f32[64,512]{1,0:T(8,128)S(1)} %get-tuple-element.47), channel_id=1, source_target_pairs={{0,8},{8,0},{16,24},{24,16},{1,9},{9,1},{17,25},{25,17},{2,10},{10... | collective-permute-start | bytes 393224 | tf_op jit(solution)/shard_map/ppermute | solution.py:380
  16.5 6.5 %collective-permute-start.3 = (f32[128,512]{1,0:T(8,128)S(1)}, f32[128,512]{1,0:T(8,128)S(1)}, u32[]{:S(2)}, u32[]{:S(2)}) collective-permute-start(f32[128,512]{1,0:T(8,128)S(1)} %pad_maximum_fusion), channel_id=1, source_target_pairs={{0,1},{1,0},{2,3},{3,2},{4,5},{5,4},{6,7},{7,6},{8,9},{9,8},{10,11... | collective-permute-start | bytes 786440 | tf_op jit(solution)/shard_map/ppermute | solution.py:380
  18.1 13.5 %collective-permute-start.9 = (f32[136,512]{1,0:T(8,128)S(1)}, f32[136,512]{1,0:T(8,128)S(1)}, u32[]{:S(2)}, u32[]{:S(2)}) collective-permute-start(f32[136,512]{1,0:T(8,128)S(1)} %constant_dynamic-update-slice_fusion.6.refs_0_), channel_id=1, source_target_pairs={{0,4},{1,5},{2,6},{3,7},{4,0},{5,1},{6,2},{7,3},{8,12},{9,13},{10,... | collective-permute-start | bytes 835592 | tf_op jit(solution)/shard_map/ppermute | solution.py:380
  19.7 14.0 %collective-permute-start.7 = (f32[136,512]{1,0:T(8,128)S(1)}, f32[136,512]{1,0:T(8,128)S(1)}, u32[]{:S(2)}, u32[]{:S(2)}) collective-permute-start(f32[136,512]{1,0:T(8,128)S(1)} %constant_dynamic-update-slice_fusion.6.refs_0_), channel_id=1, source_target_pairs={{0,2},{1,3},{2,0},{3,1},{4,6},{5,7},{6,4},{7,5},{8,10},{9,11},{10,... | collective-permute-start | bytes 835592 | tf_op jit(solution)/shard_map/ppermute | solution.py:380
  31.6 8.4 %collective-permute-start.11 = (f32[136,512]{1,0:T(8,128)S(1)}, f32[136,512]{1,0:T(8,128)S(1)}, u32[]{:S(2)}, u32[]{:S(2)}) collective-permute-start(f32[136,512]{1,0:T(8,128)S(1)} %collective-permute-done.9.refs_4_), channel_id=1, source_target_pairs={{0,2},{1,3},{2,0},{3,1},{4,6},{5,7},{6,4},{7,5},{8,10},{9,11},{10,... | collective-permute-start | bytes 835592 | tf_op jit(solution)/shard_map/ppermute | solution.py:380
  31.6 21.5 %collective-permute-start.4 = (f32[264,512]{1,0:T(8,128)S(1)}, f32[264,512]{1,0:T(8,128)S(1)}, u32[]{:S(2)}, u32[]{:S(2)}) collective-permute-start(f32[264,512]{1,0:T(8,128)S(1)} %constant_dynamic-update-slice_fusion.own), channel_id=1, source_target_pairs={{0,8},{8,0},{16,24},{24,16},{1,9},{9,1},{17,25},{25,17},{2,10},{10... | collective-permute-start | bytes 1622024 | tf_op jit(solution)/shard_map/ppermute | solution.py:380
  31.6 9.9 %collective-permute-start.6 = (f32[136,512]{1,0:T(8,128)S(1)}, f32[136,512]{1,0:T(8,128)S(1)}, u32[]{:S(2)}, u32[]{:S(2)}) collective-permute-start(f32[136,512]{1,0:T(8,128)S(1)} %constant_dynamic-update-slice_fusion.6.refs_0_), channel_id=1, source_target_pairs={{0,16},{8,24},{16,0},{24,8},{1,17},{9,25},{17,1},{25,9},{2,18},{10... | collective-permute-start | bytes 835592 | tf_op jit(solution)/shard_map/ppermute | solution.py:380
  33.2 14.0 %collective-permute-start.10 = (f32[136,512]{1,0:T(8,128)S(1)}, f32[136,512]{1,0:T(8,128)S(1)}, u32[]{:S(2)}, u32[]{:S(2)}) collective-permute-start(f32[136,512]{1,0:T(8,128)S(1)} %collective-permute-done.9.refs_4_), channel_id=1, source_target_pairs={{0,16},{8,24},{16,0},{24,8},{1,17},{9,25},{17,1},{25,9},{2,18},{10... | collective-permute-start | bytes 835592 | tf_op jit(solution)/shard_map/ppermute | solution.py:380
  33.7 19.4 %collective-permute-start.8 = (f32[136,512]{1,0:T(8,128)S(1)}, f32[136,512]{1,0:T(8,128)S(1)}, u32[]{:S(2)}, u32[]{:S(2)}) collective-permute-start(f32[136,512]{1,0:T(8,128)S(1)} %collective-permute-done.7.refs_2_), channel_id=1, source_target_pairs={{0,16},{8,24},{16,0},{24,8},{1,17},{9,25},{17,1},{25,9},{2,18},{10... | collective-permute-start | bytes 835592 | tf_op jit(solution)/shard_map/ppermute | solution.py:380
  40.0 18.6 %collective-permute-start.12 = (f32[136,512]{1,0:T(8,128)S(1)}, f32[136,512]{1,0:T(8,128)S(1)}, u32[]{:S(2)}, u32[]{:S(2)}) collective-permute-start(f32[136,512]{1,0:T(8,128)S(1)} %collective-permute-done.11.refs_6_), channel_id=1, source_target_pairs={{0,16},{8,24},{16,0},{24,8},{1,17},{9,25},{17,1},{25,9},{2,18},{10... | collective-permute-start | bytes 835592 | tf_op jit(solution)/shard_map/ppermute | solution.py:380
  63.1 1.2 collective-permute-start.13
  64.4 3.7 %collective-permute-start.14 = (f32[2,1024]{1,0:T(2,128)S(1)}, f32[2,1024]{1,0:T(2,128)S(1)}, u32[]{:S(2)}, u32[]{:S(2)}) collective-permute-start(f32[2,1024]{1,0:T(2,128)S(1)} %pad_maximum_fusion.4.stat), channel_id=1, source_target_pairs={{0,1},{1,0},{2,3},{3,2},{4,5},{5,4},{6,7},{7,6},{8,9},{9,8},{10,11... | collective-permute-start | bytes 24584 | tf_op jit(solution)/shard_map/ppermute | solution.py:380
  70.1 3.8 %collective-permute-start.15 = (f32[2,2048]{1,0:T(2,128)S(1)}, f32[2,2048]{1,0:T(2,128)S(1)}, u32[]{:S(2)}, u32[]{:S(2)}) collective-permute-start(f32[2,2048]{1,0:T(2,128)S(1)} %get-tuple-element.52), channel_id=1, source_target_pairs={{0,16},{8,24},{16,0},{24,8},{1,17},{9,25},{17,1},{25,9},{2,18},{10... | collective-permute-start | bytes 49160 | tf_op jit(solution)/shard_map/ppermute | solution.py:380
  74.0 3.8 %collective-permute-start.16 = (f32[2,2048]{1,0:T(2,128)S(1)}, f32[2,2048]{1,0:T(2,128)S(1)}, u32[]{:S(2)}, u32[]{:S(2)}) collective-permute-start(f32[2,2048]{1,0:T(2,128)S(1)} %pad_maximum_fusion.1), channel_id=1, source_target_pairs={{0,2},{1,3},{2,0},{3,1},{4,6},{5,7},{6,4},{7,5},{8,10},{9,11},{10,... | collective-permute-start | bytes 49160 | tf_op jit(solution)/shard_map/ppermute | solution.py:380
  77.9 4.7 %collective-permute-start.17 = (f32[2,2048]{1,0:T(2,128)S(1)}, f32[2,2048]{1,0:T(2,128)S(1)}, u32[]{:S(2)}, u32[]{:S(2)}) collective-permute-start(f32[2,2048]{1,0:T(2,128)S(1)} %pad_maximum_fusion.2.stat), channel_id=1, source_target_pairs={{0,4},{1,5},{2,6},{3,7},{4,0},{5,1},{6,2},{7,3},{8,12},{9,13},{10,... | collective-permute-start | bytes 49160 | tf_op jit(solution)/shard_map/ppermute | solution.py:380
  83.9 1.2 collective-permute-start.18
  85.1 3.6 %collective-permute-start.19 = (f32[1,1024]{1,0:T(1,128)S(1)}, f32[1,1024]{1,0:T(1,128)S(1)}, u32[]{:S(2)}, u32[]{:S(2)}) collective-permute-start(f32[1,1024]{1,0:T(1,128)S(1)} %add.30.total), channel_id=1, source_target_pairs={{0,1},{1,0},{2,3},{3,2},{4,5},{5,4},{6,7},{7,6},{8,9},{9,8},{10,11... | collective-permute-start | bytes 12296 | tf_op jit(solution)/shard_map/ppermute | solution.py:380
  90.5 3.7 %collective-permute-start.20 = (f32[1,2048]{1,0:T(1,128)S(1)}, f32[1,2048]{1,0:T(1,128)S(1)}, u32[]{:S(2)}, u32[]{:S(2)}) collective-permute-start(f32[1,2048]{1,0:T(1,128)S(1)} %get-tuple-element.57), channel_id=1, source_target_pairs={{0,16},{8,24},{16,0},{24,8},{1,17},{9,25},{17,1},{25,9},{2,18},{10... | collective-permute-start | bytes 24584 | tf_op jit(solution)/shard_map/ppermute | solution.py:380
  94.2 3.7 %collective-permute-start.21 = (f32[1,2048]{1,0:T(1,128)S(1)}, f32[1,2048]{1,0:T(1,128)S(1)}, u32[]{:S(2)}, u32[]{:S(2)}) collective-permute-start(f32[1,2048]{1,0:T(1,128)S(1)} %add.31), channel_id=1, source_target_pairs={{0,2},{1,3},{2,0},{3,1},{4,6},{5,7},{6,4},{7,5},{8,10},{9,11},{10,... | collective-permute-start | bytes 24584 | tf_op jit(solution)/shard_map/ppermute | solution.py:380
  97.9 4.6 %collective-permute-start.22 = (f32[1,2048]{1,0:T(1,128)S(1)}, f32[1,2048]{1,0:T(1,128)S(1)}, u32[]{:S(2)}, u32[]{:S(2)}) collective-permute-start(f32[1,2048]{1,0:T(1,128)S(1)} %add.32.total), channel_id=1, source_target_pairs={{0,4},{1,5},{2,6},{3,7},{4,0},{5,1},{6,2},{7,3},{8,12},{9,13},{10,... | collective-permute-start | bytes 24584 | tf_op jit(solution)/shard_map/ppermute | solution.py:380
  104.0 2.1 %collective-permute-start.23 = (f32[264,256]{1,0:T(8,128)S(1)}, f32[264,256]{1,0:T(8,128)S(1)}, u32[]{:S(2)}, u32[]{:S(2)}) collective-permute-start(f32[264,256]{1,0:T(8,128)S(1)} %shard_map.81), channel_id=1, source_target_pairs={{0,8},{8,0},{16,24},{24,16},{1,9},{9,1},{17,25},{25,17},{2,10},{10... | collective-permute-start | bytes 811016 | tf_op jit(solution)/shard_map/ppermute | solution.py:380
  105.5 2.6 %collective-permute-start.26 = (f32[264,256]{1,0:T(8,128)S(1)}, f32[264,256]{1,0:T(8,128)S(1)}, u32[]{:S(2)}, u32[]{:S(2)}) collective-permute-start(f32[264,256]{1,0:T(8,128)S(1)} %shard_map.84), channel_id=1, source_target_pairs={{0,8},{8,0},{16,24},{24,16},{1,9},{9,1},{17,25},{25,17},{2,10},{10... | collective-permute-start | bytes 811016 | tf_op jit(solution)/shard_map/ppermute | solution.py:380
  107.5 9.4 %collective-permute-start.24 = (f32[264,256]{1,0:T(8,128)S(1)}, f32[264,256]{1,0:T(8,128)S(1)}, u32[]{:S(2)}, u32[]{:S(2)}) collective-permute-start(f32[264,256]{1,0:T(8,128)S(1)} %shard_map.82), channel_id=1, source_target_pairs={{0,1},{1,0},{2,3},{3,2},{4,5},{5,4},{6,7},{7,6},{8,9},{9,8},{10,11... | collective-permute-start | bytes 811016 | tf_op jit(solution)/shard_map/ppermute | solution.py:380
  109.6 12.2 %collective-permute-start.27 = (f32[264,256]{1,0:T(8,128)S(1)}, f32[264,256]{1,0:T(8,128)S(1)}, u32[]{:S(2)}, u32[]{:S(2)}) collective-permute-start(f32[264,256]{1,0:T(8,128)S(1)} %shard_map.85), channel_id=1, source_target_pairs={{0,1},{1,0},{2,3},{3,2},{4,5},{5,4},{6,7},{7,6},{8,9},{9,8},{10,11... | collective-permute-start | bytes 811016 | tf_op jit(solution)/shard_map/ppermute | solution.py:380
  117.0 4.9 %collective-permute-start.25 = (f32[264,256]{1,0:T(8,128)S(1)}, f32[264,256]{1,0:T(8,128)S(1)}, u32[]{:S(2)}, u32[]{:S(2)}) collective-permute-start(f32[264,256]{1,0:T(8,128)S(1)} %add.33.refs_0_), channel_id=1, source_target_pairs={{0,8},{8,0},{16,24},{24,16},{1,9},{9,1},{17,25},{25,17},{2,10},{10... | collective-permute-start | bytes 811016 | tf_op jit(solution)/shard_map/ppermute | solution.py:380
  121.8 2.3 %collective-permute-start.28 = (f32[264,256]{1,0:T(8,128)S(1)}, f32[264,256]{1,0:T(8,128)S(1)}, u32[]{:S(2)}, u32[]{:S(2)}) collective-permute-start(f32[264,256]{1,0:T(8,128)S(1)} %add.34.refs_0_), channel_id=1, source_target_pairs={{0,8},{8,0},{16,24},{24,16},{1,9},{9,1},{17,25},{25,17},{2,10},{10... | collective-permute-start | bytes 811016 | tf_op jit(solution)/shard_map/ppermute | solution.py:380
  126.5 3.8 %collective-permute-start.29 = (f32[2,2048]{1,0:T(2,128)S(1)}, f32[2,2048]{1,0:T(2,128)S(1)}, u32[]{:S(2)}, u32[]{:S(2)}) collective-permute-start(f32[2,2048]{1,0:T(2,128)S(1)} %pad_maximum_fusion.3.refs_8_), channel_id=1, source_target_pairs={{0,16},{8,24},{16,0},{24,8},{1,17},{9,25},{17,1},{25,9},{2,18},{10... | collective-permute-start | bytes 49160 | tf_op jit(solution)/shard_map/ppermute | solution.py:380
  130.3 4.6 %collective-permute-start.30 = (f32[40,512]{1,0:T(8,128)S(1)}, f32[40,512]{1,0:T(8,128)S(1)}, u32[]{:S(2)}, u32[]{:S(2)}) collective-permute-start(f32[40,512]{1,0:T(8,128)S(1)} %get-tuple-element.73), channel_id=1, source_target_pairs={{0,2},{1,3},{2,0},{3,1},{4,6},{5,7},{6,4},{7,5},{8,10},{9,11},{10,... | collective-permute-start | bytes 245768 | tf_op jit(solution)/shard_map/ppermute | solution.py:380
  132.4 8.5 %collective-permute-start.31 = (f32[40,512]{1,0:T(8,128)S(1)}, f32[40,512]{1,0:T(8,128)S(1)}, u32[]{:S(2)}, u32[]{:S(2)}) collective-permute-start(f32[40,512]{1,0:T(8,128)S(1)} %get-tuple-element.74), channel_id=1, source_target_pairs={{0,4},{1,5},{2,6},{3,7},{4,0},{5,1},{6,2},{7,3},{8,12},{9,13},{10,... | collective-permute-start | bytes 245768 | tf_op jit(solution)/shard_map/ppermute | solution.py:380
  132.4 8.5 %collective-permute-start.32 = (f32[40,512]{1,0:T(8,128)S(1)}, f32[40,512]{1,0:T(8,128)S(1)}, u32[]{:S(2)}, u32[]{:S(2)}) collective-permute-start(f32[40,512]{1,0:T(8,128)S(1)} %get-tuple-element.75), channel_id=1, source_target_pairs={{0,6},{1,7},{2,4},{3,5},{4,2},{5,3},{6,0},{7,1},{8,14},{9,15},{10,... | collective-permute-start | bytes 245768 | tf_op jit(solution)/shard_map/ppermute | solution.py:380
  141.7 1.2 collective-permute-start.33

commit v2 on v1

--- a/solution.py
+++ b/solution.py
@@ -64,14 +64,23 @@
     return pl.ds(pl.multiple_of(index * size, 8), size)
 
 
-def joined(p, q):
-    top = jnp.maximum(p[0:1, :], q[0:1, :])
-    return top, p[1:2, :] * jnp.exp2(p[0:1, :] - top) + q[1:2, :] * jnp.exp2(q[0:1, :] - top)
-
-
-def lse2(p, q):
-    top, total = joined(p, q)
-    return top + log2(total)
+def joined(values):
+    top = values[0][0:1, :]
+    for v in values[1:]:
+        top = jnp.maximum(top, v[0:1, :])
+    return top, total([v[1:2, :] * jnp.exp2(v[0:1, :] - top) for v in values])
+
+
+def total(values):
+    acc = values[0][...]
+    for v in values[1:]:
+        acc = acc + v[...]
+    return acc
+
+
+def lse2(values):
+    top, acc = joined(values)
+    return top + log2(acc)
 
 
 class Kernels:
@@ -81,24 +90,42 @@
         self.nl, self.nr = self.N // LANES, self.M // LANES
         self.qr = pb // Q
         self.mw = min(self.qr, F)
-        self.hw = min(half, pb)
+        self.hw = min(half, self.qr)
+        self.tail = -(-(1 + 2 * (half // self.hw)) // 8) * 8
 
     def prep(self, sources, targets, source_logw, target_logw, times):
         fs, ft, A, half, pb = self.fs, self.ft, self.A, self.half, self.pb
 
         def body(x, v, la, lb, tm, sent, kept, *rest):
-            blocks, side = rest[:A], rest[A]
+            blocks, side, row, sems = rest[:A], rest[A], rest[A + 1], rest[A + 2]
             _, c, a, _ = position()
-            sent[...] = v[:, lanes_at(1 - c, half)]
-            kept[0:fs, :] = v[:, lanes_at(c, half)]
-            kept[fs : fs + 8, :] = jnp.broadcast_to(lb[0:1, lanes_at(c, half)], (8, half))
-            for k in range(A):
-                blocks[k][...] = x[:, lanes_at(a ^ k, pb)]
-            side[0:4, :] = jnp.broadcast_to(la[0:1, lanes_at(a, pb)], (4, pb))
-            side[4:8, :] = jnp.broadcast_to(tm[0:1, lanes_at(a, pb)], (4, pb))
+            pairs = [
+                (v.at[:, lanes_at(1 - c, half)], sent),
+                (v.at[:, lanes_at(c, half)], kept.at[0:fs, :]),
+                (lb.at[:, lanes_at(c, half)], row.at[0:1, 0:half]),
+                (la.at[:, lanes_at(a, pb)], row.at[1:2, 0:pb]),
+                (tm.at[:, lanes_at(a, pb)], row.at[2:3, 0:pb]),
+            ] + [(x.at[:, lanes_at(a ^ k, pb)], blocks[k]) for k in range(A)]
+            copies = [pltpu.make_async_copy(p, q, sems.at[n]) for n, (p, q) in enumerate(pairs)]
+            for copy in copies:
+                copy.start()
+            for copy in copies:
+                copy.wait()
+            kept[fs : fs + 8, :] = jnp.broadcast_to(row[0:1, 0:half], (8, half))
+            side[0:4, :] = jnp.broadcast_to(row[1:2, 0:pb], (4, pb))
+            side[4:8, :] = jnp.broadcast_to(row[2:3, 0:pb], (4, pb))
 
         outs = (sds(fs, half), sds(fs + 8, half), *(sds(ft, pb) for _ in range(A)), sds(8, pb))
-        out = call(body, outs, (), 8)(sources, targets, source_logw[None], target_logw[None], times[None])
+        out = pl.pallas_call(
+            body,
+            in_specs=[pl.BlockSpec(memory_space=pltpu.MemorySpace.HBM)] * 5,
+            out_shape=outs,
+            scratch_shapes=(pltpu.VMEM((8, max(half, pb)), F32), pltpu.SemaphoreType.DMA((5 + A,))),
+            compiler_params=pltpu.CompilerParams(vmem_limit_bytes=8 * MB),
+        )(*(
+            pltpu.with_memory_space_constraint(v, pltpu.MemorySpace.HBM)
+            for v in (sources, targets, source_logw[None], target_logw[None], times[None])
+        ))
         return out[0], out[1], out[2 : 2 + A], out[2 + A]
 
     def cross(self, own, other, pieces):
@@ -107,9 +134,9 @@
         )
 
         def body(own, other, *refs):
-            pieces = refs[: A * Y]
-            s_ref, xt_ref, yh_ref, yl_ref, hy_ref, rowc_ref, logb_ref, stat_ref = refs[A * Y : A * Y + 8]
-            x_ref, y_ref, xh_ref, xl_ref = refs[A * Y + 8 :]
+            few = len(pieces)
+            s_ref, xt_ref, yh_ref, yl_ref, hy_ref, rowc_ref, logb_ref, stat_ref = refs[few : few + 8]
+            x_ref, y_ref, xh_ref, xl_ref = refs[few + 8 :]
             y, c, a, b = position()
             for k in range(A):
                 for q in range(2):
@@ -120,13 +147,15 @@
             for row in range(2):
                 rowc_ref[row : row + 1, lanes_at(c, pb)] = own[F + 4 * row : F + 4 * row + 1, :]
                 rowc_ref[row : row + 1, lanes_at(1 - c, pb)] = other[F + 4 * row : F + 4 * row + 1, :]
-            for k in range(A):
+            for (k, m, near, away, _), p in zip(pieces, refs):
                 cols = lanes_at(a ^ k, half)
-                for m in range(Y):
-                    p = pieces[k * Y + m]
+                if near:
                     y_ref[rows_at((y ^ m) * 2 + c, fs), cols] = p[0:fs, :]
-                    y_ref[rows_at((y ^ m) * 2 + (1 - c), fs), cols] = p[fs + 8 : 2 * fs + 8, :]
-                logb_ref[0:1, cols] = pieces[k * Y][fs : fs + 1, :]
+                    if m == 0:
+                        logb_ref[0:1, cols] = p[fs : fs + 1, :]
+                if away:
+                    at = fs + 8 if near else 0
+                    y_ref[rows_at((y ^ m) * 2 + (1 - c), fs), cols] = p[at : at + fs, :]
             for j in range(N // 256):
                 cols = slice(j * 256, (j + 1) * 256)
                 v = y_ref[:, cols]
@@ -164,7 +193,7 @@
             sds(M, N), sds(M, F), sds(F, N, dtype=BF16), sds(F, N, dtype=BF16), sds(1, N), sds(3, M), sds(1, N), sds(2, M),
         )
         scratch = (pltpu.VMEM((F, M), F32), pltpu.VMEM((F, N), F32), pltpu.VMEM((M, F), BF16), pltpu.VMEM((M, F), BF16))
-        return call(body, outs, scratch, 20)(own, other, *pieces)
+        return call(body, outs, scratch, 20)(own, other, *(p[-1] for p in pieces))
 
     def fill_cols(self, col_ref, row):
         for r in range(self.nr):
@@ -195,9 +224,10 @@
     def cols(self):
         return pltpu.VMEM((self.M, LANES), F32)
 
-    def col1(self, s, stat, far, rowc):
-        def body(s_ref, stat, far, rowc, f_ref, out_ref, col_ref, m_ref, e_ref):
-            f = rowc[0:1, :] * LOG2E - lse2(stat, far)
+    def col1(self, s, rowc, stats):
+        def body(s_ref, rowc, *refs):
+            stats, (f_ref, out_ref, col_ref, m_ref, e_ref) = refs[:-5], refs[-5:]
+            f = rowc[0:1, :] * LOG2E - lse2(stats)
             f_ref[...] = f
             self.fill_cols(col_ref, f)
             self.start(m_ref, e_ref)
@@ -211,11 +241,12 @@
 
             self.finish(m_ref, e_ref, out_ref)
 
-        return call(body, (sds(1, self.M), sds(2, self.N)), (self.cols(), *self.stats()), 10)(s, stat, far, rowc)
-
-    def row2(self, s, f, stat, far, logb):
-        def body(s_ref, f, stat, far, logb, g_ref, out_ref, col_ref):
-            g_ref[...] = logb[...] * LOG2E - lse2(stat, far)
+        return call(body, (sds(1, self.M), sds(2, self.N)), (self.cols(), *self.stats()), 10)(s, rowc, *stats)
+
+    def row2(self, s, f, logb, stats):
+        def body(s_ref, f, logb, *refs):
+            stats, (g_ref, out_ref, col_ref) = refs[:-3], refs[-3:]
+            g_ref[...] = logb[...] * LOG2E - lse2(stats)
             self.fill_cols(col_ref, f)
             for r in range(self.nr):
                 rows = slice(r * LANES, (r + 1) * LANES)
@@ -226,11 +257,12 @@
                     acc = acc + jnp.exp2(s_ref[rows, lane] + fc + g_ref[:, lane])
                 out_ref[0:1, rows] = jnp.sum(acc.T, 0, keepdims=True)
 
-        return call(body, (sds(1, self.N), sds(1, self.M)), (self.cols(),), 10)(s, f, stat, far, logb)
-
-    def col2(self, s, f, g, total, far, rowc):
-        def body(s_ref, f, g, total, far, rowc, f_ref, out_ref, col_ref, acc_ref):
-            f2 = f[...] + rowc[0:1, :] * LOG2E - log2(total[...] + far[...])
+        return call(body, (sds(1, self.N), sds(1, self.M)), (self.cols(),), 10)(s, f, logb, *stats)
+
+    def col2(self, s, f, g, rowc, sums):
+        def body(s_ref, f, g, rowc, *refs):
+            sums, (f_ref, out_ref, col_ref, acc_ref) = refs[:-4], refs[-4:]
+            f2 = f[...] + rowc[0:1, :] * LOG2E - log2(total(sums))
             f_ref[...] = f2
             self.fill_cols(col_ref, f2)
             acc_ref[...] = jnp.zeros((8, self.N), F32)
@@ -247,16 +279,17 @@
             out_ref[...] = jnp.sum(acc_ref[...], 0, keepdims=True)
 
         scratch = (self.cols(), self.stats()[0])
-        return call(body, (sds(1, self.M), sds(1, self.N)), scratch, 10)(s, f, g, total, far, rowc)
-
-    def plan(self, s, f, g, total, far, logb, yh, yl, mine, q, base):
+        return call(body, (sds(1, self.M), sds(1, self.N)), scratch, 10)(s, f, g, rowc, *sums)
+
+    def plan(self, s, f, g, sums, logb, yh, yl, mine, q, base):
         N, F, qr, mw = self.N, self.F, self.qr, self.mw
 
-        def body(s_ref, f, g, total, far, logb, yh, yl, *rest):
-            extra, (w_ref, g_ref, ph_ref, pl_ref) = rest[:-4], rest[-4:]
+        def body(s_ref, f, g, logb, yh, yl, *rest):
+            few = len(sums)
+            parts, extra, (w_ref, g_ref, ph_ref, pl_ref) = rest[:few], rest[few:-4], rest[-4:]
             _, c, _, _ = position()
             at = (c if mine else 1 - c) * self.pb + q * qr
-            g_ref[...] = g[...] + logb[...] * LOG2E - log2(total[...] + far[...])
+            g_ref[...] = g[...] + logb[...] * LOG2E - log2(total(parts))
             for r in range(qr // LANES):
                 fc = to_col(f[0:1, pl.ds(pl.multiple_of(at + r * LANES, LANES), LANES)])
                 rows = pl.ds(pl.multiple_of(at + r * LANES, LANES), LANES)
@@ -276,7 +309,7 @@
             w_ref[0:qr, :] = w + extra[0][0:qr, :] if extra else w
 
         scratch = (pltpu.VMEM((1, N), F32), pltpu.VMEM((qr, N), BF16), pltpu.VMEM((qr, N), BF16))
-        args = (s, f, g, total, far, logb, yh, yl) + (() if base is None else (base,))
+        args = (s, f, g, logb, yh, yl, *sums) + (() if base is None else (base,))
         return call(body, sds(qr + 8, F), scratch, 14)(*args)
 
     def last(self, own, other, xt, f, rowc, yh, yl, hy, q):
@@ -322,46 +355,53 @@
         out = call(entry, outs, (*self.stats(), pltpu.VMEM((F, qr), F32)), 14)(own, other, xt, f, rowc, yh, yl, hy)
         return out[:A], out[A]
 
-    def pack(self, parcels, stat, far):
-        A, Q, ft, qr, pb, half, hw = self.A, self.Q, self.ft, self.qr, self.pb, self.half, self.hw
+    def pack(self, parcels, stats):
+        A, ft, qr, half, hw, tail = self.A, self.ft, self.qr, self.half, self.hw, self.tail
 
         def body(*refs):
-            parts, (p, q), outs, st = refs[: A * Q], refs[A * Q : A * Q + 2], refs[A * Q + 2 : -1], refs[-1]
+            parts, stats, outs, st = refs[:A], refs[A : -1 - A], refs[-1 - A : -1], refs[-1]
             _, _, a, _ = position()
-            st[0:1, :], st[1:2, :] = joined(p, q)
+            st[0:1, :], st[1:2, :] = joined(stats)
             for k in range(A):
-                for i in range(Q):
-                    outs[k][:, i * qr : (i + 1) * qr] = parts[i * A + k][...]
+                outs[k][0 : ft + 8, :] = parts[k][...]
                 for i in range(half // hw):
                     at = pl.ds(pl.multiple_of((a ^ k) * half + i * hw, LANES), hw)
                     outs[k][ft + 1 + 2 * i : ft + 3 + 2 * i, 0:hw] = st[0:2, at]
 
-        outs = tuple(sds(ft + 8, pb) for _ in range(A))
-        flat = [p for part in parcels for p in part]
-        return call(body, outs, (pltpu.VMEM((2, self.N), F32),), 8)(*flat, stat, far)
+        outs = tuple(sds(ft + tail, qr) for _ in range(A))
+        return call(body, outs, (pltpu.VMEM((2, self.N), F32),), 8)(*parcels, *stats)
 
     def unpack(self, got, kept):
-        A, fs, ft, pb, half, hw = self.A, self.fs, self.ft, self.pb, self.half, self.hw
+        A, Q, fs, ft, pb, qr, half, hw = self.A, self.Q, self.fs, self.ft, self.pb, self.qr, self.half, self.hw
 
         def body(*refs):
-            got, kept, moved, row_pot, pot = refs[:A], refs[A], refs[A + 1], refs[A + 2], refs[A + 3]
+            got, kept, moved, row_pot, pot = refs[: A * Q], refs[A * Q], refs[-3], refs[-2], refs[-1]
             _, _, a, _ = position()
-            for k in range(A):
-                cols = lanes_at(a ^ k, pb)
-                moved[:, cols] = got[k][0:ft, :]
-                row_pot[0:1, cols] = got[k][ft : ft + 1, :]
+            for q in range(Q):
+                for k in range(A):
+                    cols = pl.ds(pl.multiple_of((a ^ k) * pb + q * qr, LANES), qr)
+                    moved[:, cols] = got[q * A + k][0:ft, :]
+                    row_pot[0:1, cols] = got[q * A + k][ft : ft + 1, :]
             for i in range(half // hw):
-                tops = [got[k][ft + 1 + 2 * i : ft + 2 + 2 * i, 0:hw] for k in range(A)]
-                top = tops[0]
-                for v in tops[1:]:
-                    top = jnp.maximum(top, v)
-                total = jnp.zeros_like(top)
-                for k in range(A):
-                    total = total + got[k][ft + 2 + 2 * i : ft + 3 + 2 * i, 0:hw] * jnp.exp2(tops[k] - top)
+                at = slice(ft + 1 + 2 * i, ft + 3 + 2 * i)
+                v = lse2([got[(Q - 1) * A + k][at, 0:hw] for k in range(A)])
                 lanes = slice(i * hw, (i + 1) * hw)
-                pot[0:1, lanes] = EPS * (kept[fs : fs + 1, lanes] - LN2 * (top + log2(total)))
+                pot[0:1, lanes] = EPS * (kept[fs : fs + 1, lanes] - LN2 * v)
 
         return call(body, (sds(ft, A * pb), sds(1, A * pb), sds(1, half)), (), 8)(*got, kept)
+
+    def stack(self, parts):
+        def body(*refs):
+            for k, ref in enumerate(refs[:-1]):
+                refs[-1][k * self.ft : (k + 1) * self.ft, :] = ref[...]
+
+        return call(body, sds(len(parts) * self.ft, self.pb), (), 8)(*parts)
+
+    def both(self, w, far):
+        def body(p, q, out):
+            out[...] = p[...] + q[...]
+
+        return call(body, sds(self.qr + 8, self.F), (), 8)(w, far)
 
     def pair(self, pot, far):
         def body(p, q, out):
@@ -392,22 +432,27 @@
         return swap(v, "tgt", T, 2 * k)
 
     def join(p, q):
-        return jnp.concatenate(joined(p, q))
+        return jnp.concatenate(joined([p, q]))
 
     def add(p, q):
         return p + q
 
-    def last_two(v, op, sends):
-        for send in sends[:-1]:
-            v = op(v, send(v))
-        return v, sends[-1](v)
-
     def bits(size):
         return [1 << i for i in range(size.bit_length() - 1)]
 
-    over_rows = [over_c, over_b]
-    along_y = [lambda v, k=k: over_y(v, k) for k in bits(Y)]
-    over_cols = along_y + [lambda v, k=k: over_a(v, k) for k in bits(A)]
+    def along_y(v, op):
+        for k in bits(Y)[:-1]:
+            v = op(v, over_y(v, k))
+        return [v, over_y(v, bits(Y)[-1])] if Y > 1 else [v]
+
+    def over_rows(v, op):
+        v = op(v, over_c(v))
+        return [v, over_b(v)]
+
+    def over_cols(v, op):
+        v = along_y(v, op)
+        v = op(*v) if Y > 1 else v[0]
+        return [v] + [over_a(v, k) for k in range(A - 1, 0, -1)]
 
     def per_device(sources, targets, source_logw, target_logw, times):
         ft, ns = sources.shape
@@ -417,44 +462,53 @@
         kern = Kernels(ft * T, fs, ft, A, Y, half, pb, Q)
 
         sent, kept, blocks, side = kern.prep(sources, targets, source_logw, target_logw, times)
-        own = jnp.concatenate([kept, over_c(sent)])
-        chunks = {0: own}
+        away = over_c(sent)
+        whole = [(True, True, jnp.concatenate([kept, away]))]
+        halves = [(True, False, kept), (False, True, away)]
+
+        chunks = {0: whole}
         for bit in reversed(bits(A)):
             for k in list(chunks):
-                chunks[k ^ bit] = over_a(chunks[k], bit)
+                chunks[k ^ bit] = []
+                for near, far, v in halves if k == 0 and bit == A // 2 else chunks[k]:
+                    chunks[k ^ bit].append((near, far, over_a(v, bit)))
         pieces = []
         for k in range(A):
-            pieces.append(chunks[k])
-            for m in range(1, Y):
-                pieces.append(over_y(chunks[k], m))
+            for near, far, v in chunks[k]:
+                pieces.append((k, 0, near, far, v))
+                for m in range(1, Y):
+                    pieces.append((k, m, near, far, over_y(v, m)))
         parts = [blocks[0]]
         for k in range(1, A):
             parts.append(over_a(blocks[k], k))
-        xs = jnp.concatenate(parts)
+        xs = kern.stack(parts)
         xb = over_b(xs)
         x_own = jnp.concatenate([xs, xb, side])
         x_other = over_c(x_own)
 
         sc, xt, yh, yl, hy, rowc, logb, stat = kern.cross(x_own, x_other, pieces)
-        f1, stat = kern.col1(sc, *last_two(stat, join, over_rows), rowc)
-        g1, total = kern.row2(sc, f1, *last_two(stat, join, over_cols), logb)
-        f2, total = kern.col2(sc, f1, g1, *last_two(total, add, over_rows), rowc)
-        total = last_two(total, add, over_cols)
+        f1, stat = kern.col1(sc, rowc, over_rows(stat, join))
+        g1, sums = kern.row2(sc, f1, logb, over_cols(stat, join))
+        f2, sums = kern.col2(sc, f1, g1, rowc, over_rows(sums, add))
+        sums = over_cols(sums, add)
 
         def plan(mine, q, base):
-            return kern.plan(sc, f2, g1, *total, logb, yh, yl, mine, q, base)
+            return kern.plan(sc, f2, g1, sums, logb, yh, yl, mine, q, base)
 
         theirs = [over_c(plan(False, q, None)) for q in range(Q)]
-        parcels, stat = [], None
+        got, stat = [], None
         for q in range(Q):
             w = plan(True, q, theirs[q])
-            w = w + over_b(w)
-            part, fresh = kern.last(w, over_c(w), xt, f2, rowc, yh, yl, hy, q)
-            parcels.append(part)
+            far = over_b(w)
+            w = kern.both(w, far)
+            far = over_c(w)
+            parcels, fresh = kern.last(w, far, xt, f2, rowc, yh, yl, hy, q)
             stat = fresh if stat is None else join(stat, fresh)
-
-        packed = kern.pack(parcels, *last_two(stat, join, along_y))
-        got = [packed[0]] + [over_a(packed[k], k) for k in range(1, A)]
+            if q == Q - 1:
+                parcels = kern.pack(parcels, along_y(stat, join))
+            got.append(parcels[0])
+            for k in range(1, A):
+                got.append(over_a(parcels[k], k))
         moved, row_pot, pot = kern.unpack(got, kept)
         col_pot = kern.pair(pot, over_c(pot))
         return row_pot[0], moved, col_pot[0]

time: 144 us -> 143 us (level)
  starting transfers between devices: 35.6 us -> 47.9 us
  waiting for transfers between devices: 81.4 us -> 71.3 us
  local copies, waits for them, and re-layouts: 4.04 us -> 0.02 us
    ppermute x34 -> x43, starting transfers between devices: 35.6 us -> 47.9 us  [swap(): return lax.ppermute(v, axis, [(i, i ^ k) for i in range(size)])]
    ppermute x34 -> x43, waiting for transfers between devices: 81.4 us -> 71.3 us  [swap(): return lax.ppermute(v, axis, [(i, i ^ k) for i in range(size)])]
    unnamed x16 -> x1, local copies, waits for them, and re-layouts: 4.02 us -> 0.01 us
    pallas_call x3 -> x6, Pallas kernels: 4.62 us -> 5.87 us  [the longest x1 4.55 us: cross(): return call(body, outs, scratch, 20)(own, other, *(p[-1] for p in pieces))]
  transfers between devices with their start and end apart: 34 -> 43, of which waited for: 24 -> 26; matrix products, arithmetic and copies ran while one was open for 0% -> 0% of each run, Pallas kernels for 5% -> 6%
where the time goes in v2:
time: 143 us
  waiting for transfers between devices  71.3 us (50%)
  starting transfers between devices  47.9 us (33%)
  Pallas kernels  22.5 us (16%)
    ppermute x43, waiting for transfers between devices, swap(): return lax.ppermute(v, axis, [(i, i ^ k) for i in range(size)])  71.3 us
    ppermute x43, starting transfers between devices, swap(): return lax.ppermute(v, axis, [(i, i ^ k) for i in range(size)])  47.9 us
    pallas_call x4, Pallas kernels, plan(): return call(body, sds(qr + 8, F), scratch, 14)(*args)  5.76 us
    pallas_call x1, Pallas kernels, cross(): return call(body, outs, scratch, 20)(own, other, *(p[-1] for p in pieces))  4.55 us
    pallas_call x2, Pallas kernels, last(): call(entry, outs, (*self.stats(), pltpu.VMEM((F, qr), F32)), 14)  4.47 us
  transfers between devices with their start and end apart: 43, of which 26 were waited for; matrix products, arithmetic and copies ran while one was open for 0% of the time, Pallas kernels for 6%

profile of v2, /device:TPU:0, one launch (start us, length us, event | category | flops | bytes accessed | tf_op | source)
XLA Modules:
  0.0 142.7 jit_solution(1865054104132100538)
XLA Ops:
  1.8 3.1 %collective-permute-start = (f32[32,512]{1,0:T(8,128)S(1)}, f32[32,512]{1,0:T(8,128)S(1)}, u32[]{:S(2)}, u32[]{:S(2)}) collective-permute-start(f32[32,512]{1,0:T(8,128)S(1)} %get-tuple-element.42), channel_id=1, source_target_pairs={{0,2},{1,3},{2,0},{3,1},{4,6},{5,7},{6,4},{7,5},{8,10},{9,11},{10,... | collective-permute-start | bytes 196616 | tf_op jit(solution)/shard_map/ppermute | solution.py:420
  5.0 2.6 %collective-permute-start.1 = (f32[32,512]{1,0:T(8,128)S(1)}, f32[32,512]{1,0:T(8,128)S(1)}, u32[]{:S(2)}, u32[]{:S(2)}) collective-permute-start(f32[32,512]{1,0:T(8,128)S(1)} %get-tuple-element.43), channel_id=1, source_target_pairs={{0,4},{1,5},{2,6},{3,7},{4,0},{5,1},{6,2},{7,3},{8,12},{9,13},{10,... | collective-permute-start | bytes 196616 | tf_op jit(solution)/shard_map/ppermute | solution.py:420
  7.6 4.7 %collective-permute-done.1.refs_2_ = f32[32,512]{1,0:T(8,128)S(1)} collective-permute-done((f32[32,512]{1,0:T(8,128)S(1)}, f32[32,512]{1,0:T(8,128)S(1)}, u32[]{:S(2)}, u32[]{:S(2)}) %collective-permute-start.1) | collective-permute-done | bytes 65568 | tf_op jit(solution)/shard_map/ppermute | solution.py:420
  12.2 1.4 collective-permute-done.2.refs_3_
  13.6 1.6 %collective-permute-start.3 = (f32[128,512]{1,0:T(8,128)S(1)}, f32[128,512]{1,0:T(8,128)S(1)}, u32[]{:S(2)}, u32[]{:S(2)}) collective-permute-start(f32[128,512]{1,0:T(8,128)S(1)} %shard_map.77), channel_id=1, source_target_pairs={{0,1},{1,0},{2,3},{3,2},{4,5},{5,4},{6,7},{7,6},{8,9},{9,8},{10,11... | collective-permute-start | bytes 786440 | tf_op jit(solution)/shard_map/ppermute | solution.py:420
  15.2 1.6 %collective-permute-start.9 = (f32[72,512]{1,0:T(8,128)S(1)}, f32[72,512]{1,0:T(8,128)S(1)}, u32[]{:S(2)}, u32[]{:S(2)}) collective-permute-start(f32[72,512]{1,0:T(8,128)S(1)} %get-tuple-element.46.refs_8_), channel_id=1, source_target_pairs={{0,4},{1,5},{2,6},{3,7},{4,0},{5,1},{6,2},{7,3},{8,12},{9,13},{10,... | collective-permute-start | bytes 442376 | tf_op jit(solution)/shard_map/ppermute | solution.py:420
  17.7 2.5 %collective-permute-done.3 = f32[128,512]{1,0:T(8,128)S(1)} collective-permute-done((f32[128,512]{1,0:T(8,128)S(1)}, f32[128,512]{1,0:T(8,128)S(1)}, u32[]{:S(2)}, u32[]{:S(2)}) %collective-permute-start.3) | collective-permute-done | bytes 262176 | tf_op jit(solution)/shard_map/ppermute | solution.py:420
  20.3 4.7 %collective-permute-done.9.refs_4_ = f32[72,512]{1,0:T(8,128)S(1)} collective-permute-done((f32[72,512]{1,0:T(8,128)S(1)}, f32[72,512]{1,0:T(8,128)S(1)}, u32[]{:S(2)}, u32[]{:S(2)}) %collective-permute-start.9) | collective-permute-done | bytes 147488 | tf_op jit(solution)/shard_map/ppermute | solution.py:420
  24.9 3.0 %collective-permute-start.11 = (f32[64,512]{1,0:T(8,128)S(1)}, f32[64,512]{1,0:T(8,128)S(1)}, u32[]{:S(2)}, u32[]{:S(2)}) collective-permute-start(f32[64,512]{1,0:T(8,128)S(1)} %collective-permute-done.5), channel_id=1, source_target_pairs={{0,4},{1,5},{2,6},{3,7},{4,0},{5,1},{6,2},{7,3},{8,12},{9,13},{10,... | collective-permute-start | bytes 393224 | tf_op jit(solution)/shard_map/ppermute | solution.py:420
  28.0 1.5 %collective-permute-start.10 = (f32[72,512]{1,0:T(8,128)S(1)}, f32[72,512]{1,0:T(8,128)S(1)}, u32[]{:S(2)}, u32[]{:S(2)}) collective-permute-start(f32[72,512]{1,0:T(8,128)S(1)} %collective-permute-done.9.refs_4_), channel_id=1, source_target_pairs={{0,16},{8,24},{16,0},{24,8},{1,17},{9,25},{17,1},{25,9},{2,18},{10... | collective-permute-start | bytes 442376 | tf_op jit(solution)/shard_map/ppermute | solution.py:420
  29.5 4.7 %collective-permute-done.11.refs_6_ = f32[64,512]{1,0:T(8,128)S(1)} collective-permute-done((f32[64,512]{1,0:T(8,128)S(1)}, f32[64,512]{1,0:T(8,128)S(1)}, u32[]{:S(2)}, u32[]{:S(2)}) %collective-permute-start.11) | collective-permute-done | bytes 131104 | tf_op jit(solution)/shard_map/ppermute | solution.py:420
  34.8 1.5 %collective-permute-start.6 = (f32[136,512]{1,0:T(8,128)S(1)}, f32[136,512]{1,0:T(8,128)S(1)}, u32[]{:S(2)}, u32[]{:S(2)}) collective-permute-start(f32[136,512]{1,0:T(8,128)S(1)} %constant_dynamic-update-slice_fusion.refs_0_), channel_id=1, source_target_pairs={{0,16},{8,24},{16,0},{24,8},{1,17},{9,25},{17,1},{25,9},{2,18},{10... | collective-permute-start | bytes 835592 | tf_op jit(solution)/shard_map/ppermute | solution.py:420
  36.8 1.5 %collective-permute-start.12 = (f32[64,512]{1,0:T(8,128)S(1)}, f32[64,512]{1,0:T(8,128)S(1)}, u32[]{:S(2)}, u32[]{:S(2)}) collective-permute-start(f32[64,512]{1,0:T(8,128)S(1)} %collective-permute-done.11.refs_6_), channel_id=1, source_target_pairs={{0,16},{8,24},{16,0},{24,8},{1,17},{9,25},{17,1},{25,9},{2,18},{10... | collective-permute-start | bytes 393224 | tf_op jit(solution)/shard_map/ppermute | solution.py:420
  39.2 1.5 %collective-permute-start.14 = (f32[72,512]{1,0:T(8,128)S(1)}, f32[72,512]{1,0:T(8,128)S(1)}, u32[]{:S(2)}, u32[]{:S(2)}) collective-permute-start(f32[72,512]{1,0:T(8,128)S(1)} %collective-permute-done.13.refs_8_), channel_id=1, source_target_pairs={{0,16},{8,24},{16,0},{24,8},{1,17},{9,25},{17,1},{25,9},{2,18},{10... | collective-permute-start | bytes 442376 | tf_op jit(solution)/shard_map/ppermute | solution.py:420
  40.7 12.4 %collective-permute-done.12.refs_7_ = f32[64,512]{1,0:T(8,128)S(1)} collective-permute-done((f32[64,512]{1,0:T(8,128)S(1)}, f32[64,512]{1,0:T(8,128)S(1)}, u32[]{:S(2)}, u32[]{:S(2)}) %collective-permute-start.12) | collective-permute-done | bytes 131104 | tf_op jit(solution)/shard_map/ppermute | solution.py:420
  53.1 1.5 %collective-permute-start.16 = (f32[64,512]{1,0:T(8,128)S(1)}, f32[64,512]{1,0:T(8,128)S(1)}, u32[]{:S(2)}, u32[]{:S(2)}) collective-permute-start(f32[64,512]{1,0:T(8,128)S(1)} %collective-permute-done.15.refs_10_), channel_id=1, source_target_pairs={{0,16},{8,24},{16,0},{24,8},{1,17},{9,25},{17,1},{25,9},{2,18},{10... | collective-permute-start | bytes 393224 | tf_op jit(solution)/shard_map/ppermute | solution.py:420
  54.6 1.3 collective-permute-done.14.refs_9_
  55.9 2.1 %collective-permute-done.16.refs_11_ = f32[64,512]{1,0:T(8,128)S(1)} collective-permute-done((f32[64,512]{1,0:T(8,128)S(1)}, f32[64,512]{1,0:T(8,128)S(1)}, u32[]{:S(2)}, u32[]{:S(2)}) %collective-permute-start.16) | collective-permute-done | bytes 131104 | tf_op jit(solution)/shard_map/ppermute | solution.py:420
  58.0 4.6 %shard_map.78 = (f32[1024,2048]{1,0:T(8,128)S(1)}, f32[1024,256]{1,0:T(8,128)S(1)}, bf16[256,2048]{1,0:T(8,128)(2,1)S(1)}, bf16[256,2048]{1,0:T(8,128)(2,1)S(1)}...) custom-call(f32[264,512]{1,0:T(8,128)S(1)} %pad_maximum_fusion.own, ...), custom_call_target="tpu_custom_call" | custom-call | tf_op jit(solution)/shard_map/pallas_call | solution.py:196
  64.5 3.1 %collective-permute-done.18.refs_1_ = f32[2,1024]{1,0:T(2,128)S(1)} collective-permute-done((f32[2,1024]{1,0:T(2,128)S(1)}, f32[2,1024]{1,0:T(2,128)S(1)}, u32[]{:S(2)}, u32[]{:S(2)}) %collective-permute-start.18) | collective-permute-done | bytes 8224 | tf_op jit(solution)/shard_map/ppermute | solution.py:420
  67.6 2.0 %shard_map.79 = (f32[1,1024]{1,0:T(1,128)S(1)}, f32[2,2048]{1,0:T(2,128)S(1)}) custom-call(f32[1024,2048]{1,0:T(8,128)S(1)} %get-tuple-element.48.s_ref, f32[3,1024]{1,0:T(4,128)S(1)} %get-tuple-element.49.rowc.refs_4_, f32[2,1024]{1,0:T(2,128)S(1)} %pad_maximum_fusion.3.refs_0_, f32[2,1024]{1,0:T(2,128)S(1)} %collective-permute-done.18.refs_1_), custom_call_target="tpu_custom_call" | custom-call | tf_op jit(solution)/shard_map/pallas_call | solution.py:244
  69.6 1.6 %collective-permute-start.19 = (f32[2,2048]{1,0:T(2,128)S(1)}, f32[2,2048]{1,0:T(2,128)S(1)}, u32[]{:S(2)}, u32[]{:S(2)}) collective-permute-start(f32[2,2048]{1,0:T(2,128)S(1)} %get-tuple-element.53), channel_id=1, source_target_pairs={{0,16},{8,24},{16,0},{24,8},{1,17},{9,25},{17,1},{25,9},{2,18},{10... | collective-permute-start | bytes 49160 | tf_op jit(solution)/shard_map/ppermute | solution.py:420
  71.2 2.2 %collective-permute-done.19 = f32[2,2048]{1,0:T(2,128)S(1)} collective-permute-done((f32[2,2048]{1,0:T(2,128)S(1)}, f32[2,2048]{1,0:T(2,128)S(1)}, u32[]{:S(2)}, u32[]{:S(2)}) %collective-permute-start.19) | collective-permute-done | bytes 16416 | tf_op jit(solution)/shard_map/ppermute | solution.py:420
  73.5 1.3 collective-permute-start.22
  74.7 2.0 %collective-permute-start.21 = (f32[2,2048]{1,0:T(2,128)S(1)}, f32[2,2048]{1,0:T(2,128)S(1)}, u32[]{:S(2)}, u32[]{:S(2)}) collective-permute-start(f32[2,2048]{1,0:T(2,128)S(1)} %pad_maximum_fusion.1.refs_0_), channel_id=1, source_target_pairs={{0,4},{1,5},{2,6},{3,7},{4,0},{5,1},{6,2},{7,3},{8,12},{9,13},{10,... | collective-permute-start | bytes 49160 | tf_op jit(solution)/shard_map/ppermute | solution.py:420
  77.9 1.4 %collective-permute-done.21.refs_2_ = f32[2,2048]{1,0:T(2,128)S(1)} collective-permute-done((f32[2,2048]{1,0:T(2,128)S(1)}, f32[2,2048]{1,0:T(2,128)S(1)}, u32[]{:S(2)}, u32[]{:S(2)}) %collective-permute-start.21) | collective-permute-done | bytes 16416 | tf_op jit(solution)/shard_map/ppermute | solution.py:420
  79.4 2.9 %collective-permute-done.20.refs_1_ = f32[2,2048]{1,0:T(2,128)S(1)} collective-permute-done((f32[2,2048]{1,0:T(2,128)S(1)}, f32[2,2048]{1,0:T(2,128)S(1)}, u32[]{:S(2)}, u32[]{:S(2)}) %collective-permute-start.20) | collective-permute-done | bytes 16416 | tf_op jit(solution)/shard_map/ppermute | solution.py:420
  82.3 1.3 shard_map.80
  85.3 3.1 %collective-permute-done.24.refs_1_ = f32[1,1024]{1,0:T(1,128)S(1)} collective-permute-done((f32[1,1024]{1,0:T(1,128)S(1)}, f32[1,1024]{1,0:T(1,128)S(1)}, u32[]{:S(2)}, u32[]{:S(2)}) %collective-permute-start.24) | collective-permute-done | bytes 4128 | tf_op jit(solution)/shard_map/ppermute | solution.py:420
  88.4 1.8 %shard_map.81 = (f32[1,1024]{1,0:T(1,128)S(1)}, f32[1,2048]{1,0:T(1,128)S(1)}) custom-call(f32[1024,2048]{1,0:T(8,128)S(1)} %get-tuple-element.48.s_ref, f32[1,1024]{1,0:T(1,128)S(1)} %get-tuple-element.51.f, f32[1,2048]{1,0:T(1,128)S(1)} %get-tuple-element.54.g, f32[3,1024]{1,0:T(4,128)S(1)} %get-tuple-element.49.rowc.refs_4_, f32[1,1024]{1,0:T(1,128)S(1)} %add.17.refs_0_, ...), custom_call_target="tpu_custom_call" | custom-call | tf_op jit(solution)/shard_map/pallas_call | solution.py:282
  90.2 1.6 %collective-permute-start.25 = (f32[1,2048]{1,0:T(1,128)S(1)}, f32[1,2048]{1,0:T(1,128)S(1)}, u32[]{:S(2)}, u32[]{:S(2)}) collective-permute-start(f32[1,2048]{1,0:T(1,128)S(1)} %get-tuple-element.59), channel_id=1, source_target_pairs={{0,16},{8,24},{16,0},{24,8},{1,17},{9,25},{17,1},{25,9},{2,18},{10... | collective-permute-start | bytes 24584 | tf_op jit(solution)/shard_map/ppermute | solution.py:420
  91.8 2.1 %collective-permute-done.25 = f32[1,2048]{1,0:T(1,128)S(1)} collective-permute-done((f32[1,2048]{1,0:T(1,128)S(1)}, f32[1,2048]{1,0:T(1,128)S(1)}, u32[]{:S(2)}, u32[]{:S(2)}) %collective-permute-start.25) | collective-permute-done | bytes 8224 | tf_op jit(solution)/shard_map/ppermute | solution.py:420
  94.0 1.7 %collective-permute-start.27 = (f32[1,2048]{1,0:T(1,128)S(1)}, f32[1,2048]{1,0:T(1,128)S(1)}, u32[]{:S(2)}, u32[]{:S(2)}) collective-permute-start(f32[1,2048]{1,0:T(1,128)S(1)} %add.18.rest_0_), channel_id=1, source_target_pairs={{0,4},{1,5},{2,6},{3,7},{4,0},{5,1},{6,2},{7,3},{8,12},{9,13},{10,... | collective-permute-start | bytes 24584 | tf_op jit(solution)/shard_map/ppermute | solution.py:420
  95.7 2.6 %collective-permute-start.26 = (f32[1,2048]{1,0:T(1,128)S(1)}, f32[1,2048]{1,0:T(1,128)S(1)}, u32[]{:S(2)}, u32[]{:S(2)}) collective-permute-start(f32[1,2048]{1,0:T(1,128)S(1)} %add.18.rest_0_), channel_id=1, source_target_pairs={{0,6},{1,7},{2,4},{3,5},{4,2},{5,3},{6,0},{7,1},{8,14},{9,15},{10,... | collective-permute-start | bytes 24584 | tf_op jit(solution)/shard_map/ppermute | solution.py:420
  98.6 2.6 %collective-permute-done.26.rest_1_ = f32[1,2048]{1,0:T(1,128)S(1)} collective-permute-done((f32[1,2048]{1,0:T(1,128)S(1)}, f32[1,2048]{1,0:T(1,128)S(1)}, u32[]{:S(2)}, u32[]{:S(2)}) %collective-permute-start.26) | collective-permute-done | bytes 8224 | tf_op jit(solution)/shard_map/ppermute | solution.py:420
  101.2 1.4 %shard_map.82 = f32[264,256]{1,0:T(8,128)S(1)} custom-call(f32[1024,2048]{1,0:T(8,128)S(1)} %get-tuple-element.48.s_ref, f32[1,1024]{1,0:T(1,128)S(1)} %get-tuple-element.56.f.refs_3_, f32[1,2048]{1,0:T(1,128)S(1)} %get-tuple-element.54.g, f32[1,2048]{1,0:T(1,128)S(1)} %get-tuple-element.52.logb, bf16[256,2048]{1,0:T(8,128)(2,1)S(1)} %get-tuple-element.57.yh.refs_5_, ...), custom_call_target="tpu_custom_call" | custom-call | tf_op jit(solution)/shard_map/pallas_call | solution.py:313
  102.7 1.4 %shard_map.86 = f32[264,256]{1,0:T(8,128)S(1)} custom-call(f32[1024,2048]{1,0:T(8,128)S(1)} %get-tuple-element.48.s_ref, f32[1,1024]{1,0:T(1,128)S(1)} %get-tuple-element.56.f.refs_3_, f32[1,2048]{1,0:T(1,128)S(1)} %get-tuple-element.54.g, f32[1,2048]{1,0:T(1,128)S(1)} %get-tuple-element.52.logb, bf16[256,2048]{1,0:T(8,128)(2,1)S(1)} %get-tuple-element.57.yh.refs_5_, ...), custom_call_target="tpu_custom_call" | custom-call | tf_op jit(solution)/shard_map/pallas_call | solution.py:313
  104.7 1.4 %shard_map.83.p = f32[264,256]{1,0:T(8,128)S(1)} custom-call(f32[1024,2048]{1,0:T(8,128)S(1)} %get-tuple-element.48.s_ref, f32[1,1024]{1,0:T(1,128)S(1)} %get-tuple-element.56.f.refs_3_, f32[1,2048]{1,0:T(1,128)S(1)} %get-tuple-element.54.g, f32[1,2048]{1,0:T(1,128)S(1)} %get-tuple-element.52.logb, bf16[256,2048]{1,0:T(8,128)(2,1)S(1)} %get-tuple-element.57.yh.refs_5_, ...), custom_call_target="tpu_custom_call" | custom-call | tf_op jit(solution)/shard_map/pallas_call | solution.py:313
  106.8 1.4 %shard_map.87.p = f32[264,256]{1,0:T(8,128)S(1)} custom-call(f32[1024,2048]{1,0:T(8,128)S(1)} %get-tuple-element.48.s_ref, f32[1,1024]{1,0:T(1,128)S(1)} %get-tuple-element.56.f.refs_3_, f32[1,2048]{1,0:T(1,128)S(1)} %get-tuple-element.54.g, f32[1,2048]{1,0:T(1,128)S(1)} %get-tuple-element.52.logb, bf16[256,2048]{1,0:T(8,128)(2,1)S(1)} %get-tuple-element.57.yh.refs_5_, ...), custom_call_target="tpu_custom_call" | custom-call | tf_op jit(solution)/shard_map/pallas_call | solution.py:313
  108.2 1.6 %collective-permute-start.36 = (f32[264,256]{1,0:T(8,128)S(1)}, f32[264,256]{1,0:T(8,128)S(1)}, u32[]{:S(2)}, u32[]{:S(2)}) collective-permute-start(f32[264,256]{1,0:T(8,128)S(1)} %shard_map.87.p), channel_id=1, source_target_pairs={{0,1},{1,0},{2,3},{3,2},{4,5},{5,4},{6,7},{7,6},{8,9},{9,8},{10,11... | collective-permute-start | bytes 811016 | tf_op jit(solution)/shard_map/ppermute | solution.py:420
  109.8 5.8 %collective-permute-done.30.q = f32[264,256]{1,0:T(8,128)S(1)} collective-permute-done((f32[264,256]{1,0:T(8,128)S(1)}, f32[264,256]{1,0:T(8,128)S(1)}, u32[]{:S(2)}, u32[]{:S(2)}) %collective-permute-start.30) | collective-permute-done | bytes 270368 | tf_op jit(solution)/shard_map/ppermute | solution.py:420
  115.7 4.7 %collective-permute-done.36.q = f32[264,256]{1,0:T(8,128)S(1)} collective-permute-done((f32[264,256]{1,0:T(8,128)S(1)}, f32[264,256]{1,0:T(8,128)S(1)}, u32[]{:S(2)}, u32[]{:S(2)}) %collective-permute-start.36) | collective-permute-done | bytes 270368 | tf_op jit(solution)/shard_map/ppermute | solution.py:420
  120.6 2.2 %shard_map.85 = (f32[40,256]{1,0:T(8,128)S(1)}, f32[40,256]{1,0:T(8,128)S(1)}, f32[40,256]{1,0:T(8,128)S(1)}, f32[40,256]{1,0:T(8,128)S(1)}, f32[2,2048]{1,0:T(2,128)S(1)}) custom-call(f32[264,256]{1,0:T(8,128)S(1)} %shard_map.84.refs_0_, f32[264,256]{1,0:T(8,128)S(1)} %collective-permute-done.31.refs_1_, f32[1024,256]{1,0:T(8,128)S(1)} %get-tuple-element.60.refs_2_, ...), custom_call_target="tpu_custom_call" | custom-call | tf_op jit(solution)/shard_map/pallas_call | solution.py:355
  122.9 2.2 %shard_map.89 = (f32[40,256]{1,0:T(8,128)S(1)}, f32[40,256]{1,0:T(8,128)S(1)}, f32[40,256]{1,0:T(8,128)S(1)}, f32[40,256]{1,0:T(8,128)S(1)}, f32[2,2048]{1,0:T(2,128)S(1)}) custom-call(f32[264,256]{1,0:T(8,128)S(1)} %shard_map.88.refs_0_, f32[264,256]{1,0:T(8,128)S(1)} %collective-permute-done.37.refs_1_, f32[1024,256]{1,0:T(8,128)S(1)} %get-tuple-element.60.refs_2_, ...), custom_call_target="tpu_custom_call" | custom-call | tf_op jit(solution)/shard_map/pallas_call | solution.py:355
  125.2 1.6 %collective-permute-start.38 = (f32[2,2048]{1,0:T(2,128)S(1)}, f32[2,2048]{1,0:T(2,128)S(1)}, u32[]{:S(2)}, u32[]{:S(2)}) collective-permute-start(f32[2,2048]{1,0:T(2,128)S(1)} %pad_maximum_fusion.2.refs_4_), channel_id=1, source_target_pairs={{0,16},{8,24},{16,0},{24,8},{1,17},{9,25},{17,1},{25,9},{2,18},{10... | collective-permute-start | bytes 49160 | tf_op jit(solution)/shard_map/ppermute | solution.py:420
  126.8 3.2 %collective-permute-start.33 = (f32[40,256]{1,0:T(8,128)S(1)}, f32[40,256]{1,0:T(8,128)S(1)}, u32[]{:S(2)}, u32[]{:S(2)}) collective-permute-start(f32[40,256]{1,0:T(8,128)S(1)} %get-tuple-element.64), channel_id=1, source_target_pairs={{0,4},{1,5},{2,6},{3,7},{4,0},{5,1},{6,2},{7,3},{8,12},{9,13},{10,... | collective-permute-start | bytes 122888 | tf_op jit(solution)/shard_map/ppermute | solution.py:420
  131.3 3.2 %collective-permute-start.40 = (f32[40,256]{1,0:T(8,128)S(1)}, f32[40,256]{1,0:T(8,128)S(1)}, u32[]{:S(2)}, u32[]{:S(2)}) collective-permute-start(f32[40,256]{1,0:T(8,128)S(1)} %get-tuple-element.74), channel_id=1, source_target_pairs={{0,4},{1,5},{2,6},{3,7},{4,0},{5,1},{6,2},{7,3},{8,12},{9,13},{10,... | collective-permute-start | bytes 122888 | tf_op jit(solution)/shard_map/ppermute | solution.py:420
  137.0 3.2 %collective-permute-done.41.refs_7_ = f32[40,256]{1,0:T(8,128)S(1)} collective-permute-done((f32[40,256]{1,0:T(8,128)S(1)}, f32[40,256]{1,0:T(8,128)S(1)}, u32[]{:S(2)}, u32[]{:S(2)}) %collective-permute-start.41) | collective-permute-done | bytes 40992 | tf_op jit(solution)/shard_map/ppermute | solution.py:420
  (66 shorter events, 17.3 us)
Async XLA Ops:
  1.8 5.7 %collective-permute-start = (f32[32,512]{1,0:T(8,128)S(1)}, f32[32,512]{1,0:T(8,128)S(1)}, u32[]{:S(2)}, u32[]{:S(2)}) collective-permute-start(f32[32,512]{1,0:T(8,128)S(1)} %get-tuple-element.42), channel_id=1, source_target_pairs={{0,2},{1,3},{2,0},{3,1},{4,6},{5,7},{6,4},{7,5},{8,10},{9,11},{10,... | collective-permute-start | bytes 196616 | tf_op jit(solution)/shard_map/ppermute | solution.py:420
  5.0 7.3 %collective-permute-start.1 = (f32[32,512]{1,0:T(8,128)S(1)}, f32[32,512]{1,0:T(8,128)S(1)}, u32[]{:S(2)}, u32[]{:S(2)}) collective-permute-start(f32[32,512]{1,0:T(8,128)S(1)} %get-tuple-element.43), channel_id=1, source_target_pairs={{0,4},{1,5},{2,6},{3,7},{4,0},{5,1},{6,2},{7,3},{8,12},{9,13},{10,... | collective-permute-start | bytes 196616 | tf_op jit(solution)/shard_map/ppermute | solution.py:420
  7.6 6.1 %collective-permute-start.2 = (f32[32,512]{1,0:T(8,128)S(1)}, f32[32,512]{1,0:T(8,128)S(1)}, u32[]{:S(2)}, u32[]{:S(2)}) collective-permute-start(f32[32,512]{1,0:T(8,128)S(1)} %get-tuple-element.44), channel_id=1, source_target_pairs={{0,6},{1,7},{2,4},{3,5},{4,2},{5,3},{6,0},{7,1},{8,14},{9,15},{10,... | collective-permute-start | bytes 196616 | tf_op jit(solution)/shard_map/ppermute | solution.py:420
  13.6 6.5 %collective-permute-start.3 = (f32[128,512]{1,0:T(8,128)S(1)}, f32[128,512]{1,0:T(8,128)S(1)}, u32[]{:S(2)}, u32[]{:S(2)}) collective-permute-start(f32[128,512]{1,0:T(8,128)S(1)} %shard_map.77), channel_id=1, source_target_pairs={{0,1},{1,0},{2,3},{3,2},{4,5},{5,4},{6,7},{7,6},{8,9},{9,8},{10,11... | collective-permute-start | bytes 786440 | tf_op jit(solution)/shard_map/ppermute | solution.py:420
  15.2 1.6 %collective-permute-start.5 = (f32[64,512]{1,0:T(8,128)S(1)}, f32[64,512]{1,0:T(8,128)S(1)}, u32[]{:S(2)}, u32[]{:S(2)}) collective-permute-start(f32[64,512]{1,0:T(8,128)S(1)} %get-tuple-element.47), channel_id=1, source_target_pairs={{0,8},{8,0},{16,24},{24,16},{1,9},{9,1},{17,25},{25,17},{2,10},{10... | collective-permute-start | bytes 393224 | tf_op jit(solution)/shard_map/ppermute | solution.py:420
  15.2 9.7 %collective-permute-start.9 = (f32[72,512]{1,0:T(8,128)S(1)}, f32[72,512]{1,0:T(8,128)S(1)}, u32[]{:S(2)}, u32[]{:S(2)}) collective-permute-start(f32[72,512]{1,0:T(8,128)S(1)} %get-tuple-element.46.refs_8_), channel_id=1, source_target_pairs={{0,4},{1,5},{2,6},{3,7},{4,0},{5,1},{6,2},{7,3},{8,12},{9,13},{10,... | collective-permute-start | bytes 442376 | tf_op jit(solution)/shard_map/ppermute | solution.py:420
  16.8 19.5 %collective-permute-start.7 = (f32[136,512]{1,0:T(8,128)S(1)}, f32[136,512]{1,0:T(8,128)S(1)}, u32[]{:S(2)}, u32[]{:S(2)}) collective-permute-start(f32[136,512]{1,0:T(8,128)S(1)} %constant_dynamic-update-slice_fusion.refs_0_), channel_id=1, source_target_pairs={{0,2},{1,3},{2,0},{3,1},{4,6},{5,7},{6,4},{7,5},{8,10},{9,11},{10,... | collective-permute-start | bytes 835592 | tf_op jit(solution)/shard_map/ppermute | solution.py:420
  20.2 37.9 %collective-permute-start.4 = (f32[264,512]{1,0:T(8,128)S(1)}, f32[264,512]{1,0:T(8,128)S(1)}, u32[]{:S(2)}, u32[]{:S(2)}) collective-permute-start(f32[264,512]{1,0:T(8,128)S(1)} %pad_maximum_fusion.own), channel_id=1, source_target_pairs={{0,8},{8,0},{16,24},{24,16},{1,9},{9,1},{17,25},{25,17},{2,10},{10... | collective-permute-start | bytes 1622024 | tf_op jit(solution)/shard_map/ppermute | solution.py:420
  24.9 9.8 %collective-permute-start.13 = (f32[72,512]{1,0:T(8,128)S(1)}, f32[72,512]{1,0:T(8,128)S(1)}, u32[]{:S(2)}, u32[]{:S(2)}) collective-permute-start(f32[72,512]{1,0:T(8,128)S(1)} %collective-permute-done.9.refs_4_), channel_id=1, source_target_pairs={{0,2},{1,3},{2,0},{3,1},{4,6},{5,7},{6,4},{7,5},{8,10},{9,11},{10,... | collective-permute-start | bytes 442376 | tf_op jit(solution)/shard_map/ppermute | solution.py:420
  24.9 9.3 %collective-permute-start.11 = (f32[64,512]{1,0:T(8,128)S(1)}, f32[64,512]{1,0:T(8,128)S(1)}, u32[]{:S(2)}, u32[]{:S(2)}) collective-permute-start(f32[64,512]{1,0:T(8,128)S(1)} %collective-permute-done.5), channel_id=1, source_target_pairs={{0,4},{1,5},{2,6},{3,7},{4,0},{5,1},{6,2},{7,3},{8,12},{9,13},{10,... | collective-permute-start | bytes 393224 | tf_op jit(solution)/shard_map/ppermute | solution.py:420
  28.0 8.8 %collective-permute-start.10 = (f32[72,512]{1,0:T(8,128)S(1)}, f32[72,512]{1,0:T(8,128)S(1)}, u32[]{:S(2)}, u32[]{:S(2)}) collective-permute-start(f32[72,512]{1,0:T(8,128)S(1)} %collective-permute-done.9.refs_4_), channel_id=1, source_target_pairs={{0,16},{8,24},{16,0},{24,8},{1,17},{9,25},{17,1},{25,9},{2,18},{10... | collective-permute-start | bytes 442376 | tf_op jit(solution)/shard_map/ppermute | solution.py:420
  34.2 5.0 %collective-permute-start.15 = (f32[64,512]{1,0:T(8,128)S(1)}, f32[64,512]{1,0:T(8,128)S(1)}, u32[]{:S(2)}, u32[]{:S(2)}) collective-permute-start(f32[64,512]{1,0:T(8,128)S(1)} %collective-permute-done.11.refs_6_), channel_id=1, source_target_pairs={{0,2},{1,3},{2,0},{3,1},{4,6},{5,7},{6,4},{7,5},{8,10},{9,11},{10,... | collective-permute-start | bytes 393224 | tf_op jit(solution)/shard_map/ppermute | solution.py:420
  34.8 19.8 %collective-permute-start.6 = (f32[136,512]{1,0:T(8,128)S(1)}, f32[136,512]{1,0:T(8,128)S(1)}, u32[]{:S(2)}, u32[]{:S(2)}) collective-permute-start(f32[136,512]{1,0:T(8,128)S(1)} %constant_dynamic-update-slice_fusion.refs_0_), channel_id=1, source_target_pairs={{0,16},{8,24},{16,0},{24,8},{1,17},{9,25},{17,1},{25,9},{2,18},{10... | collective-permute-start | bytes 835592 | tf_op jit(solution)/shard_map/ppermute | solution.py:420
  36.3 21.8 %collective-permute-start.8 = (f32[136,512]{1,0:T(8,128)S(1)}, f32[136,512]{1,0:T(8,128)S(1)}, u32[]{:S(2)}, u32[]{:S(2)}) collective-permute-start(f32[136,512]{1,0:T(8,128)S(1)} %collective-permute-done.7.refs_2_), channel_id=1, source_target_pairs={{0,16},{8,24},{16,0},{24,8},{1,17},{9,25},{17,1},{25,9},{2,18},{10... | collective-permute-start | bytes 835592 | tf_op jit(solution)/shard_map/ppermute | solution.py:420
  36.8 16.3 %collective-permute-start.12 = (f32[64,512]{1,0:T(8,128)S(1)}, f32[64,512]{1,0:T(8,128)S(1)}, u32[]{:S(2)}, u32[]{:S(2)}) collective-permute-start(f32[64,512]{1,0:T(8,128)S(1)} %collective-permute-done.11.refs_6_), channel_id=1, source_target_pairs={{0,16},{8,24},{16,0},{24,8},{1,17},{9,25},{17,1},{25,9},{2,18},{10... | collective-permute-start | bytes 393224 | tf_op jit(solution)/shard_map/ppermute | solution.py:420
  39.2 16.7 %collective-permute-start.14 = (f32[72,512]{1,0:T(8,128)S(1)}, f32[72,512]{1,0:T(8,128)S(1)}, u32[]{:S(2)}, u32[]{:S(2)}) collective-permute-start(f32[72,512]{1,0:T(8,128)S(1)} %collective-permute-done.13.refs_8_), channel_id=1, source_target_pairs={{0,16},{8,24},{16,0},{24,8},{1,17},{9,25},{17,1},{25,9},{2,18},{10... | collective-permute-start | bytes 442376 | tf_op jit(solution)/shard_map/ppermute | solution.py:420
  53.1 5.0 %collective-permute-start.16 = (f32[64,512]{1,0:T(8,128)S(1)}, f32[64,512]{1,0:T(8,128)S(1)}, u32[]{:S(2)}, u32[]{:S(2)}) collective-permute-start(f32[64,512]{1,0:T(8,128)S(1)} %collective-permute-done.15.refs_10_), channel_id=1, source_target_pairs={{0,16},{8,24},{16,0},{24,8},{1,17},{9,25},{17,1},{25,9},{2,18},{10... | collective-permute-start | bytes 393224 | tf_op jit(solution)/shard_map/ppermute | solution.py:420
  62.6 1.2 collective-permute-start.17
  63.9 3.7 %collective-permute-start.18 = (f32[2,1024]{1,0:T(2,128)S(1)}, f32[2,1024]{1,0:T(2,128)S(1)}, u32[]{:S(2)}, u32[]{:S(2)}) collective-permute-start(f32[2,1024]{1,0:T(2,128)S(1)} %pad_maximum_fusion.3.refs_0_), channel_id=1, source_target_pairs={{0,1},{1,0},{2,3},{3,2},{4,5},{5,4},{6,7},{7,6},{8,9},{9,8},{10,11... | collective-permute-start | bytes 24584 | tf_op jit(solution)/shard_map/ppermute | solution.py:420
  69.6 3.8 %collective-permute-start.19 = (f32[2,2048]{1,0:T(2,128)S(1)}, f32[2,2048]{1,0:T(2,128)S(1)}, u32[]{:S(2)}, u32[]{:S(2)}) collective-permute-start(f32[2,2048]{1,0:T(2,128)S(1)} %get-tuple-element.53), channel_id=1, source_target_pairs={{0,16},{8,24},{16,0},{24,8},{1,17},{9,25},{17,1},{25,9},{2,18},{10... | collective-permute-start | bytes 49160 | tf_op jit(solution)/shard_map/ppermute | solution.py:420
  73.5 4.5 %collective-permute-start.22 = (f32[2,2048]{1,0:T(2,128)S(1)}, f32[2,2048]{1,0:T(2,128)S(1)}, u32[]{:S(2)}, u32[]{:S(2)}) collective-permute-start(f32[2,2048]{1,0:T(2,128)S(1)} %pad_maximum_fusion.1.refs_0_), channel_id=1, source_target_pairs={{0,2},{1,3},{2,0},{3,1},{4,6},{5,7},{6,4},{7,5},{8,10},{9,11},{10,... | collective-permute-start | bytes 49160 | tf_op jit(solution)/shard_map/ppermute | solution.py:420
  74.7 4.6 %collective-permute-start.21 = (f32[2,2048]{1,0:T(2,128)S(1)}, f32[2,2048]{1,0:T(2,128)S(1)}, u32[]{:S(2)}, u32[]{:S(2)}) collective-permute-start(f32[2,2048]{1,0:T(2,128)S(1)} %pad_maximum_fusion.1.refs_0_), channel_id=1, source_target_pairs={{0,4},{1,5},{2,6},{3,7},{4,0},{5,1},{6,2},{7,3},{8,12},{9,13},{10,... | collective-permute-start | bytes 49160 | tf_op jit(solution)/shard_map/ppermute | solution.py:420
  76.7 5.5 %collective-permute-start.20 = (f32[2,2048]{1,0:T(2,128)S(1)}, f32[2,2048]{1,0:T(2,128)S(1)}, u32[]{:S(2)}, u32[]{:S(2)}) collective-permute-start(f32[2,2048]{1,0:T(2,128)S(1)} %pad_maximum_fusion.1.refs_0_), channel_id=1, source_target_pairs={{0,6},{1,7},{2,4},{3,5},{4,2},{5,3},{6,0},{7,1},{8,14},{9,15},{10,... | collective-permute-start | bytes 49160 | tf_op jit(solution)/shard_map/ppermute | solution.py:420
  83.6 1.2 collective-permute-start.23
  84.8 3.6 %collective-permute-start.24 = (f32[1,1024]{1,0:T(1,128)S(1)}, f32[1,1024]{1,0:T(1,128)S(1)}, u32[]{:S(2)}, u32[]{:S(2)}) collective-permute-start(f32[1,1024]{1,0:T(1,128)S(1)} %add.17.refs_0_), channel_id=1, source_target_pairs={{0,1},{1,0},{2,3},{3,2},{4,5},{5,4},{6,7},{7,6},{8,9},{9,8},{10,11... | collective-permute-start | bytes 12296 | tf_op jit(solution)/shard_map/ppermute | solution.py:420
  90.2 3.7 %collective-permute-start.25 = (f32[1,2048]{1,0:T(1,128)S(1)}, f32[1,2048]{1,0:T(1,128)S(1)}, u32[]{:S(2)}, u32[]{:S(2)}) collective-permute-start(f32[1,2048]{1,0:T(1,128)S(1)} %get-tuple-element.59), channel_id=1, source_target_pairs={{0,16},{8,24},{16,0},{24,8},{1,17},{9,25},{17,1},{25,9},{2,18},{10... | collective-permute-start | bytes 24584 | tf_op jit(solution)/shard_map/ppermute | solution.py:420
  93.9 4.5 %collective-permute-start.28 = (f32[1,2048]{1,0:T(1,128)S(1)}, f32[1,2048]{1,0:T(1,128)S(1)}, u32[]{:S(2)}, u32[]{:S(2)}) collective-permute-start(f32[1,2048]{1,0:T(1,128)S(1)} %add.18.rest_0_), channel_id=1, source_target_pairs={{0,2},{1,3},{2,0},{3,1},{4,6},{5,7},{6,4},{7,5},{8,10},{9,11},{10,... | collective-permute-start | bytes 24584 | tf_op jit(solution)/shard_map/ppermute | solution.py:420
  94.0 4.6 %collective-permute-start.27 = (f32[1,2048]{1,0:T(1,128)S(1)}, f32[1,2048]{1,0:T(1,128)S(1)}, u32[]{:S(2)}, u32[]{:S(2)}) collective-permute-start(f32[1,2048]{1,0:T(1,128)S(1)} %add.18.rest_0_), channel_id=1, source_target_pairs={{0,4},{1,5},{2,6},{3,7},{4,0},{5,1},{6,2},{7,3},{8,12},{9,13},{10,... | collective-permute-start | bytes 24584 | tf_op jit(solution)/shard_map/ppermute | solution.py:420
  95.7 5.4 %collective-permute-start.26 = (f32[1,2048]{1,0:T(1,128)S(1)}, f32[1,2048]{1,0:T(1,128)S(1)}, u32[]{:S(2)}, u32[]{:S(2)}) collective-permute-start(f32[1,2048]{1,0:T(1,128)S(1)} %add.18.rest_0_), channel_id=1, source_target_pairs={{0,6},{1,7},{2,4},{3,5},{4,2},{5,3},{6,0},{7,1},{8,14},{9,15},{10,... | collective-permute-start | bytes 24584 | tf_op jit(solution)/shard_map/ppermute | solution.py:420
  102.6 2.1 %collective-permute-start.29 = (f32[264,256]{1,0:T(8,128)S(1)}, f32[264,256]{1,0:T(8,128)S(1)}, u32[]{:S(2)}, u32[]{:S(2)}) collective-permute-start(f32[264,256]{1,0:T(8,128)S(1)} %shard_map.82), channel_id=1, source_target_pairs={{0,8},{8,0},{16,24},{24,16},{1,9},{9,1},{17,25},{25,17},{2,10},{10... | collective-permute-start | bytes 811016 | tf_op jit(solution)/shard_map/ppermute | solution.py:420
  104.2 2.6 %collective-permute-start.35 = (f32[264,256]{1,0:T(8,128)S(1)}, f32[264,256]{1,0:T(8,128)S(1)}, u32[]{:S(2)}, u32[]{:S(2)}) collective-permute-start(f32[264,256]{1,0:T(8,128)S(1)} %shard_map.86), channel_id=1, source_target_pairs={{0,8},{8,0},{16,24},{24,16},{1,9},{9,1},{17,25},{25,17},{2,10},{10... | collective-permute-start | bytes 811016 | tf_op jit(solution)/shard_map/ppermute | solution.py:420
  106.2 9.4 %collective-permute-start.30 = (f32[264,256]{1,0:T(8,128)S(1)}, f32[264,256]{1,0:T(8,128)S(1)}, u32[]{:S(2)}, u32[]{:S(2)}) collective-permute-start(f32[264,256]{1,0:T(8,128)S(1)} %shard_map.83.p), channel_id=1, source_target_pairs={{0,1},{1,0},{2,3},{3,2},{4,5},{5,4},{6,7},{7,6},{8,9},{9,8},{10,11... | collective-permute-start | bytes 811016 | tf_op jit(solution)/shard_map/ppermute | solution.py:420
  108.2 12.2 %collective-permute-start.36 = (f32[264,256]{1,0:T(8,128)S(1)}, f32[264,256]{1,0:T(8,128)S(1)}, u32[]{:S(2)}, u32[]{:S(2)}) collective-permute-start(f32[264,256]{1,0:T(8,128)S(1)} %shard_map.87.p), channel_id=1, source_target_pairs={{0,1},{1,0},{2,3},{3,2},{4,5},{5,4},{6,7},{7,6},{8,9},{9,8},{10,11... | collective-permute-start | bytes 811016 | tf_op jit(solution)/shard_map/ppermute | solution.py:420
  115.6 4.9 %collective-permute-start.31 = (f32[264,256]{1,0:T(8,128)S(1)}, f32[264,256]{1,0:T(8,128)S(1)}, u32[]{:S(2)}, u32[]{:S(2)}) collective-permute-start(f32[264,256]{1,0:T(8,128)S(1)} %shard_map.84.refs_0_), channel_id=1, source_target_pairs={{0,8},{8,0},{16,24},{24,16},{1,9},{9,1},{17,25},{25,17},{2,10},{10... | collective-permute-start | bytes 811016 | tf_op jit(solution)/shard_map/ppermute | solution.py:420
  120.5 2.4 %collective-permute-start.37 = (f32[264,256]{1,0:T(8,128)S(1)}, f32[264,256]{1,0:T(8,128)S(1)}, u32[]{:S(2)}, u32[]{:S(2)}) collective-permute-start(f32[264,256]{1,0:T(8,128)S(1)} %shard_map.88.refs_0_), channel_id=1, source_target_pairs={{0,8},{8,0},{16,24},{24,16},{1,9},{9,1},{17,25},{25,17},{2,10},{10... | collective-permute-start | bytes 811016 | tf_op jit(solution)/shard_map/ppermute | solution.py:420
  122.8 11.7 %collective-permute-start.32 = (f32[40,256]{1,0:T(8,128)S(1)}, f32[40,256]{1,0:T(8,128)S(1)}, u32[]{:S(2)}, u32[]{:S(2)}) collective-permute-start(f32[40,256]{1,0:T(8,128)S(1)} %get-tuple-element.63), channel_id=1, source_target_pairs={{0,2},{1,3},{2,0},{3,1},{4,6},{5,7},{6,4},{7,5},{8,10},{9,11},{10,... | collective-permute-start | bytes 122888 | tf_op jit(solution)/shard_map/ppermute | solution.py:420
  125.2 6.0 %collective-permute-start.38 = (f32[2,2048]{1,0:T(2,128)S(1)}, f32[2,2048]{1,0:T(2,128)S(1)}, u32[]{:S(2)}, u32[]{:S(2)}) collective-permute-start(f32[2,2048]{1,0:T(2,128)S(1)} %pad_maximum_fusion.2.refs_4_), channel_id=1, source_target_pairs={{0,16},{8,24},{16,0},{24,8},{1,17},{9,25},{17,1},{25,9},{2,18},{10... | collective-permute-start | bytes 49160 | tf_op jit(solution)/shard_map/ppermute | solution.py:420
  126.8 8.9 %collective-permute-start.33 = (f32[40,256]{1,0:T(8,128)S(1)}, f32[40,256]{1,0:T(8,128)S(1)}, u32[]{:S(2)}, u32[]{:S(2)}) collective-permute-start(f32[40,256]{1,0:T(8,128)S(1)} %get-tuple-element.64), channel_id=1, source_target_pairs={{0,4},{1,5},{2,6},{3,7},{4,0},{5,1},{6,2},{7,3},{8,12},{9,13},{10,... | collective-permute-start | bytes 122888 | tf_op jit(solution)/shard_map/ppermute | solution.py:420
  130.0 6.3 %collective-permute-start.34 = (f32[40,256]{1,0:T(8,128)S(1)}, f32[40,256]{1,0:T(8,128)S(1)}, u32[]{:S(2)}, u32[]{:S(2)}) collective-permute-start(f32[40,256]{1,0:T(8,128)S(1)} %get-tuple-element.65), channel_id=1, source_target_pairs={{0,6},{1,7},{2,4},{3,5},{4,2},{5,3},{6,0},{7,1},{8,14},{9,15},{10,... | collective-permute-start | bytes 122888 | tf_op jit(solution)/shard_map/ppermute | solution.py:420
  131.2 5.0 %collective-permute-start.39 = (f32[40,256]{1,0:T(8,128)S(1)}, f32[40,256]{1,0:T(8,128)S(1)}, u32[]{:S(2)}, u32[]{:S(2)}) collective-permute-start(f32[40,256]{1,0:T(8,128)S(1)} %get-tuple-element.73), channel_id=1, source_target_pairs={{0,2},{1,3},{2,0},{3,1},{4,6},{5,7},{6,4},{7,5},{8,10},{9,11},{10,... | collective-permute-start | bytes 122888 | tf_op jit(solution)/shard_map/ppermute | solution.py:420
  131.3 5.8 %collective-permute-start.40 = (f32[40,256]{1,0:T(8,128)S(1)}, f32[40,256]{1,0:T(8,128)S(1)}, u32[]{:S(2)}, u32[]{:S(2)}) collective-permute-start(f32[40,256]{1,0:T(8,128)S(1)} %get-tuple-element.74), channel_id=1, source_target_pairs={{0,4},{1,5},{2,6},{3,7},{4,0},{5,1},{6,2},{7,3},{8,12},{9,13},{10,... | collective-permute-start | bytes 122888 | tf_op jit(solution)/shard_map/ppermute | solution.py:420
  134.4 5.8 %collective-permute-start.41 = (f32[40,256]{1,0:T(8,128)S(1)}, f32[40,256]{1,0:T(8,128)S(1)}, u32[]{:S(2)}, u32[]{:S(2)}) collective-permute-start(f32[40,256]{1,0:T(8,128)S(1)} %get-tuple-element.75), channel_id=1, source_target_pairs={{0,6},{1,7},{2,4},{3,5},{4,2},{5,3},{6,0},{7,1},{8,14},{9,15},{10,... | collective-permute-start | bytes 122888 | tf_op jit(solution)/shard_map/ppermute | solution.py:420
  141.0 1.2 collective-permute-start.42

commit v3 on v2

--- a/solution.py
+++ b/solution.py
@@ -128,16 +128,11 @@
         ))
         return out[0], out[1], out[2 : 2 + A], out[2 + A]
 
-    def cross(self, own, other, pieces):
-        F, M, N, A, Y, fs, ft, half, pb, nl = (
-            self.F, self.M, self.N, self.A, self.Y, self.fs, self.ft, self.half, self.pb, self.nl,
-        )
-
-        def body(own, other, *refs):
-            few = len(pieces)
-            s_ref, xt_ref, yh_ref, yl_ref, hy_ref, rowc_ref, logb_ref, stat_ref = refs[few : few + 8]
-            x_ref, y_ref, xh_ref, xl_ref = refs[few + 8 :]
-            y, c, a, b = position()
+    def rows(self, own, other):
+        F, M, A, ft, pb = self.F, self.M, self.A, self.ft, self.pb
+
+        def body(own, other, xt_ref, xh_ref, xl_ref, rowc_ref, x_ref):
+            _, c, a, b = position()
             for k in range(A):
                 for q in range(2):
                     at = rows_at((a ^ k) * 2 + (b ^ q), ft)
@@ -147,20 +142,6 @@
             for row in range(2):
                 rowc_ref[row : row + 1, lanes_at(c, pb)] = own[F + 4 * row : F + 4 * row + 1, :]
                 rowc_ref[row : row + 1, lanes_at(1 - c, pb)] = other[F + 4 * row : F + 4 * row + 1, :]
-            for (k, m, near, away, _), p in zip(pieces, refs):
-                cols = lanes_at(a ^ k, half)
-                if near:
-                    y_ref[rows_at((y ^ m) * 2 + c, fs), cols] = p[0:fs, :]
-                    if m == 0:
-                        logb_ref[0:1, cols] = p[fs : fs + 1, :]
-                if away:
-                    at = fs + 8 if near else 0
-                    y_ref[rows_at((y ^ m) * 2 + (1 - c), fs), cols] = p[at : at + fs, :]
-            for j in range(N // 256):
-                cols = slice(j * 256, (j + 1) * 256)
-                v = y_ref[:, cols]
-                hy_ref[0:1, cols] = (0.5 * L) * jnp.sum(v * v, 0, keepdims=True)
-                yh_ref[:, cols], yl_ref[:, cols] = split(v)
             for r in range(self.nr):
                 rows = slice(r * LANES, (r + 1) * LANES)
                 v = x_ref[:, rows]
@@ -168,32 +149,69 @@
                 vt = v.T
                 xt_ref[rows, :] = vt
                 xh_ref[rows, :], xl_ref[rows, :] = split(vt * L)
-            wide = 512
+
+        outs = (sds(M, F), sds(M, F, dtype=BF16), sds(M, F, dtype=BF16), sds(3, M))
+        return call(body, outs, (pltpu.VMEM((F, M), F32),), 10)(own, other)
+
+    def cross(self, xh, xl, pieces, before):
+        F, M, fs, half = self.F, self.M, self.fs, self.half
+        nb = half // LANES
+
+        def body(xh_ref, xl_ref, *refs):
+            few = len(pieces)
+            parts, prior = refs[:few], refs[few : few + len(before)]
+            s_ref, yh_ref, yl_ref, hy_ref, logb_ref, stat_ref, y_ref = refs[few + len(before) :]
+            y, c, _, _ = position()
+            for (m, near, away, _), p in zip(pieces, parts):
+                if near:
+                    y_ref[rows_at((y ^ m) * 2 + c, fs), :] = p[0:fs, :]
+                    if m == 0:
+                        logb_ref[...] = p[fs : fs + 1, :] * LOG2E
+                if away:
+                    at = fs + 8 if near else 0
+                    y_ref[rows_at((y ^ m) * 2 + (1 - c), fs), :] = p[at : at + fs, :]
+            for j in range(half // LANES):
+                cols = slice(j * LANES, (j + 1) * LANES)
+                v = y_ref[:, cols]
+                hy_ref[0:1, cols] = (0.5 * L) * jnp.sum(v * v, 0, keepdims=True)
+                yh_ref[:, cols], yl_ref[:, cols] = split(v)
             deep = min(256, M)
             for r in range(M // deep):
                 rows = slice(r * deep, (r + 1) * deep)
-                for j in range(N // wide):
-                    cols = slice(j * wide, (j + 1) * wide)
-                    s = dot3(xh_ref[rows, :], xl_ref[rows, :], yh_ref[:, cols], yl_ref[:, cols], ((1,), (0,)))
-                    s_ref[rows, cols] = s - hy_ref[0:1, cols]
+                s = dot3(xh_ref[rows, :], xl_ref[rows, :], yh_ref[...], yl_ref[...], ((1,), (0,)))
+                s_ref[rows, :] = s - hy_ref[...]
                 for h in range(deep // LANES):
                     at = r * deep + h * LANES
                     sub = slice(at, at + LANES)
                     top = s_ref[sub, 0:LANES]
-                    for l in range(1, nl):
+                    for l in range(1, nb):
                         top = jnp.maximum(top, s_ref[sub, l * LANES : (l + 1) * LANES])
                     peak = jnp.broadcast_to(jnp.max(top, 1, keepdims=True), (LANES, LANES))
                     acc = jnp.zeros((LANES, LANES), F32)
-                    for l in range(nl):
+                    for l in range(nb):
                         acc = acc + jnp.exp2(s_ref[sub, l * LANES : (l + 1) * LANES] - peak)
                     stat_ref[0:1, sub] = jnp.max(top.T, 0, keepdims=True)
                     stat_ref[1:2, sub] = jnp.sum(acc.T, 0, keepdims=True)
+            if before:
+                top, acc = joined([stat_ref[...]] + [v[...] for v in prior])
+                stat_ref[0:1, :] = top
+                stat_ref[1:2, :] = acc
 
         outs = (
-            sds(M, N), sds(M, F), sds(F, N, dtype=BF16), sds(F, N, dtype=BF16), sds(1, N), sds(3, M), sds(1, N), sds(2, M),
+            sds(M, half), sds(F, half, dtype=BF16), sds(F, half, dtype=BF16), sds(1, half), sds(1, half), sds(2, M),
         )
-        scratch = (pltpu.VMEM((F, M), F32), pltpu.VMEM((F, N), F32), pltpu.VMEM((M, F), BF16), pltpu.VMEM((M, F), BF16))
-        return call(body, outs, scratch, 20)(own, other, *(p[-1] for p in pieces))
+        return call(body, outs, (pltpu.VMEM((F, half), F32),), 10)(xh, xl, *(p[-1] for p in pieces), *before)
+
+    def blocks(self):
+        nb = self.half // LANES
+        return [(k, slice(l * LANES, (l + 1) * LANES), k * nb + l) for k in range(self.A) for l in range(nb)]
+
+    def chunk(self, k):
+        _, _, a, _ = position()
+        return lanes_at(a ^ k, self.half)
+
+    def own_order(self, k):
+        return slice(k * self.half, (k + 1) * self.half)
 
     def fill_cols(self, col_ref, row):
         for r in range(self.nr):
@@ -209,10 +227,11 @@
         m_ref[:, lane] = new
 
     def finish(self, m_ref, e_ref, out_ref):
-        m = m_ref[...]
-        top = jnp.max(m, 0, keepdims=True)
-        out_ref[0:1, :] = top
-        out_ref[1:2, :] = jnp.sum(e_ref[...] * jnp.exp2(m - top), 0, keepdims=True)
+        for k in range(self.A):
+            m = m_ref[:, self.own_order(k)]
+            top = jnp.max(m, 0, keepdims=True)
+            out_ref[0:1, self.chunk(k)] = top
+            out_ref[1:2, self.chunk(k)] = jnp.sum(e_ref[:, self.own_order(k)] * jnp.exp2(m - top), 0, keepdims=True)
 
     def start(self, m_ref, e_ref):
         m_ref[...] = jnp.full((8, self.N), -1e30, F32)
@@ -225,8 +244,10 @@
         return pltpu.VMEM((self.M, LANES), F32)
 
     def col1(self, s, rowc, stats):
-        def body(s_ref, rowc, *refs):
-            stats, (f_ref, out_ref, col_ref, m_ref, e_ref) = refs[:-5], refs[-5:]
+        A = self.A
+
+        def body(*refs):
+            s_refs, rowc, stats, (f_ref, out_ref, col_ref, m_ref, e_ref) = refs[:A], refs[A], refs[A + 1 : -5], refs[-5:]
             f = rowc[0:1, :] * LOG2E - lse2(stats)
             f_ref[...] = f
             self.fill_cols(col_ref, f)
@@ -236,32 +257,37 @@
             def _(r):
                 rows = pl.ds(pl.multiple_of(r * LANES, LANES), LANES)
                 fc = col_ref[rows, :]
-                for l in range(self.nl):
-                    self.online(s_ref[rows, l * LANES : (l + 1) * LANES] + fc, l, m_ref, e_ref)
+                for k, lane, l in self.blocks():
+                    self.online(s_refs[k][rows, lane] + fc, l, m_ref, e_ref)
 
             self.finish(m_ref, e_ref, out_ref)
 
-        return call(body, (sds(1, self.M), sds(2, self.N)), (self.cols(), *self.stats()), 10)(s, rowc, *stats)
+        return call(body, (sds(1, self.M), sds(2, self.N)), (self.cols(), *self.stats()), 10)(*s, rowc, *stats)
 
     def row2(self, s, f, logb, stats):
-        def body(s_ref, f, logb, *refs):
-            stats, (g_ref, out_ref, col_ref) = refs[:-3], refs[-3:]
-            g_ref[...] = logb[...] * LOG2E - lse2(stats)
+        A = self.A
+
+        def body(*refs):
+            s_refs, f, logb, stats, (g_ref, out_ref, col_ref) = refs[:A], refs[A], refs[A + 1 : 2 * A + 1], refs[2 * A + 1 : -3], refs[-3:]
+            for k in range(A):
+                g_ref[:, self.own_order(k)] = logb[k][...] - lse2([v[:, self.chunk(k)] for v in stats])
             self.fill_cols(col_ref, f)
             for r in range(self.nr):
                 rows = slice(r * LANES, (r + 1) * LANES)
                 fc = col_ref[rows, :]
                 acc = jnp.zeros((LANES, LANES), F32)
-                for l in range(self.nl):
-                    lane = slice(l * LANES, (l + 1) * LANES)
-                    acc = acc + jnp.exp2(s_ref[rows, lane] + fc + g_ref[:, lane])
+                for k, lane, l in self.blocks():
+                    acc = acc + jnp.exp2(s_refs[k][rows, lane] + fc + g_ref[:, l * LANES : (l + 1) * LANES])
                 out_ref[0:1, rows] = jnp.sum(acc.T, 0, keepdims=True)
 
-        return call(body, (sds(1, self.N), sds(1, self.M)), (self.cols(),), 10)(s, f, logb, *stats)
+        return call(body, (sds(1, self.N), sds(1, self.M)), (self.cols(),), 10)(*s, f, *logb, *stats)
 
     def col2(self, s, f, g, rowc, sums):
-        def body(s_ref, f, g, rowc, *refs):
-            sums, (f_ref, out_ref, col_ref, acc_ref) = refs[:-4], refs[-4:]
+        A = self.A
+
+        def body(*refs):
+            s_refs, f, g, rowc = refs[:A], refs[A], refs[A + 1], refs[A + 2]
+            sums, (f_ref, out_ref, col_ref, acc_ref) = refs[A + 3 : -4], refs[-4:]
             f2 = f[...] + rowc[0:1, :] * LOG2E - log2(total(sums))
             f_ref[...] = f2
             self.fill_cols(col_ref, f2)
@@ -271,59 +297,69 @@
             def _(r):
                 rows = pl.ds(pl.multiple_of(r * LANES, LANES), LANES)
                 fc = col_ref[rows, :]
-                for l in range(self.nl):
-                    lane = slice(l * LANES, (l + 1) * LANES)
-                    p = jnp.exp2(s_ref[rows, lane] + fc + g[:, lane])
-                    acc_ref[:, lane] = acc_ref[:, lane] + jnp.sum(groups(p), 0)
-
-            out_ref[...] = jnp.sum(acc_ref[...], 0, keepdims=True)
+                for k, lane, l in self.blocks():
+                    at = slice(l * LANES, (l + 1) * LANES)
+                    p = jnp.exp2(s_refs[k][rows, lane] + fc + g[:, at])
+                    acc_ref[:, at] = acc_ref[:, at] + jnp.sum(groups(p), 0)
+
+            for k in range(A):
+                out_ref[0:1, self.chunk(k)] = jnp.sum(acc_ref[:, self.own_order(k)], 0, keepdims=True)
 
         scratch = (self.cols(), self.stats()[0])
-        return call(body, (sds(1, self.M), sds(1, self.N)), scratch, 10)(s, f, g, rowc, *sums)
+        return call(body, (sds(1, self.M), sds(1, self.N)), scratch, 10)(*s, f, g, rowc, *sums)
 
     def plan(self, s, f, g, sums, logb, yh, yl, mine, q, base):
-        N, F, qr, mw = self.N, self.F, self.qr, self.mw
-
-        def body(s_ref, f, g, logb, yh, yl, *rest):
+        N, F, A, qr, mw = self.N, self.F, self.A, self.qr, self.mw
+
+        def body(*refs):
+            s_refs, logb, yh, yl, (f, g), rest = (
+                refs[:A], refs[A : 2 * A], refs[2 * A : 3 * A], refs[3 * A : 4 * A], refs[4 * A : 4 * A + 2], refs[4 * A + 2 :],
+            )
             few = len(sums)
             parts, extra, (w_ref, g_ref, ph_ref, pl_ref) = rest[:few], rest[few:-4], rest[-4:]
             _, c, _, _ = position()
             at = (c if mine else 1 - c) * self.pb + q * qr
-            g_ref[...] = g[...] + logb[...] * LOG2E - log2(total(parts))
+            for k in range(A):
+                cols = self.own_order(k)
+                g_ref[:, cols] = g[:, cols] + logb[k][...] - log2(total([v[:, self.chunk(k)] for v in parts]))
             for r in range(qr // LANES):
-                fc = to_col(f[0:1, pl.ds(pl.multiple_of(at + r * LANES, LANES), LANES)])
                 rows = pl.ds(pl.multiple_of(at + r * LANES, LANES), LANES)
+                fc = to_col(f[0:1, rows])
                 local = slice(r * LANES, (r + 1) * LANES)
                 acc = jnp.zeros((LANES, LANES), F32)
-                for l in range(self.nl):
-                    lane = slice(l * LANES, (l + 1) * LANES)
-                    p = jnp.exp2(s_ref[rows, lane] + fc + g_ref[:, lane])
+                for k, lane, l in self.blocks():
+                    cols = slice(l * LANES, (l + 1) * LANES)
+                    p = jnp.exp2(s_refs[k][rows, lane] + fc + g_ref[:, cols])
                     acc = acc + p
-                    ph_ref[local, lane], pl_ref[local, lane] = split(p)
+                    ph_ref[local, cols], pl_ref[local, cols] = split(p)
                 i, j = divmod(r * LANES, mw)
                 mass = jnp.sum(acc.T, 0, keepdims=True)
                 if extra:
                     mass = mass + extra[0][qr + i : qr + i + 1, j : j + LANES]
                 w_ref[qr + i : qr + i + 1, j : j + LANES] = mass
-            w = dot3(ph_ref[...], pl_ref[...], yh[...], yl[...], ((1,), (1,)))
+            w = None
+            for k in range(A):
+                cols = self.own_order(k)
+                d = dot3(ph_ref[:, cols], pl_ref[:, cols], yh[k][...], yl[k][...], ((1,), (1,)))
+                w = d if w is None else w + d
             w_ref[0:qr, :] = w + extra[0][0:qr, :] if extra else w
 
         scratch = (pltpu.VMEM((1, N), F32), pltpu.VMEM((qr, N), BF16), pltpu.VMEM((qr, N), BF16))
-        args = (s, f, g, logb, yh, yl, *sums) + (() if base is None else (base,))
+        args = (*s, *logb, *yh, *yl, f, g, *sums) + (() if base is None else (base,))
         return call(body, sds(qr + 8, F), scratch, 14)(*args)
 
     def last(self, own, other, xt, f, rowc, yh, yl, hy, q):
         F, M, N, A, ft, pb, qr, mw = self.F, self.M, self.N, self.A, self.ft, self.pb, self.qr, self.mw
 
         def entry(*refs):
-            ins, outs, (m_ref, e_ref, mt_ref) = refs[:8], refs[8:-3], refs[-3:]
+            ins, ys, outs, (m_ref, e_ref, mt_ref) = refs[:5], refs[5 : 5 + 3 * A], refs[5 + 3 * A : -3], refs[-3:]
             parcels, out_ref = outs[:A], outs[A]
-            body(*ins, parcels, out_ref, m_ref, e_ref, mt_ref)
+            body(*ins, ys[:A], ys[A : 2 * A], ys[2 * A :], parcels, out_ref, m_ref, e_ref, mt_ref)
 
         def body(own, other, xt, f, rowc, yh, yl, hy, parcels, out_ref, m_ref, e_ref, mt_ref):
             _, c, a, b = position()
             self.start(m_ref, e_ref)
-            wide = min(512, N)
+            wide = self.half
             for src, core in ((own, c), (other, 1 - c)):
                 for r in range(qr // LANES):
                     at = pl.ds(pl.multiple_of(core * pb + (q * qr + r * LANES), LANES), LANES)
@@ -341,9 +377,8 @@
                             parcels[k][ft : ft + 8, lane] = jnp.broadcast_to((EPS * LN2) * (f[0:1, at] + nx), (8, LANES))
                     fc = to_col(f[0:1, at] + nx - (0.5 * L) * jnp.sum(mt * mt, 0, keepdims=True))
                     mh, ml = split(mv * L)
-                    for n in range(N // wide):
-                        cols = slice(n * wide, (n + 1) * wide)
-                        v = dot3(mh, ml, yh[:, cols], yl[:, cols], ((1,), (0,))) - hy[0:1, cols]
+                    for n in range(A):
+                        v = dot3(mh, ml, yh[n][...], yl[n][...], ((1,), (0,))) - hy[n][...]
                         for l in range(wide // LANES):
                             lane = slice(l * LANES, (l + 1) * LANES)
                             self.online(v[:, lane] + fc, n * (wide // LANES) + l, m_ref, e_ref)
@@ -352,7 +387,7 @@
             self.finish(m_ref, e_ref, out_ref)
 
         outs = (*(sds(ft + 8, qr) for _ in range(A)), sds(2, N))
-        out = call(entry, outs, (*self.stats(), pltpu.VMEM((F, qr), F32)), 14)(own, other, xt, f, rowc, yh, yl, hy)
+        out = call(entry, outs, (*self.stats(), pltpu.VMEM((F, qr), F32)), 14)(own, other, xt, f, rowc, *yh, *yl, *hy)
         return out[:A], out[A]
 
     def pack(self, parcels, stats):
@@ -452,7 +487,7 @@
     def over_cols(v, op):
         v = along_y(v, op)
         v = op(*v) if Y > 1 else v[0]
-        return [v] + [over_a(v, k) for k in range(A - 1, 0, -1)]
+        return [v] + [over_a(v, k) for k in range(1, A)]
 
     def per_device(sources, targets, source_logw, target_logw, times):
         ft, ns = sources.shape
@@ -472,12 +507,12 @@
                 chunks[k ^ bit] = []
                 for near, far, v in halves if k == 0 and bit == A // 2 else chunks[k]:
                     chunks[k ^ bit].append((near, far, over_a(v, bit)))
-        pieces = []
+        pieces = [[] for _ in range(A)]
         for k in range(A):
             for near, far, v in chunks[k]:
-                pieces.append((k, 0, near, far, v))
+                pieces[k].append((0, near, far, v))
                 for m in range(1, Y):
-                    pieces.append((k, m, near, far, over_y(v, m)))
+                    pieces[k].append((m, near, far, over_y(v, m)))
         parts = [blocks[0]]
         for k in range(1, A):
             parts.append(over_a(blocks[k], k))
@@ -486,7 +521,14 @@
         x_own = jnp.concatenate([xs, xb, side])
         x_other = over_c(x_own)
 
-        sc, xt, yh, yl, hy, rowc, logb, stat = kern.cross(x_own, x_other, pieces)
+        xt, xh, xl, rowc = kern.rows(x_own, x_other)
+        found, stats = [], []
+        for k in range(A):
+            out = kern.cross(xh, xl, pieces[k], stats if k == A - 1 else [])
+            found.append(out[:-1])
+            stats.append(out[-1])
+        sc, yh, yl, hy, logb = zip(*found)
+        stat = stats[-1]
         f1, stat = kern.col1(sc, rowc, over_rows(stat, join))
         g1, sums = kern.row2(sc, f1, logb, over_cols(stat, join))
         f2, sums = kern.col2(sc, f1, g1, rowc, over_rows(sums, add))

time: 143 us -> 132 us (0.923)
  waiting for transfers between devices: 71.3 us -> 54.7 us
  starting transfers between devices: 47.9 us -> 52.5 us
    ppermute x43, waiting for transfers between devices: 71.3 us -> 54.7 us  [swap(): return lax.ppermute(v, axis, [(i, i ^ k) for i in range(size)])]
    ppermute x43, starting transfers between devices: 47.9 us -> 52.5 us  [swap(): return lax.ppermute(v, axis, [(i, i ^ k) for i in range(size)])]
    pallas_call x1 -> x5, Pallas kernels: 4.55 us -> 5.95 us  [the longest x4 5.53 us: cross(): call(body, outs, (pltpu.VMEM((F, half), F32),), 10)]
  transfers between devices with their start and end apart: 43 -> 43, of which waited for: 26 -> 26; matrix products, arithmetic and copies ran while one was open for 0% -> 0% of each run, Pallas kernels for 6% -> 10%
where the time goes in v3:
time: 132 us
  waiting for transfers between devices  54.7 us (41%)
  starting transfers between devices  52.5 us (40%)
  Pallas kernels  23.7 us (18%)
    ppermute x43, waiting for transfers between devices, swap(): return lax.ppermute(v, axis, [(i, i ^ k) for i in range(size)])  54.7 us
    ppermute x43, starting transfers between devices, swap(): return lax.ppermute(v, axis, [(i, i ^ k) for i in range(size)])  52.5 us
    pallas_call x4, Pallas kernels, plan(): return call(body, sds(qr + 8, F), scratch, 14)(*args)  5.85 us
    pallas_call x4, Pallas kernels, cross(): call(body, outs, (pltpu.VMEM((F, half), F32),), 10)  5.53 us
    pallas_call x2, Pallas kernels, last(): call(entry, outs, (*self.stats(), pltpu.VMEM((F, qr), F32)), 14)  4.2 us
  transfers between devices with their start and end apart: 43, of which 26 were waited for; matrix products, arithmetic and copies ran while one was open for 0% of the time, Pallas kernels for 10%

profile of v3, /device:TPU:0, one launch (start us, length us, event | category | flops | bytes accessed | tf_op | source)
XLA Modules:
  0.0 132.1 jit_solution(9504066641565930585)
XLA Ops:
  1.8 3.1 %collective-permute-start = (f32[32,512]{1,0:T(8,128)S(1)}, f32[32,512]{1,0:T(8,128)S(1)}, u32[]{:S(2)}, u32[]{:S(2)}) collective-permute-start(f32[32,512]{1,0:T(8,128)S(1)} %get-tuple-element.62), channel_id=1, source_target_pairs={{0,2},{1,3},{2,0},{3,1},{4,6},{5,7},{6,4},{7,5},{8,10},{9,11},{10,... | collective-permute-start | bytes 196616 | tf_op jit(solution)/shard_map/ppermute | solution.py:455
  5.0 2.6 %collective-permute-start.1 = (f32[32,512]{1,0:T(8,128)S(1)}, f32[32,512]{1,0:T(8,128)S(1)}, u32[]{:S(2)}, u32[]{:S(2)}) collective-permute-start(f32[32,512]{1,0:T(8,128)S(1)} %get-tuple-element.63), channel_id=1, source_target_pairs={{0,4},{1,5},{2,6},{3,7},{4,0},{5,1},{6,2},{7,3},{8,12},{9,13},{10,... | collective-permute-start | bytes 196616 | tf_op jit(solution)/shard_map/ppermute | solution.py:455
  7.6 4.7 %collective-permute-done.1.refs_2_ = f32[32,512]{1,0:T(8,128)S(1)} collective-permute-done((f32[32,512]{1,0:T(8,128)S(1)}, f32[32,512]{1,0:T(8,128)S(1)}, u32[]{:S(2)}, u32[]{:S(2)}) %collective-permute-start.1) | collective-permute-done | bytes 65568 | tf_op jit(solution)/shard_map/ppermute | solution.py:455
  12.2 1.4 %collective-permute-done.2.refs_3_ = f32[32,512]{1,0:T(8,128)S(1)} collective-permute-done((f32[32,512]{1,0:T(8,128)S(1)}, f32[32,512]{1,0:T(8,128)S(1)}, u32[]{:S(2)}, u32[]{:S(2)}) %collective-permute-start.2) | collective-permute-done | bytes 65568 | tf_op jit(solution)/shard_map/ppermute | solution.py:455
  13.6 1.6 %collective-permute-start.3 = (f32[128,512]{1,0:T(8,128)S(1)}, f32[128,512]{1,0:T(8,128)S(1)}, u32[]{:S(2)}, u32[]{:S(2)}) collective-permute-start(f32[128,512]{1,0:T(8,128)S(1)} %shard_map.77), channel_id=1, source_target_pairs={{0,1},{1,0},{2,3},{3,2},{4,5},{5,4},{6,7},{7,6},{8,9},{9,8},{10,11... | collective-permute-start | bytes 786440 | tf_op jit(solution)/shard_map/ppermute | solution.py:455
  16.6 3.5 %collective-permute-done.3 = f32[128,512]{1,0:T(8,128)S(1)} collective-permute-done((f32[128,512]{1,0:T(8,128)S(1)}, f32[128,512]{1,0:T(8,128)S(1)}, u32[]{:S(2)}, u32[]{:S(2)}) %collective-permute-start.3) | collective-permute-done | bytes 262176 | tf_op jit(solution)/shard_map/ppermute | solution.py:455
  20.3 2.1 %collective-permute-start.9 = (f32[72,512]{1,0:T(8,128)S(1)}, f32[72,512]{1,0:T(8,128)S(1)}, u32[]{:S(2)}, u32[]{:S(2)}) collective-permute-start(f32[72,512]{1,0:T(8,128)S(1)} %get-tuple-element.68.refs_8_), channel_id=1, source_target_pairs={{0,4},{1,5},{2,6},{3,7},{4,0},{5,1},{6,2},{7,3},{8,12},{9,13},{10,... | collective-permute-start | bytes 442376 | tf_op jit(solution)/shard_map/ppermute | solution.py:455
  22.4 5.1 %collective-permute-done.7.refs_0_ = f32[136,512]{1,0:T(8,128)S(1)} collective-permute-done((f32[136,512]{1,0:T(8,128)S(1)}, f32[136,512]{1,0:T(8,128)S(1)}, u32[]{:S(2)}, u32[]{:S(2)}) %collective-permute-start.7) | collective-permute-done | bytes 278560 | tf_op jit(solution)/shard_map/ppermute | solution.py:455
  27.5 1.5 %collective-permute-start.8 = (f32[136,512]{1,0:T(8,128)S(1)}, f32[136,512]{1,0:T(8,128)S(1)}, u32[]{:S(2)}, u32[]{:S(2)}) collective-permute-start(f32[136,512]{1,0:T(8,128)S(1)} %collective-permute-done.7.refs_0_), channel_id=1, source_target_pairs={{0,16},{8,24},{16,0},{24,8},{1,17},{9,25},{17,1},{25,9},{2,18},{10... | collective-permute-start | bytes 835592 | tf_op jit(solution)/shard_map/ppermute | solution.py:455
  29.3 3.3 %collective-permute-done.9.refs_0_ = f32[72,512]{1,0:T(8,128)S(1)} collective-permute-done((f32[72,512]{1,0:T(8,128)S(1)}, f32[72,512]{1,0:T(8,128)S(1)}, u32[]{:S(2)}, u32[]{:S(2)}) %collective-permute-start.9) | collective-permute-done | bytes 147488 | tf_op jit(solution)/shard_map/ppermute | solution.py:455
  32.6 2.9 %collective-permute-start.6 = (f32[136,512]{1,0:T(8,128)S(1)}, f32[136,512]{1,0:T(8,128)S(1)}, u32[]{:S(2)}, u32[]{:S(2)}) collective-permute-start(f32[136,512]{1,0:T(8,128)S(1)} %constant_dynamic-update-slice_fusion.refs_0_), channel_id=1, source_target_pairs={{0,16},{8,24},{16,0},{24,8},{1,17},{9,25},{17,1},{25,9},{2,18},{10... | collective-permute-start | bytes 835592 | tf_op jit(solution)/shard_map/ppermute | solution.py:455
  37.5 2.0 %collective-permute-done.13.refs_0_ = f32[72,512]{1,0:T(8,128)S(1)} collective-permute-done((f32[72,512]{1,0:T(8,128)S(1)}, f32[72,512]{1,0:T(8,128)S(1)}, u32[]{:S(2)}, u32[]{:S(2)}) %collective-permute-start.13) | collective-permute-done | bytes 147488 | tf_op jit(solution)/shard_map/ppermute | solution.py:455
  39.5 2.4 %collective-permute-start.10 = (f32[72,512]{1,0:T(8,128)S(1)}, f32[72,512]{1,0:T(8,128)S(1)}, u32[]{:S(2)}, u32[]{:S(2)}) collective-permute-start(f32[72,512]{1,0:T(8,128)S(1)} %collective-permute-done.9.refs_0_), channel_id=1, source_target_pairs={{0,16},{8,24},{16,0},{24,8},{1,17},{9,25},{17,1},{25,9},{2,18},{10... | collective-permute-start | bytes 442376 | tf_op jit(solution)/shard_map/ppermute | solution.py:455
  41.9 1.8 %collective-permute-start.14 = (f32[72,512]{1,0:T(8,128)S(1)}, f32[72,512]{1,0:T(8,128)S(1)}, u32[]{:S(2)}, u32[]{:S(2)}) collective-permute-start(f32[72,512]{1,0:T(8,128)S(1)} %collective-permute-done.13.refs_0_), channel_id=1, source_target_pairs={{0,16},{8,24},{16,0},{24,8},{1,17},{9,25},{17,1},{25,9},{2,18},{10... | collective-permute-start | bytes 442376 | tf_op jit(solution)/shard_map/ppermute | solution.py:455
  43.9 1.8 %collective-permute-start.16 = (f32[64,512]{1,0:T(8,128)S(1)}, f32[64,512]{1,0:T(8,128)S(1)}, u32[]{:S(2)}, u32[]{:S(2)}) collective-permute-start(f32[64,512]{1,0:T(8,128)S(1)} %collective-permute-done.15.refs_2_), channel_id=1, source_target_pairs={{0,16},{8,24},{16,0},{24,8},{1,17},{9,25},{17,1},{25,9},{2,18},{10... | collective-permute-start | bytes 393224 | tf_op jit(solution)/shard_map/ppermute | solution.py:455
  46.2 1.4 %shard_map.80 = (f32[1024,512]{1,0:T(8,128)S(1)}, bf16[256,512]{1,0:T(8,128)(2,1)S(1)}, bf16[256,512]{1,0:T(8,128)(2,1)S(1)}, f32[1,512]{1,0:T(1,128)S(1)}, f32[1,512]{1,0:T(1,128)S(1)}, /*index=5*/f32[2,1024]{1,0:T(2,128)S(1)}) custom-call(bf16[1024,256]{1,0:T(8,128)(2,1)S(1)} %get-tuple-element.66.xh_ref, bf16[1024,256]{1,0:T(8,128)(2,1)S(1)} %get-tuple-element.67.xl_ref, ...), custom_call_target="tpu_custom_call" | custom-call | tf_op jit(solution)/shard_map/pallas_call | solution.py:203
  47.6 1.4 %shard_map.79 = (f32[1024,512]{1,0:T(8,128)S(1)}, bf16[256,512]{1,0:T(8,128)(2,1)S(1)}, bf16[256,512]{1,0:T(8,128)(2,1)S(1)}, f32[1,512]{1,0:T(1,128)S(1)}, f32[1,512]{1,0:T(1,128)S(1)}, /*index=5*/f32[2,1024]{1,0:T(2,128)S(1)}) custom-call(bf16[1024,256]{1,0:T(8,128)(2,1)S(1)} %get-tuple-element.66.xh_ref, bf16[1024,256]{1,0:T(8,128)(2,1)S(1)} %get-tuple-element.67.xl_ref, ...), custom_call_target="tpu_custom_call" | custom-call | tf_op jit(solution)/shard_map/pallas_call | solution.py:203
  48.9 3.4 %collective-permute-done.12.refs_3_ = f32[64,512]{1,0:T(8,128)S(1)} collective-permute-done((f32[64,512]{1,0:T(8,128)S(1)}, f32[64,512]{1,0:T(8,128)S(1)}, u32[]{:S(2)}, u32[]{:S(2)}) %collective-permute-start.12) | collective-permute-done | bytes 131104 | tf_op jit(solution)/shard_map/ppermute | solution.py:455
  52.3 1.4 %shard_map.81 = (f32[1024,512]{1,0:T(8,128)S(1)}, bf16[256,512]{1,0:T(8,128)(2,1)S(1)}, bf16[256,512]{1,0:T(8,128)(2,1)S(1)}, f32[1,512]{1,0:T(1,128)S(1)}, f32[1,512]{1,0:T(1,128)S(1)}, /*index=5*/f32[2,1024]{1,0:T(2,128)S(1)}) custom-call(bf16[1024,256]{1,0:T(8,128)(2,1)S(1)} %get-tuple-element.66.xh_ref, bf16[1024,256]{1,0:T(8,128)(2,1)S(1)} %get-tuple-element.67.xl_ref, ...), custom_call_target="tpu_custom_call" | custom-call | tf_op jit(solution)/shard_map/pallas_call | solution.py:203
  53.8 1.4 %shard_map.82 = (f32[1024,512]{1,0:T(8,128)S(1)}, bf16[256,512]{1,0:T(8,128)(2,1)S(1)}, bf16[256,512]{1,0:T(8,128)(2,1)S(1)}, f32[1,512]{1,0:T(1,128)S(1)}, f32[1,512]{1,0:T(1,128)S(1)}, /*index=5*/f32[2,1024]{1,0:T(2,128)S(1)}) custom-call(bf16[1024,256]{1,0:T(8,128)(2,1)S(1)} %get-tuple-element.66.xh_ref, bf16[1024,256]{1,0:T(8,128)(2,1)S(1)} %get-tuple-element.67.xl_ref, ...), custom_call_target="tpu_custom_call" | custom-call | tf_op jit(solution)/shard_map/pallas_call | solution.py:203
  56.5 1.9 %collective-permute-start.18 = (f32[2,1024]{1,0:T(2,128)S(1)}, f32[2,1024]{1,0:T(2,128)S(1)}, u32[]{:S(2)}, u32[]{:S(2)}) collective-permute-start(f32[2,1024]{1,0:T(2,128)S(1)} %pad_maximum_fusion.3.refs_5_), channel_id=1, source_target_pairs={{0,1},{1,0},{2,3},{3,2},{4,5},{5,4},{6,7},{7,6},{8,9},{9,8},{10,11... | collective-permute-start | bytes 24584 | tf_op jit(solution)/shard_map/ppermute | solution.py:455
  58.4 1.8 %collective-permute-done.18.refs_6_ = f32[2,1024]{1,0:T(2,128)S(1)} collective-permute-done((f32[2,1024]{1,0:T(2,128)S(1)}, f32[2,1024]{1,0:T(2,128)S(1)}, u32[]{:S(2)}, u32[]{:S(2)}) %collective-permute-start.18) | collective-permute-done | bytes 8224 | tf_op jit(solution)/shard_map/ppermute | solution.py:455
  60.2 2.0 %shard_map.83 = (f32[1,1024]{1,0:T(1,128)S(1)}, f32[2,2048]{1,0:T(2,128)S(1)}) custom-call(f32[1024,512]{1,0:T(8,128)S(1)} %get-tuple-element.70.refs_0_, f32[1024,512]{1,0:T(8,128)S(1)} %get-tuple-element.71.refs_1_, f32[1024,512]{1,0:T(8,128)S(1)} %get-tuple-element.72.refs_2_, f32[1024,512]{1,0:T(8,128)S(1)} %get-tuple-element.76.refs_3_, ...), custom_call_target="tpu_custom_call" | custom-call | tf_op jit(solution)/shard_map/pallas_call | solution.py:265
  62.3 2.1 %collective-permute-start.19 = (f32[2,2048]{1,0:T(2,128)S(1)}, f32[2,2048]{1,0:T(2,128)S(1)}, u32[]{:S(2)}, u32[]{:S(2)}) collective-permute-start(f32[2,2048]{1,0:T(2,128)S(1)} %get-tuple-element.92), channel_id=1, source_target_pairs={{0,16},{8,24},{16,0},{24,8},{1,17},{9,25},{17,1},{25,9},{2,18},{10... | collective-permute-start | bytes 49160 | tf_op jit(solution)/shard_map/ppermute | solution.py:455
  64.3 1.8 %collective-permute-done.19 = f32[2,2048]{1,0:T(2,128)S(1)} collective-permute-done((f32[2,2048]{1,0:T(2,128)S(1)}, f32[2,2048]{1,0:T(2,128)S(1)}, u32[]{:S(2)}, u32[]{:S(2)}) %collective-permute-start.19) | collective-permute-done | bytes 16416 | tf_op jit(solution)/shard_map/ppermute | solution.py:455
  66.1 1.8 %collective-permute-start.22 = (f32[2,2048]{1,0:T(2,128)S(1)}, f32[2,2048]{1,0:T(2,128)S(1)}, u32[]{:S(2)}, u32[]{:S(2)}) collective-permute-start(f32[2,2048]{1,0:T(2,128)S(1)} %pad_maximum_fusion.1.refs_9_), channel_id=1, source_target_pairs={{0,6},{1,7},{2,4},{3,5},{4,2},{5,3},{6,0},{7,1},{8,14},{9,15},{10,... | collective-permute-start | bytes 49160 | tf_op jit(solution)/shard_map/ppermute | solution.py:455
  68.6 2.0 %collective-permute-start.20 = (f32[2,2048]{1,0:T(2,128)S(1)}, f32[2,2048]{1,0:T(2,128)S(1)}, u32[]{:S(2)}, u32[]{:S(2)}) collective-permute-start(f32[2,2048]{1,0:T(2,128)S(1)} %pad_maximum_fusion.1.refs_9_), channel_id=1, source_target_pairs={{0,2},{1,3},{2,0},{3,1},{4,6},{5,7},{6,4},{7,5},{8,10},{9,11},{10,... | collective-permute-start | bytes 49160 | tf_op jit(solution)/shard_map/ppermute | solution.py:455
  75.1 2.0 %collective-permute-start.24 = (f32[1,1024]{1,0:T(1,128)S(1)}, f32[1,1024]{1,0:T(1,128)S(1)}, u32[]{:S(2)}, u32[]{:S(2)}) collective-permute-start(f32[1,1024]{1,0:T(1,128)S(1)} %add.17.refs_7_), channel_id=1, source_target_pairs={{0,1},{1,0},{2,3},{3,2},{4,5},{5,4},{6,7},{7,6},{8,9},{9,8},{10,11... | collective-permute-start | bytes 12296 | tf_op jit(solution)/shard_map/ppermute | solution.py:455
  77.1 1.6 %collective-permute-done.24.refs_8_ = f32[1,1024]{1,0:T(1,128)S(1)} collective-permute-done((f32[1,1024]{1,0:T(1,128)S(1)}, f32[1,1024]{1,0:T(1,128)S(1)}, u32[]{:S(2)}, u32[]{:S(2)}) %collective-permute-start.24) | collective-permute-done | bytes 4128 | tf_op jit(solution)/shard_map/ppermute | solution.py:455
  78.7 1.7 %shard_map.85 = (f32[1,1024]{1,0:T(1,128)S(1)}, f32[1,2048]{1,0:T(1,128)S(1)}) custom-call(f32[1024,512]{1,0:T(8,128)S(1)} %get-tuple-element.70.refs_0_, f32[1024,512]{1,0:T(8,128)S(1)} %get-tuple-element.71.refs_1_, f32[1024,512]{1,0:T(8,128)S(1)} %get-tuple-element.72.refs_2_, f32[1024,512]{1,0:T(8,128)S(1)} %get-tuple-element.76.refs_3_, ...), custom_call_target="tpu_custom_call" | custom-call | tf_op jit(solution)/shard_map/pallas_call | solution.py:309
  80.5 2.1 %collective-permute-start.25 = (f32[1,2048]{1,0:T(1,128)S(1)}, f32[1,2048]{1,0:T(1,128)S(1)}, u32[]{:S(2)}, u32[]{:S(2)}) collective-permute-start(f32[1,2048]{1,0:T(1,128)S(1)} %get-tuple-element.96), channel_id=1, source_target_pairs={{0,16},{8,24},{16,0},{24,8},{1,17},{9,25},{17,1},{25,9},{2,18},{10... | collective-permute-start | bytes 24584 | tf_op jit(solution)/shard_map/ppermute | solution.py:455
  82.5 1.7 %collective-permute-done.25 = f32[1,2048]{1,0:T(1,128)S(1)} collective-permute-done((f32[1,2048]{1,0:T(1,128)S(1)}, f32[1,2048]{1,0:T(1,128)S(1)}, u32[]{:S(2)}, u32[]{:S(2)}) %collective-permute-start.25) | collective-permute-done | bytes 8224 | tf_op jit(solution)/shard_map/ppermute | solution.py:455
  84.2 2.2 %collective-permute-start.28 = (f32[1,2048]{1,0:T(1,128)S(1)}, f32[1,2048]{1,0:T(1,128)S(1)}, u32[]{:S(2)}, u32[]{:S(2)}) collective-permute-start(f32[1,2048]{1,0:T(1,128)S(1)} %add.18.refs_18_), channel_id=1, source_target_pairs={{0,6},{1,7},{2,4},{3,5},{4,2},{5,3},{6,0},{7,1},{8,14},{9,15},{10,... | collective-permute-start | bytes 24584 | tf_op jit(solution)/shard_map/ppermute | solution.py:455
  91.1 1.5 %shard_map.86 = f32[264,256]{1,0:T(8,128)S(1)} custom-call(f32[1024,512]{1,0:T(8,128)S(1)} %get-tuple-element.70.refs_0_, f32[1024,512]{1,0:T(8,128)S(1)} %get-tuple-element.71.refs_1_, f32[1024,512]{1,0:T(8,128)S(1)} %get-tuple-element.72.refs_2_, f32[1024,512]{1,0:T(8,128)S(1)} %get-tuple-element.76.refs_3_, ...), custom_call_target="tpu_custom_call" | custom-call | tf_op jit(solution)/shard_map/pallas_call | solution.py:349
  92.7 1.5 %shard_map.90 = f32[264,256]{1,0:T(8,128)S(1)} custom-call(f32[1024,512]{1,0:T(8,128)S(1)} %get-tuple-element.70.refs_0_, f32[1024,512]{1,0:T(8,128)S(1)} %get-tuple-element.71.refs_1_, f32[1024,512]{1,0:T(8,128)S(1)} %get-tuple-element.72.refs_2_, f32[1024,512]{1,0:T(8,128)S(1)} %get-tuple-element.76.refs_3_, ...), custom_call_target="tpu_custom_call" | custom-call | tf_op jit(solution)/shard_map/pallas_call | solution.py:349
  94.7 1.5 %shard_map.87.p = f32[264,256]{1,0:T(8,128)S(1)} custom-call(f32[1024,512]{1,0:T(8,128)S(1)} %get-tuple-element.70.refs_0_, f32[1024,512]{1,0:T(8,128)S(1)} %get-tuple-element.71.refs_1_, f32[1024,512]{1,0:T(8,128)S(1)} %get-tuple-element.72.refs_2_, f32[1024,512]{1,0:T(8,128)S(1)} %get-tuple-element.76.refs_3_, ...), custom_call_target="tpu_custom_call" | custom-call | tf_op jit(solution)/shard_map/pallas_call | solution.py:349
  96.2 1.9 %collective-permute-start.30 = (f32[264,256]{1,0:T(8,128)S(1)}, f32[264,256]{1,0:T(8,128)S(1)}, u32[]{:S(2)}, u32[]{:S(2)}) collective-permute-start(f32[264,256]{1,0:T(8,128)S(1)} %shard_map.87.p), channel_id=1, source_target_pairs={{0,1},{1,0},{2,3},{3,2},{4,5},{5,4},{6,7},{7,6},{8,9},{9,8},{10,11... | collective-permute-start | bytes 811016 | tf_op jit(solution)/shard_map/ppermute | solution.py:455
  98.1 1.5 %shard_map.91.p = f32[264,256]{1,0:T(8,128)S(1)} custom-call(f32[1024,512]{1,0:T(8,128)S(1)} %get-tuple-element.70.refs_0_, f32[1024,512]{1,0:T(8,128)S(1)} %get-tuple-element.71.refs_1_, f32[1024,512]{1,0:T(8,128)S(1)} %get-tuple-element.72.refs_2_, f32[1024,512]{1,0:T(8,128)S(1)} %get-tuple-element.76.refs_3_, ...), custom_call_target="tpu_custom_call" | custom-call | tf_op jit(solution)/shard_map/pallas_call | solution.py:349
  99.8 5.8 %collective-permute-done.30.q = f32[264,256]{1,0:T(8,128)S(1)} collective-permute-done((f32[264,256]{1,0:T(8,128)S(1)}, f32[264,256]{1,0:T(8,128)S(1)}, u32[]{:S(2)}, u32[]{:S(2)}) %collective-permute-start.30) | collective-permute-done | bytes 270368 | tf_op jit(solution)/shard_map/ppermute | solution.py:455
  105.7 4.8 %collective-permute-done.36.q = f32[264,256]{1,0:T(8,128)S(1)} collective-permute-done((f32[264,256]{1,0:T(8,128)S(1)}, f32[264,256]{1,0:T(8,128)S(1)}, u32[]{:S(2)}, u32[]{:S(2)}) %collective-permute-start.36) | collective-permute-done | bytes 270368 | tf_op jit(solution)/shard_map/ppermute | solution.py:455
  110.7 2.1 %shard_map.89 = (f32[40,256]{1,0:T(8,128)S(1)}, f32[40,256]{1,0:T(8,128)S(1)}, f32[40,256]{1,0:T(8,128)S(1)}, f32[40,256]{1,0:T(8,128)S(1)}, f32[2,2048]{1,0:T(2,128)S(1)}) custom-call(f32[264,256]{1,0:T(8,128)S(1)} %shard_map.88.refs_0_, f32[264,256]{1,0:T(8,128)S(1)} %collective-permute-done.31.refs_1_, f32[1024,256]{1,0:T(8,128)S(1)} %get-tuple-element.97.refs_2_, ...), custom_call_target="tpu_custom_call" | custom-call | tf_op jit(solution)/shard_map/pallas_call | solution.py:390
  112.8 1.4 %collective-permute-start.32 = (f32[40,256]{1,0:T(8,128)S(1)}, f32[40,256]{1,0:T(8,128)S(1)}, u32[]{:S(2)}, u32[]{:S(2)}) collective-permute-start(f32[40,256]{1,0:T(8,128)S(1)} %get-tuple-element.103), channel_id=1, source_target_pairs={{0,2},{1,3},{2,0},{3,1},{4,6},{5,7},{6,4},{7,5},{8,10},{9,11},{10,... | collective-permute-start | bytes 122888 | tf_op jit(solution)/shard_map/ppermute | solution.py:455
  114.2 2.1 %shard_map.93 = (f32[40,256]{1,0:T(8,128)S(1)}, f32[40,256]{1,0:T(8,128)S(1)}, f32[40,256]{1,0:T(8,128)S(1)}, f32[40,256]{1,0:T(8,128)S(1)}, f32[2,2048]{1,0:T(2,128)S(1)}) custom-call(f32[264,256]{1,0:T(8,128)S(1)} %shard_map.92.refs_0_, f32[264,256]{1,0:T(8,128)S(1)} %collective-permute-done.37.refs_1_, f32[1024,256]{1,0:T(8,128)S(1)} %get-tuple-element.97.refs_2_, ...), custom_call_target="tpu_custom_call" | custom-call | tf_op jit(solution)/shard_map/pallas_call | solution.py:390
  116.4 1.8 %collective-permute-start.38 = (f32[2,2048]{1,0:T(2,128)S(1)}, f32[2,2048]{1,0:T(2,128)S(1)}, u32[]{:S(2)}, u32[]{:S(2)}) collective-permute-start(f32[2,2048]{1,0:T(2,128)S(1)} %pad_maximum_fusion.2.refs_4_), channel_id=1, source_target_pairs={{0,16},{8,24},{16,0},{24,8},{1,17},{9,25},{17,1},{25,9},{2,18},{10... | collective-permute-start | bytes 49160 | tf_op jit(solution)/shard_map/ppermute | solution.py:455
  119.3 2.1 %collective-permute-start.34 = (f32[40,256]{1,0:T(8,128)S(1)}, f32[40,256]{1,0:T(8,128)S(1)}, u32[]{:S(2)}, u32[]{:S(2)}) collective-permute-start(f32[40,256]{1,0:T(8,128)S(1)} %get-tuple-element.105), channel_id=1, source_target_pairs={{0,6},{1,7},{2,4},{3,5},{4,2},{5,3},{6,0},{7,1},{8,14},{9,15},{10,... | collective-permute-start | bytes 122888 | tf_op jit(solution)/shard_map/ppermute | solution.py:455
  121.7 2.0 %collective-permute-start.40 = (f32[40,256]{1,0:T(8,128)S(1)}, f32[40,256]{1,0:T(8,128)S(1)}, u32[]{:S(2)}, u32[]{:S(2)}) collective-permute-start(f32[40,256]{1,0:T(8,128)S(1)} %get-tuple-element.114), channel_id=1, source_target_pairs={{0,4},{1,5},{2,6},{3,7},{4,0},{5,1},{6,2},{7,3},{8,12},{9,13},{10,... | collective-permute-start | bytes 122888 | tf_op jit(solution)/shard_map/ppermute | solution.py:455
  123.8 2.1 %collective-permute-start.41 = (f32[40,256]{1,0:T(8,128)S(1)}, f32[40,256]{1,0:T(8,128)S(1)}, u32[]{:S(2)}, u32[]{:S(2)}) collective-permute-start(f32[40,256]{1,0:T(8,128)S(1)} %get-tuple-element.115), channel_id=1, source_target_pairs={{0,6},{1,7},{2,4},{3,5},{4,2},{5,3},{6,0},{7,1},{8,14},{9,15},{10,... | collective-permute-start | bytes 122888 | tf_op jit(solution)/shard_map/ppermute | solution.py:455
  126.9 2.7 %collective-permute-done.41.refs_7_ = f32[40,256]{1,0:T(8,128)S(1)} collective-permute-done((f32[40,256]{1,0:T(8,128)S(1)}, f32[40,256]{1,0:T(8,128)S(1)}, u32[]{:S(2)}, u32[]{:S(2)}) %collective-permute-start.41) | collective-permute-done | bytes 40992 | tf_op jit(solution)/shard_map/ppermute | solution.py:455
  (70 shorter events, 23.2 us)
Async XLA Ops:
  1.8 5.7 %collective-permute-start = (f32[32,512]{1,0:T(8,128)S(1)}, f32[32,512]{1,0:T(8,128)S(1)}, u32[]{:S(2)}, u32[]{:S(2)}) collective-permute-start(f32[32,512]{1,0:T(8,128)S(1)} %get-tuple-element.62), channel_id=1, source_target_pairs={{0,2},{1,3},{2,0},{3,1},{4,6},{5,7},{6,4},{7,5},{8,10},{9,11},{10,... | collective-permute-start | bytes 196616 | tf_op jit(solution)/shard_map/ppermute | solution.py:455
  5.0 7.3 %collective-permute-start.1 = (f32[32,512]{1,0:T(8,128)S(1)}, f32[32,512]{1,0:T(8,128)S(1)}, u32[]{:S(2)}, u32[]{:S(2)}) collective-permute-start(f32[32,512]{1,0:T(8,128)S(1)} %get-tuple-element.63), channel_id=1, source_target_pairs={{0,4},{1,5},{2,6},{3,7},{4,0},{5,1},{6,2},{7,3},{8,12},{9,13},{10,... | collective-permute-start | bytes 196616 | tf_op jit(solution)/shard_map/ppermute | solution.py:455
  7.6 6.1 %collective-permute-start.2 = (f32[32,512]{1,0:T(8,128)S(1)}, f32[32,512]{1,0:T(8,128)S(1)}, u32[]{:S(2)}, u32[]{:S(2)}) collective-permute-start(f32[32,512]{1,0:T(8,128)S(1)} %get-tuple-element.64), channel_id=1, source_target_pairs={{0,6},{1,7},{2,4},{3,5},{4,2},{5,3},{6,0},{7,1},{8,14},{9,15},{10,... | collective-permute-start | bytes 196616 | tf_op jit(solution)/shard_map/ppermute | solution.py:455
  13.6 6.5 %collective-permute-start.3 = (f32[128,512]{1,0:T(8,128)S(1)}, f32[128,512]{1,0:T(8,128)S(1)}, u32[]{:S(2)}, u32[]{:S(2)}) collective-permute-start(f32[128,512]{1,0:T(8,128)S(1)} %shard_map.77), channel_id=1, source_target_pairs={{0,1},{1,0},{2,3},{3,2},{4,5},{5,4},{6,7},{7,6},{8,9},{9,8},{10,11... | collective-permute-start | bytes 786440 | tf_op jit(solution)/shard_map/ppermute | solution.py:455
  15.2 1.3 %collective-permute-start.5 = (f32[64,512]{1,0:T(8,128)S(1)}, f32[64,512]{1,0:T(8,128)S(1)}, u32[]{:S(2)}, u32[]{:S(2)}) collective-permute-start(f32[64,512]{1,0:T(8,128)S(1)} %get-tuple-element.69), channel_id=1, source_target_pairs={{0,8},{8,0},{16,24},{24,16},{1,9},{9,1},{17,25},{25,17},{2,10},{10... | collective-permute-start | bytes 393224 | tf_op jit(solution)/shard_map/ppermute | solution.py:455
  16.6 10.9 %collective-permute-start.7 = (f32[136,512]{1,0:T(8,128)S(1)}, f32[136,512]{1,0:T(8,128)S(1)}, u32[]{:S(2)}, u32[]{:S(2)}) collective-permute-start(f32[136,512]{1,0:T(8,128)S(1)} %constant_dynamic-update-slice_fusion.refs_0_), channel_id=1, source_target_pairs={{0,2},{1,3},{2,0},{3,1},{4,6},{5,7},{6,4},{7,5},{8,10},{9,11},{10,... | collective-permute-start | bytes 835592 | tf_op jit(solution)/shard_map/ppermute | solution.py:455
  20.2 23.8 %collective-permute-start.4 = (f32[264,512]{1,0:T(8,128)S(1)}, f32[264,512]{1,0:T(8,128)S(1)}, u32[]{:S(2)}, u32[]{:S(2)}) collective-permute-start(f32[264,512]{1,0:T(8,128)S(1)} %pad_maximum_fusion.own), channel_id=1, source_target_pairs={{0,8},{8,0},{16,24},{24,16},{1,9},{9,1},{17,25},{25,17},{2,10},{10... | collective-permute-start | bytes 1622024 | tf_op jit(solution)/shard_map/ppermute | solution.py:455
  20.3 12.3 %collective-permute-start.9 = (f32[72,512]{1,0:T(8,128)S(1)}, f32[72,512]{1,0:T(8,128)S(1)}, u32[]{:S(2)}, u32[]{:S(2)}) collective-permute-start(f32[72,512]{1,0:T(8,128)S(1)} %get-tuple-element.68.refs_8_), channel_id=1, source_target_pairs={{0,4},{1,5},{2,6},{3,7},{4,0},{5,1},{6,2},{7,3},{8,12},{9,13},{10,... | collective-permute-start | bytes 442376 | tf_op jit(solution)/shard_map/ppermute | solution.py:455
  27.5 16.2 %collective-permute-start.8 = (f32[136,512]{1,0:T(8,128)S(1)}, f32[136,512]{1,0:T(8,128)S(1)}, u32[]{:S(2)}, u32[]{:S(2)}) collective-permute-start(f32[136,512]{1,0:T(8,128)S(1)} %collective-permute-done.7.refs_0_), channel_id=1, source_target_pairs={{0,16},{8,24},{16,0},{24,8},{1,17},{9,25},{17,1},{25,9},{2,18},{10... | collective-permute-start | bytes 835592 | tf_op jit(solution)/shard_map/ppermute | solution.py:455
  29.0 7.3 %collective-permute-start.11 = (f32[64,512]{1,0:T(8,128)S(1)}, f32[64,512]{1,0:T(8,128)S(1)}, u32[]{:S(2)}, u32[]{:S(2)}) collective-permute-start(f32[64,512]{1,0:T(8,128)S(1)} %collective-permute-done.5), channel_id=1, source_target_pairs={{0,4},{1,5},{2,6},{3,7},{4,0},{5,1},{6,2},{7,3},{8,12},{9,13},{10,... | collective-permute-start | bytes 393224 | tf_op jit(solution)/shard_map/ppermute | solution.py:455
  32.6 6.9 %collective-permute-start.13 = (f32[72,512]{1,0:T(8,128)S(1)}, f32[72,512]{1,0:T(8,128)S(1)}, u32[]{:S(2)}, u32[]{:S(2)}) collective-permute-start(f32[72,512]{1,0:T(8,128)S(1)} %collective-permute-done.9.refs_0_), channel_id=1, source_target_pairs={{0,2},{1,3},{2,0},{3,1},{4,6},{5,7},{6,4},{7,5},{8,10},{9,11},{10,... | collective-permute-start | bytes 442376 | tf_op jit(solution)/shard_map/ppermute | solution.py:455
  32.6 15.0 %collective-permute-start.6 = (f32[136,512]{1,0:T(8,128)S(1)}, f32[136,512]{1,0:T(8,128)S(1)}, u32[]{:S(2)}, u32[]{:S(2)}) collective-permute-start(f32[136,512]{1,0:T(8,128)S(1)} %constant_dynamic-update-slice_fusion.refs_0_), channel_id=1, source_target_pairs={{0,16},{8,24},{16,0},{24,8},{1,17},{9,25},{17,1},{25,9},{2,18},{10... | collective-permute-start | bytes 835592 | tf_op jit(solution)/shard_map/ppermute | solution.py:455
  36.3 5.6 %collective-permute-start.15 = (f32[64,512]{1,0:T(8,128)S(1)}, f32[64,512]{1,0:T(8,128)S(1)}, u32[]{:S(2)}, u32[]{:S(2)}) collective-permute-start(f32[64,512]{1,0:T(8,128)S(1)} %collective-permute-done.11.refs_2_), channel_id=1, source_target_pairs={{0,2},{1,3},{2,0},{3,1},{4,6},{5,7},{6,4},{7,5},{8,10},{9,11},{10,... | collective-permute-start | bytes 393224 | tf_op jit(solution)/shard_map/ppermute | solution.py:455
  39.5 9.4 %collective-permute-start.10 = (f32[72,512]{1,0:T(8,128)S(1)}, f32[72,512]{1,0:T(8,128)S(1)}, u32[]{:S(2)}, u32[]{:S(2)}) collective-permute-start(f32[72,512]{1,0:T(8,128)S(1)} %collective-permute-done.9.refs_0_), channel_id=1, source_target_pairs={{0,16},{8,24},{16,0},{24,8},{1,17},{9,25},{17,1},{25,9},{2,18},{10... | collective-permute-start | bytes 442376 | tf_op jit(solution)/shard_map/ppermute | solution.py:455
  41.9 11.8 %collective-permute-start.14 = (f32[72,512]{1,0:T(8,128)S(1)}, f32[72,512]{1,0:T(8,128)S(1)}, u32[]{:S(2)}, u32[]{:S(2)}) collective-permute-start(f32[72,512]{1,0:T(8,128)S(1)} %collective-permute-done.13.refs_0_), channel_id=1, source_target_pairs={{0,16},{8,24},{16,0},{24,8},{1,17},{9,25},{17,1},{25,9},{2,18},{10... | collective-permute-start | bytes 442376 | tf_op jit(solution)/shard_map/ppermute | solution.py:455
  43.7 8.6 %collective-permute-start.12 = (f32[64,512]{1,0:T(8,128)S(1)}, f32[64,512]{1,0:T(8,128)S(1)}, u32[]{:S(2)}, u32[]{:S(2)}) collective-permute-start(f32[64,512]{1,0:T(8,128)S(1)} %collective-permute-done.11.refs_2_), channel_id=1, source_target_pairs={{0,16},{8,24},{16,0},{24,8},{1,17},{9,25},{17,1},{25,9},{2,18},{10... | collective-permute-start | bytes 393224 | tf_op jit(solution)/shard_map/ppermute | solution.py:455
  43.9 9.9 %collective-permute-start.16 = (f32[64,512]{1,0:T(8,128)S(1)}, f32[64,512]{1,0:T(8,128)S(1)}, u32[]{:S(2)}, u32[]{:S(2)}) collective-permute-start(f32[64,512]{1,0:T(8,128)S(1)} %collective-permute-done.15.refs_2_), channel_id=1, source_target_pairs={{0,16},{8,24},{16,0},{24,8},{1,17},{9,25},{17,1},{25,9},{2,18},{10... | collective-permute-start | bytes 393224 | tf_op jit(solution)/shard_map/ppermute | solution.py:455
  55.2 1.2 collective-permute-start.17
  56.5 3.7 %collective-permute-start.18 = (f32[2,1024]{1,0:T(2,128)S(1)}, f32[2,1024]{1,0:T(2,128)S(1)}, u32[]{:S(2)}, u32[]{:S(2)}) collective-permute-start(f32[2,1024]{1,0:T(2,128)S(1)} %pad_maximum_fusion.3.refs_5_), channel_id=1, source_target_pairs={{0,1},{1,0},{2,3},{3,2},{4,5},{5,4},{6,7},{7,6},{8,9},{9,8},{10,11... | collective-permute-start | bytes 24584 | tf_op jit(solution)/shard_map/ppermute | solution.py:455
  62.3 3.8 %collective-permute-start.19 = (f32[2,2048]{1,0:T(2,128)S(1)}, f32[2,2048]{1,0:T(2,128)S(1)}, u32[]{:S(2)}, u32[]{:S(2)}) collective-permute-start(f32[2,2048]{1,0:T(2,128)S(1)} %get-tuple-element.92), channel_id=1, source_target_pairs={{0,16},{8,24},{16,0},{24,8},{1,17},{9,25},{17,1},{25,9},{2,18},{10... | collective-permute-start | bytes 49160 | tf_op jit(solution)/shard_map/ppermute | solution.py:455
  66.1 5.6 %collective-permute-start.22 = (f32[2,2048]{1,0:T(2,128)S(1)}, f32[2,2048]{1,0:T(2,128)S(1)}, u32[]{:S(2)}, u32[]{:S(2)}) collective-permute-start(f32[2,2048]{1,0:T(2,128)S(1)} %pad_maximum_fusion.1.refs_9_), channel_id=1, source_target_pairs={{0,6},{1,7},{2,4},{3,5},{4,2},{5,3},{6,0},{7,1},{8,14},{9,15},{10,... | collective-permute-start | bytes 49160 | tf_op jit(solution)/shard_map/ppermute | solution.py:455
  67.9 4.6 %collective-permute-start.21 = (f32[2,2048]{1,0:T(2,128)S(1)}, f32[2,2048]{1,0:T(2,128)S(1)}, u32[]{:S(2)}, u32[]{:S(2)}) collective-permute-start(f32[2,2048]{1,0:T(2,128)S(1)} %pad_maximum_fusion.1.refs_9_), channel_id=1, source_target_pairs={{0,4},{1,5},{2,6},{3,7},{4,0},{5,1},{6,2},{7,3},{8,12},{9,13},{10,... | collective-permute-start | bytes 49160 | tf_op jit(solution)/shard_map/ppermute | solution.py:455
  68.6 3.9 %collective-permute-start.20 = (f32[2,2048]{1,0:T(2,128)S(1)}, f32[2,2048]{1,0:T(2,128)S(1)}, u32[]{:S(2)}, u32[]{:S(2)}) collective-permute-start(f32[2,2048]{1,0:T(2,128)S(1)} %pad_maximum_fusion.1.refs_9_), channel_id=1, source_target_pairs={{0,2},{1,3},{2,0},{3,1},{4,6},{5,7},{6,4},{7,5},{8,10},{9,11},{10,... | collective-permute-start | bytes 49160 | tf_op jit(solution)/shard_map/ppermute | solution.py:455
  73.9 1.2 collective-permute-start.23
  75.1 3.6 %collective-permute-start.24 = (f32[1,1024]{1,0:T(1,128)S(1)}, f32[1,1024]{1,0:T(1,128)S(1)}, u32[]{:S(2)}, u32[]{:S(2)}) collective-permute-start(f32[1,1024]{1,0:T(1,128)S(1)} %add.17.refs_7_), channel_id=1, source_target_pairs={{0,1},{1,0},{2,3},{3,2},{4,5},{5,4},{6,7},{7,6},{8,9},{9,8},{10,11... | collective-permute-start | bytes 12296 | tf_op jit(solution)/shard_map/ppermute | solution.py:455
  80.5 3.7 %collective-permute-start.25 = (f32[1,2048]{1,0:T(1,128)S(1)}, f32[1,2048]{1,0:T(1,128)S(1)}, u32[]{:S(2)}, u32[]{:S(2)}) collective-permute-start(f32[1,2048]{1,0:T(1,128)S(1)} %get-tuple-element.96), channel_id=1, source_target_pairs={{0,16},{8,24},{16,0},{24,8},{1,17},{9,25},{17,1},{25,9},{2,18},{10... | collective-permute-start | bytes 24584 | tf_op jit(solution)/shard_map/ppermute | solution.py:455
  84.2 5.5 %collective-permute-start.28 = (f32[1,2048]{1,0:T(1,128)S(1)}, f32[1,2048]{1,0:T(1,128)S(1)}, u32[]{:S(2)}, u32[]{:S(2)}) collective-permute-start(f32[1,2048]{1,0:T(1,128)S(1)} %add.18.refs_18_), channel_id=1, source_target_pairs={{0,6},{1,7},{2,4},{3,5},{4,2},{5,3},{6,0},{7,1},{8,14},{9,15},{10,... | collective-permute-start | bytes 24584 | tf_op jit(solution)/shard_map/ppermute | solution.py:455
  86.4 4.6 %collective-permute-start.27 = (f32[1,2048]{1,0:T(1,128)S(1)}, f32[1,2048]{1,0:T(1,128)S(1)}, u32[]{:S(2)}, u32[]{:S(2)}) collective-permute-start(f32[1,2048]{1,0:T(1,128)S(1)} %add.18.refs_18_), channel_id=1, source_target_pairs={{0,4},{1,5},{2,6},{3,7},{4,0},{5,1},{6,2},{7,3},{8,12},{9,13},{10,... | collective-permute-start | bytes 24584 | tf_op jit(solution)/shard_map/ppermute | solution.py:455
  87.5 3.7 %collective-permute-start.26 = (f32[1,2048]{1,0:T(1,128)S(1)}, f32[1,2048]{1,0:T(1,128)S(1)}, u32[]{:S(2)}, u32[]{:S(2)}) collective-permute-start(f32[1,2048]{1,0:T(1,128)S(1)} %add.18.refs_18_), channel_id=1, source_target_pairs={{0,2},{1,3},{2,0},{3,1},{4,6},{5,7},{6,4},{7,5},{8,10},{9,11},{10,... | collective-permute-start | bytes 24584 | tf_op jit(solution)/shard_map/ppermute | solution.py:455
  92.6 2.1 %collective-permute-start.29 = (f32[264,256]{1,0:T(8,128)S(1)}, f32[264,256]{1,0:T(8,128)S(1)}, u32[]{:S(2)}, u32[]{:S(2)}) collective-permute-start(f32[264,256]{1,0:T(8,128)S(1)} %shard_map.86), channel_id=1, source_target_pairs={{0,8},{8,0},{16,24},{24,16},{1,9},{9,1},{17,25},{25,17},{2,10},{10... | collective-permute-start | bytes 811016 | tf_op jit(solution)/shard_map/ppermute | solution.py:455
  94.2 4.0 %collective-permute-start.35 = (f32[264,256]{1,0:T(8,128)S(1)}, f32[264,256]{1,0:T(8,128)S(1)}, u32[]{:S(2)}, u32[]{:S(2)}) collective-permute-start(f32[264,256]{1,0:T(8,128)S(1)} %shard_map.90), channel_id=1, source_target_pairs={{0,8},{8,0},{16,24},{24,16},{1,9},{9,1},{17,25},{25,17},{2,10},{10... | collective-permute-start | bytes 811016 | tf_op jit(solution)/shard_map/ppermute | solution.py:455
  96.2 9.4 %collective-permute-start.30 = (f32[264,256]{1,0:T(8,128)S(1)}, f32[264,256]{1,0:T(8,128)S(1)}, u32[]{:S(2)}, u32[]{:S(2)}) collective-permute-start(f32[264,256]{1,0:T(8,128)S(1)} %shard_map.87.p), channel_id=1, source_target_pairs={{0,1},{1,0},{2,3},{3,2},{4,5},{5,4},{6,7},{7,6},{8,9},{9,8},{10,11... | collective-permute-start | bytes 811016 | tf_op jit(solution)/shard_map/ppermute | solution.py:455
  99.6 11.0 %collective-permute-start.36 = (f32[264,256]{1,0:T(8,128)S(1)}, f32[264,256]{1,0:T(8,128)S(1)}, u32[]{:S(2)}, u32[]{:S(2)}) collective-permute-start(f32[264,256]{1,0:T(8,128)S(1)} %shard_map.91.p), channel_id=1, source_target_pairs={{0,1},{1,0},{2,3},{3,2},{4,5},{5,4},{6,7},{7,6},{8,9},{9,8},{10,11... | collective-permute-start | bytes 811016 | tf_op jit(solution)/shard_map/ppermute | solution.py:455
  105.7 5.0 %collective-permute-start.31 = (f32[264,256]{1,0:T(8,128)S(1)}, f32[264,256]{1,0:T(8,128)S(1)}, u32[]{:S(2)}, u32[]{:S(2)}) collective-permute-start(f32[264,256]{1,0:T(8,128)S(1)} %shard_map.88.refs_0_), channel_id=1, source_target_pairs={{0,8},{8,0},{16,24},{24,16},{1,9},{9,1},{17,25},{25,17},{2,10},{10... | collective-permute-start | bytes 811016 | tf_op jit(solution)/shard_map/ppermute | solution.py:455
  110.6 3.6 %collective-permute-start.37 = (f32[264,256]{1,0:T(8,128)S(1)}, f32[264,256]{1,0:T(8,128)S(1)}, u32[]{:S(2)}, u32[]{:S(2)}) collective-permute-start(f32[264,256]{1,0:T(8,128)S(1)} %shard_map.92.refs_0_), channel_id=1, source_target_pairs={{0,8},{8,0},{16,24},{24,16},{1,9},{9,1},{17,25},{25,17},{2,10},{10... | collective-permute-start | bytes 811016 | tf_op jit(solution)/shard_map/ppermute | solution.py:455
  112.8 11.0 %collective-permute-start.32 = (f32[40,256]{1,0:T(8,128)S(1)}, f32[40,256]{1,0:T(8,128)S(1)}, u32[]{:S(2)}, u32[]{:S(2)}) collective-permute-start(f32[40,256]{1,0:T(8,128)S(1)} %get-tuple-element.103), channel_id=1, source_target_pairs={{0,2},{1,3},{2,0},{3,1},{4,6},{5,7},{6,4},{7,5},{8,10},{9,11},{10,... | collective-permute-start | bytes 122888 | tf_op jit(solution)/shard_map/ppermute | solution.py:455
  116.4 5.0 %collective-permute-start.38 = (f32[2,2048]{1,0:T(2,128)S(1)}, f32[2,2048]{1,0:T(2,128)S(1)}, u32[]{:S(2)}, u32[]{:S(2)}) collective-permute-start(f32[2,2048]{1,0:T(2,128)S(1)} %pad_maximum_fusion.2.refs_4_), channel_id=1, source_target_pairs={{0,16},{8,24},{16,0},{24,8},{1,17},{9,25},{17,1},{25,9},{2,18},{10... | collective-permute-start | bytes 49160 | tf_op jit(solution)/shard_map/ppermute | solution.py:455
  118.2 7.7 %collective-permute-start.33 = (f32[40,256]{1,0:T(8,128)S(1)}, f32[40,256]{1,0:T(8,128)S(1)}, u32[]{:S(2)}, u32[]{:S(2)}) collective-permute-start(f32[40,256]{1,0:T(8,128)S(1)} %get-tuple-element.104), channel_id=1, source_target_pairs={{0,4},{1,5},{2,6},{3,7},{4,0},{5,1},{6,2},{7,3},{8,12},{9,13},{10,... | collective-permute-start | bytes 122888 | tf_op jit(solution)/shard_map/ppermute | solution.py:455
  119.3 6.6 %collective-permute-start.34 = (f32[40,256]{1,0:T(8,128)S(1)}, f32[40,256]{1,0:T(8,128)S(1)}, u32[]{:S(2)}, u32[]{:S(2)}) collective-permute-start(f32[40,256]{1,0:T(8,128)S(1)} %get-tuple-element.105), channel_id=1, source_target_pairs={{0,6},{1,7},{2,4},{3,5},{4,2},{5,3},{6,0},{7,1},{8,14},{9,15},{10,... | collective-permute-start | bytes 122888 | tf_op jit(solution)/shard_map/ppermute | solution.py:455
  121.4 4.5 %collective-permute-start.39 = (f32[40,256]{1,0:T(8,128)S(1)}, f32[40,256]{1,0:T(8,128)S(1)}, u32[]{:S(2)}, u32[]{:S(2)}) collective-permute-start(f32[40,256]{1,0:T(8,128)S(1)} %get-tuple-element.113), channel_id=1, source_target_pairs={{0,2},{1,3},{2,0},{3,1},{4,6},{5,7},{6,4},{7,5},{8,10},{9,11},{10,... | collective-permute-start | bytes 122888 | tf_op jit(solution)/shard_map/ppermute | solution.py:455
  121.7 5.1 %collective-permute-start.40 = (f32[40,256]{1,0:T(8,128)S(1)}, f32[40,256]{1,0:T(8,128)S(1)}, u32[]{:S(2)}, u32[]{:S(2)}) collective-permute-start(f32[40,256]{1,0:T(8,128)S(1)} %get-tuple-element.114), channel_id=1, source_target_pairs={{0,4},{1,5},{2,6},{3,7},{4,0},{5,1},{6,2},{7,3},{8,12},{9,13},{10,... | collective-permute-start | bytes 122888 | tf_op jit(solution)/shard_map/ppermute | solution.py:455
  123.8 5.8 %collective-permute-start.41 = (f32[40,256]{1,0:T(8,128)S(1)}, f32[40,256]{1,0:T(8,128)S(1)}, u32[]{:S(2)}, u32[]{:S(2)}) collective-permute-start(f32[40,256]{1,0:T(8,128)S(1)} %get-tuple-element.115), channel_id=1, source_target_pairs={{0,6},{1,7},{2,4},{3,5},{4,2},{5,3},{6,0},{7,1},{8,14},{9,15},{10,... | collective-permute-start | bytes 122888 | tf_op jit(solution)/shard_map/ppermute | solution.py:455
  130.3 1.2 collective-permute-start.42
